TPU v7x, 128 devices: a whole 4x4x4 slice. The times are simulated.
128 devices in a mesh: tm: 16 (over z, y), roll: 8 (over x, core).
Axes of the slice: x: 4, y: 4, z: 4, core: 2. Of those that a mesh axis runs over, the one named last changes fastest.
Arguments:
- inputs: bfloat16 [8, 128, 32, 2048], P('roll', 'tm'), may hold values from -30 to 30
- cotangent: bfloat16 [8, 128, 32, 2048], P('roll', 'tm'), may hold values from -6 to 6
- memory_lists: int32 [8, 128, 8], P('roll', 'tm'), may hold values from -1 to 119, as said below
- w_query: bfloat16 [2048, 1024], replicated, may hold values from -1 to 1
- w_key: bfloat16 [2048, 1024], replicated, may hold values from -1 to 1
- w_value: bfloat16 [2048, 1024], replicated, may hold values from -0.125 to 0.125
- w_output: bfloat16 [1024, 2048], replicated, may hold values from -0.1875 to 0.1875
Outputs:
- attended: bfloat16 [8, 128, 32, 2048], P('roll', 'tm')
- grad_input: bfloat16 [8, 128, 32, 2048], P('roll', 'tm')
- grad_w_query: float32 [2048, 1024], P('tm')
- grad_w_key: float32 [2048, 1024], P('tm')
- grad_w_value: float32 [2048, 1024], P('tm')
- grad_w_output: float32 [1024, 2048], P('tm')
Inputs may be any that keep to these rules, and one draw needn't show every extreme that they name: `memory_lists`: every entry is -1 or a frame of the same rollout that lies in an earlier block of 8 frames and before frame f - 4. The frames named in one list differ, and -1 entries come after them. The frames of one block name at most 3 distinct frames of any other block, and exactly 3 of the block just before theirs.
All inputs are finite; a program needn't handle non-finite values.
Results may differ from a plain program's by a relative error of at most 0.02.
Values may be sent and summed in bfloat16 or wider, within the bound.
No kernel may reach another device: no remote copies, remote signals or barrier semaphores. Data moves between devices by JAX's collectives and lax.ppermute only.
A program may use at most 192 MiB of HBM per device.

v0:
```python
import jax
import jax.numpy as jnp
from jax import lax
from jax.sharding import PartitionSpec as P

HEADS = 8
HEAD = 128
BAND = 4
MEM = 8
CAP = 3


masked_score = -1e30


def from_behind(block, axis, distance):
    devices = range(lax.axis_size(axis))
    route = [(i - distance, i) for i in devices if i - distance in devices]
    return lax.ppermute(block, axis, route)


def from_everyone(x, axis):
    copies = jnp.broadcast_to(x, (lax.axis_size(axis), *x.shape))
    return lax.all_to_all(copies, axis, split_axis=0, concat_axis=0, tiled=True)


def joined_along(parts, dim):
    shape = list(parts.shape[1:])
    shape[dim] *= parts.shape[0]
    return jnp.moveaxis(parts, 0, dim).reshape(shape)


def gathered_copies(x, axis, dim):
    parts = from_everyone(x, axis)
    return joined_along(parts, dim)


def cut_along(x, dim, length):
    before, after = (x.shape[:dim], x.shape[dim + 1 :])
    return jnp.moveaxis(x.reshape(*before, length, -1, *after), dim, 0)


def edges_of(length, count):
    unit = 8 if length >= 8 * count else 1
    return [length // unit * k // count * unit for k in range(1, count)]


def several_exchanges(x, axis, pieces, split_dim, concat_dim):
    parts = cut_along(x, split_dim, lax.axis_size(axis))
    cut = max(range(1, max(2, parts.ndim - 1)), key=lambda d: parts.shape[d])
    gathered = []
    for piece in jnp.split(parts, edges_of(parts.shape[cut], pieces), axis=cut):
        if piece.size:
            gathered.append(lax.all_to_all(piece, axis, split_axis=0, concat_axis=0, tiled=True))
    return joined_along(jnp.concatenate(gathered, axis=cut), concat_dim)


def sent_together(arrays, axis, dim, along):
    both = jnp.concatenate(arrays, axis=along)
    result, at, gathered = (lax.psum_scatter(both, axis, scatter_dimension=dim, tiled=True), 0, [])
    for a in arrays:
        gathered.append(lax.slice_in_dim(result, at, at + a.shape[along], axis=along))
        at += a.shape[along]
    return tuple(gathered)


def together(arrays, axis):
    ends = [0]
    for a in arrays:
        ends.append(ends[-1] + a.size)
    so_far = lax.psum(jnp.concatenate([a.ravel() for a in arrays]), axis)
    return tuple((so_far[b:e].reshape(a.shape) for a, b, e in zip(arrays, ends, ends[1:])))


def dot_last(left, right):
    return lax.dot_general(
        left, right, (((1,), (1,)), ((), ())), preferred_element_type=jnp.float32
    )


def dot_first(left, right):
    return lax.dot_general(
        left, right, (((0,), (0,)), ((), ())), preferred_element_type=jnp.float32
    )


def attend(queries, key_set, value_set, key_valid, grad_heads):
    frame_count, key_count, frame_tokens, inner_width = key_set.shape
    score_scale = HEAD ** (-0.5)
    query_h = queries.reshape(frame_count, frame_tokens, HEADS, HEAD)
    key_h = key_set.reshape(frame_count, key_count * frame_tokens, HEADS, HEAD)
    value_h = value_set.reshape(frame_count, key_count * frame_tokens, HEADS, HEAD)
    grad_h = grad_heads.reshape(frame_count, frame_tokens, HEADS, HEAD)
    scores = (
        jnp.einsum("fqhe,fkhe->fhqk", query_h, key_h, preferred_element_type=jnp.float32)
        * score_scale
    )
    key_mask = jnp.repeat(key_valid, frame_tokens, axis=1)[:, None, None, :]
    scores = jnp.where(key_mask, scores, masked_score)
    row_max = jnp.max(scores, axis=-1, keepdims=True)
    weights = jnp.exp(scores - row_max)
    weights = weights / jnp.sum(weights, axis=-1, keepdims=True)
    rounded = weights.astype(jnp.bfloat16)
    heads_out = jnp.einsum(
        "fhqk,fkhe->fqhe", rounded, value_h, preferred_element_type=jnp.float32
    ).astype(jnp.bfloat16)
    grad_prob = jnp.einsum("fqhe,fkhe->fhqk", grad_h, value_h, preferred_element_type=jnp.float32)
    row_dot = jnp.sum(weights * grad_prob, axis=-1, keepdims=True)
    dscore = (weights * (grad_prob - row_dot)).astype(jnp.bfloat16)
    grad_query = (
        jnp.einsum("fhqk,fkhe->fqhe", dscore, key_h, preferred_element_type=jnp.float32)
        * score_scale
    ).astype(jnp.bfloat16)
    grad_keys = (
        jnp.einsum("fhqk,fqhe->fkhe", dscore, query_h, preferred_element_type=jnp.float32)
        * score_scale
    )
    grad_values = jnp.einsum("fhqk,fqhe->fkhe", rounded, grad_h, preferred_element_type=jnp.float32)
    block_shape = (frame_count, key_count, frame_tokens, inner_width)
    return (
        heads_out.reshape(frame_count, frame_tokens, inner_width),
        grad_query.reshape(frame_count, frame_tokens, inner_width),
        grad_keys.reshape(block_shape),
        grad_values.reshape(block_shape),
    )


def spread_band(grad_band):
    frame_count, unused, frame_tokens, inner_width = grad_band.shape
    spread = jnp.zeros((frame_count + BAND, frame_tokens, inner_width), jnp.float32)
    for offset in range(BAND + 1):
        spread = spread + jnp.pad(grad_band[:, offset], ((offset, BAND - offset), (0, 0), (0, 0)))
    return spread


def slot_sum(hit_matrix, part):
    flat = part.reshape(part.shape[0] * part.shape[1], -1)
    high = flat.astype(jnp.bfloat16)
    low = (flat - high.astype(jnp.float32)).astype(jnp.bfloat16)
    return dot_first(hit_matrix, high) + dot_first(hit_matrix, low)


def local(inputs, cotangent, memory_lists, w_query, w_key, w_value, w_output):
    frame_count, frame_tokens, model_width = inputs.shape[1:]
    inner_width = w_query.shape[1]
    blocks = lax.axis_size("tm")
    position = lax.axis_index("tm")
    row_count = frame_count * frame_tokens
    flat_input = inputs.reshape(row_count, model_width)
    grad_flat = cotangent.reshape(row_count, model_width)
    queries = jnp.dot(flat_input, w_query, preferred_element_type=jnp.float32).astype(jnp.bfloat16)
    key_rows = jnp.dot(flat_input, w_key, preferred_element_type=jnp.float32).astype(jnp.bfloat16)
    value_rows = jnp.dot(flat_input, w_value, preferred_element_type=jnp.float32).astype(
        jnp.bfloat16
    )
    key_frames = key_rows.reshape(frame_count, frame_tokens, inner_width)
    value_frames = value_rows.reshape(frame_count, frame_tokens, inner_width)
    grad_heads = dot_last(grad_flat, w_output).astype(jnp.bfloat16)
    recalled = memory_lists[0]
    first_frame = position * frame_count
    last_frames = jnp.concatenate(
        [key_frames[frame_count - BAND :], value_frames[frame_count - BAND :]], axis=-1
    )
    before = from_behind(last_frames, "tm", 1)
    extended_keys = jnp.concatenate([before[..., :inner_width], key_frames], axis=0)
    extended_values = jnp.concatenate([before[..., inner_width:], value_frames], axis=0)
    band_keys = jnp.stack(
        [extended_keys[offset : offset + frame_count] for offset in range(BAND + 1)], axis=1
    )
    band_values = jnp.stack(
        [extended_values[offset : offset + frame_count] for offset in range(BAND + 1)], axis=1
    )
    band_index = (
        jnp.arange(frame_count, dtype=jnp.int32)[:, None]
        + jnp.arange(BAND + 1, dtype=jnp.int32)[None, :]
    )
    band_ok = first_frame + band_index - BAND >= 0
    all_lists = gathered_copies(recalled, "tm", 0)
    targets = jnp.arange(blocks * frame_count, dtype=jnp.int32)
    wanted = jnp.any(recalled.reshape(-1, 1) == targets[None, :], axis=0).reshape(
        blocks, frame_count
    )
    slot_rank = jnp.cumsum(wanted.astype(jnp.int32), axis=1) - 1
    slot_table = (jnp.arange(blocks, dtype=jnp.int32)[:, None] * CAP + slot_rank).reshape(-1)
    mem_ok = recalled >= 0
    safe_ids = jnp.where(mem_ok, recalled, 0)
    slot_ids = jnp.where(mem_ok, slot_table[safe_ids], 0)
    own_frames = first_frame + jnp.arange(frame_count, dtype=jnp.int32)
    requested = jnp.any(
        all_lists.reshape(blocks, frame_count * MEM, 1) == own_frames[None, None, :], axis=1
    )
    asked_rank = jnp.cumsum(requested.astype(jnp.int32), axis=1) - 1
    picker = requested[:, None, :] & (
        asked_rank[:, None, :] == jnp.arange(CAP, dtype=jnp.int32)[None, :, None]
    )
    picker = picker.astype(jnp.bfloat16)
    out_keys = jnp.einsum(
        "bcp,pz->bcz", picker, key_rows.reshape(frame_count, -1), preferred_element_type=jnp.float32
    )
    out_values = jnp.einsum(
        "bcp,pz->bcz",
        picker,
        value_rows.reshape(frame_count, -1),
        preferred_element_type=jnp.float32,
    )
    piece_shape = (blocks, CAP, frame_tokens, inner_width)
    outgoing = jnp.concatenate(
        [
            out_keys.astype(jnp.bfloat16).reshape(piece_shape),
            out_values.astype(jnp.bfloat16).reshape(piece_shape),
        ],
        axis=-1,
    )
    incoming = several_exchanges(outgoing, "tm", 2, 0, 0)
    slot_rows = incoming.reshape(blocks * CAP, frame_tokens, 2 * inner_width)
    memory_keys = slot_rows[..., :inner_width][slot_ids]
    memory_values = slot_rows[..., inner_width:][slot_ids]
    key_set = jnp.concatenate([band_keys, memory_keys], axis=1)
    value_set = jnp.concatenate([band_values, memory_values], axis=1)
    key_valid = jnp.concatenate([band_ok, mem_ok], axis=1)
    heads_out, grad_query, grad_keys_all, grad_values_all = attend(
        queries.reshape(frame_count, frame_tokens, inner_width),
        key_set,
        value_set,
        key_valid,
        grad_heads.reshape(frame_count, frame_tokens, inner_width),
    )
    key_spread = spread_band(grad_keys_all[:, : BAND + 1])
    value_spread = spread_band(grad_values_all[:, : BAND + 1])
    rim = jnp.concatenate([key_spread[:BAND], value_spread[:BAND]], axis=-1).astype(jnp.bfloat16)
    passed = from_behind(rim, "tm", -1)
    passed_full = jnp.pad(passed.astype(jnp.float32), ((frame_count - BAND, 0), (0, 0), (0, 0)))
    slot_hits = (
        slot_ids.reshape(-1, 1) == jnp.arange(blocks * CAP, dtype=jnp.int32)[None, :]
    ) & mem_ok.reshape(-1, 1)
    hit_matrix = slot_hits.astype(jnp.bfloat16)
    slot_keys = (
        slot_sum(hit_matrix, grad_keys_all[:, BAND + 1 :]).astype(jnp.bfloat16).reshape(piece_shape)
    )
    slot_values = (
        slot_sum(hit_matrix, grad_values_all[:, BAND + 1 :])
        .astype(jnp.bfloat16)
        .reshape(piece_shape)
    )
    slot_grad = jnp.concatenate([slot_keys, slot_values], axis=-1)
    returned = lax.all_to_all(slot_grad, "tm", split_axis=0, concat_axis=0, tiled=True)
    gathered_back = jnp.einsum(
        "bcp,bcz->pz", picker, returned.reshape(blocks, CAP, -1), preferred_element_type=jnp.float32
    )
    gathered_back = gathered_back.reshape(frame_count, frame_tokens, 2 * inner_width)
    grad_keys = (
        key_spread[BAND:] + passed_full[..., :inner_width] + gathered_back[..., :inner_width]
    ).astype(jnp.bfloat16)
    grad_values = (
        value_spread[BAND:] + passed_full[..., inner_width:] + gathered_back[..., inner_width:]
    ).astype(jnp.bfloat16)
    grad_keys = grad_keys.reshape(row_count, inner_width)
    grad_values = grad_values.reshape(row_count, inner_width)
    query_rows = grad_query.reshape(row_count, inner_width)
    heads_rows = heads_out.reshape(row_count, inner_width)
    grad_input = (
        dot_last(query_rows, w_query) + dot_last(grad_keys, w_key) + dot_last(grad_values, w_value)
    )
    grad_input = grad_input.astype(jnp.bfloat16).reshape(1, frame_count, frame_tokens, model_width)
    attended = jnp.dot(heads_rows, w_output, preferred_element_type=jnp.float32).astype(
        jnp.bfloat16
    )
    attended = attended.reshape(1, frame_count, frame_tokens, model_width)
    partials = (
        dot_first(flat_input, query_rows).astype(jnp.bfloat16),
        dot_first(flat_input, grad_keys).astype(jnp.bfloat16),
        dot_first(flat_input, grad_values).astype(jnp.bfloat16),
        dot_first(heads_rows, grad_flat).astype(jnp.bfloat16),
    )
    shares = (
        *tuple(
            (
                part.astype(jnp.float32)
                for part in sent_together((partials[0], partials[1], partials[2]), "tm", 0, 1)
            )
        ),
        lax.psum_scatter(partials[3], "tm", scatter_dimension=0, tiled=True).astype(jnp.float32),
    )
    totals = tuple(
        (
            part.astype(jnp.float32)
            for part in together(
                (
                    shares[0].astype(jnp.bfloat16),
                    shares[1].astype(jnp.bfloat16),
                    shares[2].astype(jnp.bfloat16),
                    shares[3].astype(jnp.bfloat16),
                ),
                "roll",
            )
        )
    )
    return (attended, grad_input, totals[0], totals[1], totals[2], totals[3])


def solution(mesh):
    return jax.shard_map(
        local,
        mesh=mesh,
        in_specs=(
            P("roll", "tm", None, None),
            P("roll", "tm", None, None),
            P("roll", "tm", None),
            P(),
            P(),
            P(),
            P(),
        ),
        out_specs=(
            P("roll", "tm", None, None),
            P("roll", "tm", None, None),
            P("tm", None),
            P("tm", None),
            P("tm", None),
            P("tm", None),
        ),
        check_vma=False,
    )
```

profile of v0, /device:TPU:1, one launch (start us, length us, event | category | flops | bytes accessed | tf_op | source)
XLA Modules:
  0.0 638.9 jit_solution(17510725195059354099)
XLA Ops:
  8.6 8.6 %all-to-all-start = ((s32[16,8,8]{2,1,0:T(8,128)}), s32[16,8,8]{2,1,0:T(8,128)S(1)}, u32[]{:S(2)}, u32[]{:S(2)}) async-start(s32[16,8,8]{2,1,0:T(8,128)} %broadcast_in_dim.17), calls=%async_computation | async-start | bytes 131072 | tf_op jit(solution)/shard_map/all_to_all | solution.py:24
  34.6 5.8 all-to-all-start.1
  46.9 38.9 %all-to-all-done.1 = bf16[16,1,3,16,2048]{4,3,2,1,0:T(8,128)(2,1)} async-done(((bf16[16,1,3,16,2048]{4,3,2,1,0:T(8,128)(2,1)}), bf16[16,1,3,16,2048]{4,3,2,1,0:T(8,128)(2,1)}, u32[]{:S(2)}, u32[]{:S(2)}) %all-to-all-start.1) | async-done | bytes 3145760 | tf_op jit(solution)/shard_map/all_to_all | solution.py:54
  85.8 4.7 all-to-all-start.2
  105.1 29.8 %all-to-all-done.2 = bf16[16,1,3,16,2048]{4,3,2,1,0:T(8,128)(2,1)} async-done(((bf16[16,1,3,16,2048]{4,3,2,1,0:T(8,128)(2,1)}), bf16[16,1,3,16,2048]{4,3,2,1,0:T(8,128)(2,1)}, u32[]{:S(2)}, u32[]{:S(2)}) %all-to-all-start.2) | async-done | bytes 3145760 | tf_op jit(solution)/shard_map/all_to_all | solution.py:54
  142.6 4.6 gather_fusion.2
  147.3 4.7 gather_fusion.1
  152.0 5.0 constant_dynamic-update-slice_fusion.2
  157.0 4.9 copy.184
  164.3 4.7 copy.183
  176.0 4.5 multiply_reduce_fusion
  180.5 6.5 %convolution_bitcast_fusion = f32[8,416,8,128]{3,1,2,0:T(8,128)} fusion(bf16[8,32,8,128]{3,2,1,0:T(8,128)(2,1)S(1)} %bitcast.296, f32[8,8,32,416]{3,2,1,0:T(8,128)S(1)} %get-tuple-element.32, f32[8,8,32]{2,1,0:T(8,128)S(1)} %get-tuple-element.31), kind=kOutput, calls=%fused_computation.16 | convolution fusion | flops 219807744 | bytes 17571840 | tf_op jit(solution)/shard_map/fhqk,fqhe->fkhe/dot_general | solution.py:118
  188.0 17.5 %copy.149 = f32[8,416,8,128]{3,2,1,0:T(8,128)} copy(f32[8,416,8,128]{3,1,2,0:T(8,128)} %convolution_bitcast_fusion) | data formatting | bytes 27262976 | tf_op jit(solution)/shard_map/fhqk,fqhe->fkhe/transpose | solution.py:118
  205.5 15.6 %reshape.248 = f32[8,13,32,1024]{3,2,1,0:T(8,128)} reshape(f32[8,416,8,128]{3,2,1,0:T(8,128)} %copy.149) | data formatting | bytes 27262976 | tf_op jit(solution)/shard_map/reshape | solution.py:124
  221.2 4.2 slice_bitcast_fusion
  225.4 5.0 copy.190
  237.4 6.3 multiply_bitcast_fusion
  243.7 17.3 %copy.142 = f32[8,416,8,128]{3,2,1,0:T(8,128)} copy(f32[8,416,8,128]{3,1,2,0:T(8,128)} %multiply_bitcast_fusion) | data formatting | bytes 27262976 | tf_op jit(solution)/shard_map/mul | solution.py:115
  261.0 15.9 %reshape.247 = f32[8,13,32,1024]{3,2,1,0:T(8,128)} reshape(f32[8,416,8,128]{3,2,1,0:T(8,128)} %copy.142) | data formatting | bytes 27262976 | tf_op jit(solution)/shard_map/reshape | solution.py:123
  276.9 4.2 slice_bitcast_fusion.1
  281.1 5.0 copy.188
  293.8 5.0 all-to-all-start.3
  298.9 4.6 convolution_convert_fusion.2
  327.7 76.8 %collective-permute-done.1 = bf16[4,32,2048]{2,0,1:T(4,128)(2,1)S(1)} collective-permute-done((bf16[4,32,2048]{2,0,1:T(4,128)(2,1)S(1)}, bf16[4,32,2048]{2,0,1:T(4,128)(2,1)S(1)}, u32[]{:S(2)}, u32[]{:S(2)}) %collective-permute-start.1) | collective-permute-done | bytes 524320 | tf_op jit(solution)/shard_map/ppermute | solution.py:19
  404.8 6.6 %copy.155 = bf16[16,3,32,2048]{3,2,0,1:T(8,128)(2,1)} copy(bf16[16,3,32,2048]{3,2,1,0:T(8,128)(2,1)} %all-to-all-done.3) | data formatting | bytes 12582912 | tf_op jit(solution)/shard_map/all_to_all | solution.py:246
  411.4 8.2 %reshape.253 = bf16[16,3,65536]{2,0,1:T(8,128)(2,1)} reshape(bf16[16,3,32,2048]{3,2,0,1:T(8,128)(2,1)} %copy.155) | data formatting | bytes 12582912 | tf_op jit(solution)/shard_map/reshape | solution.py:248
  428.8 21.1 %pad_maximum_fusion = bf16[2048,3072]{0,1:T(8,128)(2,1)} fusion(bf16[2048,1024]{0,1:T(8,128)(2,1)S(1)} %convert_bitcast_fusion, bf16[2048,1024]{0,1:T(8,128)(2,1)S(1)} %convert_bitcast_fusion.1, bf16[2048,1024]{0,1:T(8,128)(2,1)S(1)} %copy-done.2), kind=kLoop, calls=%fused_computation.11 | loop fusion | flops 37748736 | bytes 25165824 | tf_op jit(solution)/shard_map/concatenate | solution.py:59
  450.0 16.6 %copy.164 = bf16[2048,3072]{1,0:T(8,128)(2,1)} copy(bf16[2048,3072]{0,1:T(8,128)(2,1)} %pad_maximum_fusion) | data formatting | bytes 25165824
  467.7 4.6 convolution_convert_fusion.3
  475.8 88.8 %reduce-scatter.7.cloned.1.call-done = bf16[128,3072]{1,0:T(8,128)(2,1)} async-done(((bf16[2048,3072]{1,0:T(8,128)(2,1)}), bf16[128,3072]{1,0:T(8,128)(2,1)}) %reduce-scatter.7.cloned.1.call-update) | async-done | bytes 786448
  567.1 4.3 convolution_add_fusion.3
  573.6 53.4 %all-reduce.13.cloned.1.call-done = bf16[524288]{0:T(1024)(128)(2,1)} async-done(((bf16[524288]{0:T(1024)(128)(2,1)}), bf16[524288]{0:T(1024)(128)(2,1)}) %all-reduce.13.cloned.1.call-update) | async-done | bytes 1048592 | tf_op jit(solution)/shard_map/psum | solution.py:71
  (186 shorter events, 119.9 us)
Async XLA Ops:
  7.2 10.0 %copy-start = (bf16[1,8,32,2048]{3,2,1,0:T(8,128)(2,1)S(1)}, bf16[1,8,32,2048]{3,2,1,0:T(8,128)(2,1)}, u32[]{:S(2)}) copy-start(bf16[1,8,32,2048]{3,2,1,0:T(8,128)(2,1)} %param.7) | copy-start | bytes 3145732
  8.6 15.1 %all-to-all-start = ((s32[16,8,8]{2,1,0:T(8,128)}), s32[16,8,8]{2,1,0:T(8,128)S(1)}, u32[]{:S(2)}, u32[]{:S(2)}) async-start(s32[16,8,8]{2,1,0:T(8,128)} %broadcast_in_dim.17), calls=%async_computation | async-start | bytes 131072 | tf_op jit(solution)/shard_map/all_to_all | solution.py:24
  17.2 3.6 copy-start.13
  24.4 3.3 copy-start.22
  24.6 3.1 copy-start.20
  34.6 10.7 %copy-start.19 = (s32[1,8,8]{2,1,0:T(8,128)S(1)}, s32[1,8,8]{2,1,0:T(8,128)}, u32[]{:S(2)}) copy-start(s32[1,8,8]{2,1,0:T(8,128)} %param.9) | copy-start | bytes 772
  34.6 51.2 %all-to-all-start.1 = ((bf16[16,1,3,16,2048]{4,3,2,1,0:T(8,128)(2,1)}), bf16[16,1,3,16,2048]{4,3,2,1,0:T(8,128)(2,1)}, u32[]{:S(2)}, u32[]{:S(2)}) async-start(bf16[16,1,3,16,2048]{4,3,2,1,0:T(8,128)(2,1)} %get-tuple-element.18), calls=%async_computation.1 | async-start | bytes 6291456 | tf_op jit(solution)/shard_map/all_to_all | solution.py:54
  41.3 54.8 %collective-permute-start = (bf16[4,32,2048]{2,1,0:T(8,128)(2,1)}, bf16[4,32,2048]{2,1,0:T(8,128)(2,1)}, u32[]{:S(2)}, u32[]{:S(2)}) collective-permute-start(bf16[4,32,2048]{2,1,0:T(8,128)(2,1)} %pad_maximum_fusion.7), channel_id=1, source_target_pairs={{0,8},{8,16},{16,24},{24,32},{32,40},{40,48},{48,56},{56,64},{64,7... | collective-permute-start | bytes 1572872 | tf_op jit(solution)/shard_map/ppermute | solution.py:19
  85.8 49.2 %all-to-all-start.2 = ((bf16[16,1,3,16,2048]{4,3,2,1,0:T(8,128)(2,1)}), bf16[16,1,3,16,2048]{4,3,2,1,0:T(8,128)(2,1)}, u32[]{:S(2)}, u32[]{:S(2)}) async-start(bf16[16,1,3,16,2048]{4,3,2,1,0:T(8,128)(2,1)} %get-tuple-element.19), calls=%async_computation.2 | async-start | bytes 6291456 | tf_op jit(solution)/shard_map/all_to_all | solution.py:54
  90.9 3.7 copy-start.18
  90.9 3.8 copy-start.24
  94.6 74.5 %copy-start.11 = (bf16[32,8,8,128]{3,2,1,0:T(8,128)(2,1)}, bf16[32,8,8,128]{3,2,1,0:T(8,128)(2,1)S(1)}, u32[]{:S(2)}) copy-start(bf16[32,8,8,128]{3,2,1,0:T(8,128)(2,1)S(1)} %copy.180) | copy-start | bytes 1572868
  157.0 4.9 copy-start.3
  169.0 2.9 copy-start.1
  174.4 6.0 copy-start.4
  231.5 4.8 copy-start.14
  232.9 3.4 copy-start.5
  293.8 111.0 %all-to-all-start.3 = ((bf16[16,3,32,2048]{3,2,1,0:T(8,128)(2,1)}), bf16[16,3,32,2048]{3,2,1,0:T(8,128)(2,1)}, u32[]{:S(2)}, u32[]{:S(2)}) async-start(bf16[16,3,32,2048]{3,2,1,0:T(8,128)(2,1)} %pad_maximum_fusion.3), calls=%async_computation.3 | async-start | bytes 12582912 | tf_op jit(solution)/shard_map/all_to_all | solution.py:246
  298.8 176.0 %reduce-scatter.5.cloned.1.call-start = ((), (), s32[]{:S(2)}) async-start(), calls=%async_computation.6 | async-start | bytes 4456448 | tf_op jit(solution)/shard_map/reduce_scatter | solution.py:282
  303.5 261.2 %reduce-scatter.7.cloned.1.call-start = ((), (), s32[]{:S(2)}) async-start(), calls=%async_computation.8 | async-start | bytes 13369344
  316.7 6.1 slice-start
  318.6 4.3 slice-start.1
  321.3 83.2 %collective-permute-start.1 = (bf16[4,32,2048]{2,0,1:T(4,128)(2,1)S(1)}, bf16[4,32,2048]{2,0,1:T(4,128)(2,1)S(1)}, u32[]{:S(2)}, u32[]{:S(2)}) collective-permute-start(bf16[4,32,2048]{2,0,1:T(4,128)(2,1)S(1)} %pad_maximum_fusion.8), channel_id=1, source_target_pairs={{8,0},{16,8},{24,16},{32,24},{40,32},{48,40},{56,48},{64,56},{72,6... | collective-permute-start | bytes 1572872 | tf_op jit(solution)/shard_map/ppermute | solution.py:19
  324.4 3.3 copy-start.16
  411.4 8.2 %copy-start.21 = (s32[16,8]{0,1:T(8,128)S(1)}, s32[16,8]{0,1:T(8,128)}, u32[]{:S(2)}) copy-start(s32[16,8]{0,1:T(8,128)} %copy-done.20) | copy-start | bytes 1540
  411.4 8.2 %copy-start.23 = (pred[16,8]{0,1:T(8,128)(4,1)S(1)}, pred[16,8]{0,1:T(8,128)(4,1)}, u32[]{:S(2)}) copy-start(pred[16,8]{0,1:T(8,128)(4,1)} %copy-done.22) | copy-start | bytes 388
  419.6 4.0 copy-start.8
  419.6 4.1 copy-start.10
  466.6 5.6 copy-start.17
  466.7 160.4 %all-reduce.13.cloned.1.call-start = ((), (), s32[]{:S(2)}) async-start(), calls=%async_computation.7 | async-start | bytes 2097152 | tf_op jit(solution)/shard_map/psum | solution.py:71
  467.7 4.6 copy-start.25
  567.0 4.3 copy-start.26
  (6 other events, 8.8 us)
Sparse Core Ops, SparseCore 0:
  303.6 143.0 reduce-scatter.4
  466.8 97.8 reduce-scatter.6
  567.2 59.8 all-reduce.12
where the time goes:
time: 649 us; the launch traced here: 639 us
  waiting for transfers between devices  289 us (45%)
  local copies, waits for them, and re-layouts  190 us (29%)
  matrix products  68.3 us (11%)
  other arithmetic  46.6 us (7%)
  starting transfers between devices  30.1 us (5%)
  between operations  15 us (2%)
    unnamed x4, waiting for transfers between devices  88.9 us
    ppermute x2, waiting for transfers between devices, from_behind(): return lax.ppermute(block, axis, route)  76.8 us
    unnamed x88, local copies, waits for them, and re-layouts  68.7 us
    all_to_all x2, waiting for transfers between devices, several_exchanges(): lax.all_to_all(piece, axis, split_axis=0, concat_axis=0, tiled=True)  68.7 us
    psum x1, waiting for transfers between devices, together(): so_far = lax.psum(jnp.concatenate([a.ravel() for a in arrays]), axis)  53.4 us
    concatenate x1, other arithmetic, sent_together(): both = jnp.concatenate(arrays, axis=along)  21.1 us
    transpose x1, local copies, waits for them, and re-layouts, attend(): jnp.einsum('fhqk,fqhe->fkhe', rounded, grad_h, preferred_element_type=jnp...  17.5 us
    mul x1, local copies, waits for them, and re-layouts, attend(): jnp.einsum('fhqk,fqhe->fkhe', dscore, query_h, preferred_element_type=jnp...  17.3 us
  transfers between devices with their start and end apart: 9, of which 6 were waited for; matrix products, arithmetic and copies ran while one was open for 19% of the time, Pallas kernels for 0%

commit v1 on v0

v1 whole, which is shorter than its diff:
```python
import functools

import jax
import jax.numpy as jnp
from jax import lax
from jax.experimental import pallas as pl
from jax.experimental.pallas import tpu as pltpu
from jax.sharding import PartitionSpec as P

HEADS = 8
HEAD = 128
BAND = 4
MEM = 8
CAP = 3
FRAMES = 8
TOK = 32
BLOCKS = 16
ROWS = FRAMES * TOK
SPARE = BLOCKS * CAP
masked_score = -1e30
f32, bf16 = jnp.float32, jnp.bfloat16
VMEM_LIMIT = 60 * 1024 * 1024


def params(n=1):
    return pltpu.CompilerParams(
        dimension_semantics=("arbitrary",) * n, vmem_limit_bytes=VMEM_LIMIT
    )


def dot_last(left, right):
    return lax.dot_general(left, right, (((1,), (1,)), ((), ())), preferred_element_type=f32)


def dot_first(left, right):
    return lax.dot_general(left, right, (((0,), (0,)), ((), ())), preferred_element_type=f32)


def dot(left, right):
    return lax.dot_general(left, right, (((1,), (0,)), ((), ())), preferred_element_type=f32)


def keyval_body(x_ref, wk_ref, wv_ref, out_ref):
    pieces = []
    for h in range(wk_ref.shape[1] // HEAD):
        pieces += [wk_ref[:, h * HEAD : (h + 1) * HEAD], wv_ref[:, h * HEAD : (h + 1) * HEAD]]
    out_ref[...] = dot(x_ref[...], jnp.concatenate(pieces, axis=1)).astype(bf16)


def keyval_rows(x, w_key, w_value):
    rows, width = x.shape
    inner = w_key.shape[1]
    cols = 256
    return pl.pallas_call(
        keyval_body,
        grid=(inner // cols,),
        in_specs=[
            pl.BlockSpec((rows, width), lambda j: (0, 0)),
            pl.BlockSpec((width, cols), lambda j: (0, j)),
            pl.BlockSpec((width, cols), lambda j: (0, j)),
        ],
        out_specs=pl.BlockSpec((rows, 2 * cols), lambda j: (0, j)),
        out_shape=jax.ShapeDtypeStruct((rows, 2 * inner), bf16),
        compiler_params=params(),
        name="keyval",
    )(x, w_key, w_value)


def send_body(pick_ref, kv_ref, out_ref, sem):
    def copy(i):
        at = pl.multiple_of(pick_ref[i] * TOK, TOK)
        return pltpu.make_async_copy(
            kv_ref.at[pl.ds(at, TOK), :], out_ref.at[pl.ds(i * TOK, TOK), :], sem.at[i]
        )

    for i in range(BLOCKS * CAP):
        copy(i).start()
    for i in range(BLOCKS * CAP):
        copy(i).wait()


def named_frames(pick, kv):
    rows, width = kv.shape
    return pl.pallas_call(
        send_body,
        grid_spec=pltpu.PrefetchScalarGridSpec(
            num_scalar_prefetch=1,
            grid=(1,),
            in_specs=[pl.BlockSpec((rows, width), lambda i, *_: (0, 0))],
            out_specs=pl.BlockSpec(memory_space=pl.ANY),
            scratch_shapes=[pltpu.SemaphoreType.DMA((BLOCKS * CAP,))],
        ),
        out_shape=jax.ShapeDtypeStruct((BLOCKS * CAP * TOK, width), bf16),
        compiler_params=params(),
        name="send",
    )(pick, kv)


def attend_body(
    read_ref, add_ref, bias_ref, q_ref, g_ref, own_ref, prev_ref, slot_ref,
    o_ref, dq_ref, down_ref, rim_ref, dslot_ref, acc_own, acc_prev, acc_slot,
):
    scale = HEAD ** (-0.5)
    acc_own[...] = jnp.zeros_like(acc_own)
    acc_prev[...] = jnp.zeros_like(acc_prev)
    acc_slot[...] = jnp.zeros_like(acc_slot)
    for f in range(FRAMES):
        rows = slice(f * TOK, (f + 1) * TOK)
        pieces = []
        if f < BAND:
            pieces.append(prev_ref[f * TOK : BAND * TOK, :])
        pieces.append(own_ref[max(f - BAND, 0) * TOK : (f + 1) * TOK, :])
        for m in range(MEM):
            at = pl.multiple_of(read_ref[f * MEM + m] * TOK, TOK)
            pieces.append(slot_ref[pl.ds(at, TOK), :])
        kv = jnp.concatenate(pieces, axis=0)
        k, v = kv[:, :HEAD], kv[:, HEAD:]
        q, g = q_ref[rows, :], g_ref[rows, :]
        s = dot_last(q, k) * scale + bias_ref[f : f + 1, :]
        e = jnp.exp(s - jnp.max(s, axis=1, keepdims=True))
        w = e / jnp.sum(e, axis=1, keepdims=True)
        half = w.astype(bf16)
        o_ref[rows, :] = dot(half, v).astype(bf16)
        gp = dot_last(g, v)
        ds = (w * (gp - jnp.sum(w * gp, axis=1, keepdims=True))).astype(bf16)
        dq_ref[rows, :] = (dot(ds, k) * scale).astype(bf16)
        dkv = jnp.concatenate([dot_first(ds, q) * scale, dot_first(half, g)], axis=1)
        start = 0
        if f < BAND:
            start = (BAND - f) * TOK
            acc_prev[f * TOK : BAND * TOK, :] += dkv[:start]
        acc_own[max(f - BAND, 0) * TOK : (f + 1) * TOK, :] += dkv[start : (BAND + 1) * TOK]
        spots = [pl.multiple_of(add_ref[f * MEM + m] * TOK, TOK) for m in range(MEM)]
        base = (BAND + 1) * TOK
        olds = [acc_slot[pl.ds(at, TOK), :] for at in spots]
        for m, at in enumerate(spots):
            acc_slot[pl.ds(at, TOK), :] = olds[m] + dkv[base + m * TOK : base + (m + 1) * TOK]
    down_ref[...] = acc_own[...]
    rim_ref[...] = acc_prev[...].astype(bf16)
    dslot_ref[...] = acc_slot[: SPARE * TOK, :].astype(bf16)


def attend(read, add, bias, q, g, own, prev, slots):
    heads = q.shape[1] // HEAD
    col = lambda rows, width: pl.BlockSpec((rows, width), lambda h, *_: (0, h))
    return pl.pallas_call(
        attend_body,
        grid_spec=pltpu.PrefetchScalarGridSpec(
            num_scalar_prefetch=2,
            grid=(heads,),
            in_specs=[
                pl.BlockSpec(bias.shape, lambda h, *_: (0, 0)),
                col(ROWS, HEAD), col(ROWS, HEAD),
                col(ROWS, 2 * HEAD), col(BAND * TOK, 2 * HEAD), col(SPARE * TOK, 2 * HEAD),
            ],
            out_specs=[
                col(ROWS, HEAD), col(ROWS, HEAD),
                col(ROWS, 2 * HEAD), col(BAND * TOK, 2 * HEAD), col(SPARE * TOK, 2 * HEAD),
            ],
            scratch_shapes=[
                pltpu.VMEM((ROWS, 2 * HEAD), f32),
                pltpu.VMEM((BAND * TOK, 2 * HEAD), f32),
                pltpu.VMEM(((SPARE + 1) * TOK, 2 * HEAD), f32),
            ],
        ),
        out_shape=[
            jax.ShapeDtypeStruct(q.shape, bf16),
            jax.ShapeDtypeStruct(q.shape, bf16),
            jax.ShapeDtypeStruct(own.shape, f32),
            jax.ShapeDtypeStruct(prev.shape, bf16),
            jax.ShapeDtypeStruct(slots.shape, bf16),
        ],
        compiler_params=params(),
        name="attend",
    )(read, add, bias, q, g, own, prev, slots)


def collect_body(pick_ref, own_ref, rim_ref, back_ref, dk_ref, dv_ref, acc):
    acc[:ROWS, :] = own_ref[...]
    acc[ROWS:, :] = jnp.zeros_like(acc[ROWS:, :])
    tail = slice((FRAMES - BAND) * TOK, ROWS)
    acc[tail, :] += rim_ref[...].astype(f32)
    for i in range(BLOCKS * CAP):
        at = pl.multiple_of(pick_ref[i] * TOK, TOK)
        acc[pl.ds(at, TOK), :] += back_ref[i * TOK : (i + 1) * TOK, :].astype(f32)
    for h in range(own_ref.shape[1] // (2 * HEAD)):
        dk_ref[:, h * HEAD : (h + 1) * HEAD] = acc[:ROWS, 2 * h * HEAD : (2 * h + 1) * HEAD].astype(bf16)
        dv_ref[:, h * HEAD : (h + 1) * HEAD] = acc[:ROWS, (2 * h + 1) * HEAD : (2 * h + 2) * HEAD].astype(bf16)


def collect(pick, own, rim, back):
    width = own.shape[1]
    cols = 512
    col = lambda rows, w: pl.BlockSpec((rows, w), lambda h, *_: (0, h))
    return pl.pallas_call(
        collect_body,
        grid_spec=pltpu.PrefetchScalarGridSpec(
            num_scalar_prefetch=1,
            grid=(width // cols,),
            in_specs=[col(ROWS, cols), col(BAND * TOK, cols), col(SPARE * TOK, cols)],
            out_specs=[col(ROWS, cols // 2), col(ROWS, cols // 2)],
            scratch_shapes=[pltpu.VMEM((ROWS + TOK, cols), f32)],
        ),
        out_shape=[jax.ShapeDtypeStruct((ROWS, width // 2), bf16)] * 2,
        compiler_params=params(),
        name="collect",
    )(pick, own, rim, back)


def partial_body(a_ref, b_ref, out_ref):
    out_ref[...] = dot_first(a_ref[...], b_ref[...]).astype(bf16)


def weight_partial(a, b):
    rows, m = a.shape
    n = b.shape[1]
    cut = 512 if m >= 2048 else 256
    return pl.pallas_call(
        partial_body,
        grid=(m // cut,),
        in_specs=[
            pl.BlockSpec((rows, cut), lambda i: (0, i)),
            pl.BlockSpec((rows, n), lambda i: (0, 0)),
        ],
        out_specs=pl.BlockSpec((cut, n), lambda i: (i, 0)),
        out_shape=jax.ShapeDtypeStruct((m, n), bf16),
        compiler_params=params(),
        name="wgrad",
    )(a, b)


def other_core(x):
    return lax.ppermute(x, "roll", [(i, i ^ 1) for i in range(lax.axis_size("roll"))])


def core_sum(kept, sent):
    return (kept.astype(f32) + other_core(sent).astype(f32)).astype(bf16)


def from_behind(block, distance):
    return lax.ppermute(
        block, "tm", [(i - distance, i) for i in range(BLOCKS) if 0 <= i - distance < BLOCKS]
    )


def exchange(x):
    rows = x.shape[0] // BLOCKS
    y = lax.all_to_all(
        x.reshape(BLOCKS, rows, x.shape[1]), "tm", split_axis=0, concat_axis=0, tiled=True
    )
    return y.reshape(x.shape)


def local(inputs, cotangent, memory_lists, w_query, w_key, w_value, w_output):
    model_width = inputs.shape[-1]
    inner = w_query.shape[1]
    position = lax.axis_index("tm")
    core = lax.axis_index("roll") % 2
    x = inputs.reshape(ROWS, model_width)
    cot = cotangent.reshape(ROWS, model_width)
    recalled = memory_lists[0]
    first_frame = position * FRAMES

    targets = jnp.arange(BLOCKS * FRAMES, dtype=jnp.int32)
    wanted = jnp.any(recalled.reshape(-1, 1) == targets[None, :], axis=0)
    wanted = wanted.astype(jnp.int32).reshape(BLOCKS, FRAMES)
    asked = lax.all_to_all(wanted, "tm", split_axis=0, concat_axis=0, tiled=True)

    keyval = keyval_rows(x, w_key, w_value)
    queries = jnp.dot(x, w_query, preferred_element_type=f32).astype(bf16)
    grad_heads = dot_last(cot, w_output).astype(bf16)
    before = from_behind(keyval[(FRAMES - BAND) * TOK :], 1)

    slot_rank = jnp.cumsum(wanted, axis=1) - 1
    slot_table = (jnp.arange(BLOCKS, dtype=jnp.int32)[:, None] * CAP + slot_rank).reshape(-1)
    mem_ok = recalled >= 0
    flat = jnp.where(mem_ok, recalled, 0).reshape(-1)
    hit = flat[:, None] == targets[None, :]
    slot_ids = jnp.sum(jnp.where(hit, slot_table[None, :], 0), axis=1)
    ok_flat = mem_ok.reshape(-1)
    read = jnp.clip(jnp.where(ok_flat, slot_ids, 0), 0, SPARE - 1)
    add = jnp.clip(jnp.where(ok_flat, slot_ids, SPARE), 0, SPARE)
    band_index = (
        jnp.arange(FRAMES, dtype=jnp.int32)[:, None] + jnp.arange(BAND + 1, dtype=jnp.int32)[None, :]
    )
    band_ok = first_frame + band_index - BAND >= 0
    key_valid = jnp.concatenate([band_ok, mem_ok], axis=1)
    bias = jnp.repeat(jnp.where(key_valid, 0.0, masked_score).astype(f32), TOK, axis=1)

    asked_rank = jnp.cumsum(asked, axis=1) - 1
    places = jnp.arange(CAP, dtype=jnp.int32)[None, :, None]
    chosen = (asked[:, None, :] > 0) & (asked_rank[:, None, :] == places)
    frame_no = jnp.arange(FRAMES, dtype=jnp.int32)[None, None, :]
    pick = jnp.sum(jnp.where(chosen, frame_no, 0), axis=2).reshape(-1)
    pick_add = jnp.where(jnp.any(chosen, axis=2).reshape(-1), pick, FRAMES)

    slots = exchange(named_frames(pick, keyval))
    heads_out, grad_query, own_grad, rim, slot_grad = attend(
        read, add, bias, queries, grad_heads, keyval, before, slots
    )
    returned = exchange(slot_grad)
    passed = from_behind(rim, -1)

    half_in, half_out = inner // 2, model_width // 2
    other = 1 - core
    q_keep = lax.dynamic_slice_in_dim(grad_query, core * half_in, half_in, 1)
    q_send = lax.dynamic_slice_in_dim(grad_query, other * half_in, half_in, 1)
    c_keep = lax.dynamic_slice_in_dim(cot, core * half_out, half_out, 1)
    c_send = lax.dynamic_slice_in_dim(cot, other * half_out, half_out, 1)
    sum_q = core_sum(weight_partial(x, q_keep), weight_partial(x, q_send))
    sum_o = core_sum(weight_partial(heads_out, c_keep), weight_partial(heads_out, c_send))
    share_q = lax.psum_scatter(sum_q, "tm", scatter_dimension=0, tiled=True)
    share_o = lax.psum_scatter(sum_o, "tm", scatter_dimension=0, tiled=True)
    attended = jnp.dot(heads_out, w_output, preferred_element_type=f32).astype(bf16)

    grad_keys, grad_values = collect(pick_add, own_grad, passed, returned)
    kv_keep = jnp.where(core == 0, grad_keys, grad_values)
    kv_send = jnp.where(core == 0, grad_values, grad_keys)
    sum_kv = core_sum(weight_partial(x, kv_keep), weight_partial(x, kv_send))
    share_kv = lax.psum_scatter(sum_kv, "tm", scatter_dimension=0, tiled=True)
    grad_input = (
        dot_last(grad_query, w_query) + dot_last(grad_keys, w_key) + dot_last(grad_values, w_value)
    ).astype(bf16)

    def over_chips(share):
        m, n = share.shape
        groups = [[c + 2 * i for i in range(4)] for c in range(2)]
        parts = lax.all_to_all(
            share.reshape(4, m // 4, n), "roll", split_axis=0, concat_axis=0, tiled=True,
            axis_index_groups=groups,
        )
        total = jnp.sum(parts.astype(f32), axis=0).astype(bf16)
        every = lax.all_gather(total, "roll", axis=0)
        return jnp.swapaxes(every.reshape(4, 2, m // 4, n), 0, 1).reshape(2, m, n).astype(f32)

    both_q = over_chips(share_q)
    both_o = over_chips(share_o)
    both_kv = over_chips(share_kv)
    total_q = jnp.concatenate([both_q[0], both_q[1]], axis=1)
    total_o = jnp.concatenate([both_o[0], both_o[1]], axis=1)
    shape = (1, FRAMES, TOK, model_width)
    return (
        attended.reshape(shape), grad_input.reshape(shape),
        total_q, both_kv[0], both_kv[1], total_o,
    )


def solution(mesh):
    block = P("roll", "tm", None, None)
    return jax.shard_map(
        local,
        mesh=mesh,
        in_specs=(block, block, P("roll", "tm", None), P(), P(), P(), P()),
        out_specs=(block, block, P("tm", None), P("tm", None), P("tm", None), P("tm", None)),
        check_vma=False,
    )
```

time: 649 us -> 532 us (0.82); the launches traced: 639 us -> 530 us
  local copies, waits for them, and re-layouts: 190 us -> 11.1 us
  Pallas kernels: 0 us -> 93.5 us
  blocking collectives: 0 us -> 45.7 us
  matrix products: 68.3 us -> 24.3 us
  other arithmetic: 46.6 us -> 21.1 us
  starting transfers between devices: 30.1 us -> 52.1 us
  waiting for transfers between devices: 289 us -> 268 us
    reduce_scatter x1 -> x3, waiting for transfers between devices: 0.01 us -> 107 us  [the longest x1 65 us: local(): share_o = lax.psum_scatter(sum_o, 'tm', scatter_dimension=0, tiled=True)]
    pallas_call x0 -> x10, Pallas kernels: none -> 93.5 us  [the longest x1 48.3 us: attend(): pl.pallas_call(attend_body, grid_spec=pltpu.PrefetchScalarGridSpec(num_sc...]
    unnamed x4 -> x3, waiting for transfers between devices: 88.9 us -> 0.05 us
    ppermute x2 -> x5, waiting for transfers between devices: 76.8 us -> 157 us  [the longest x2 157 us: from_behind(): lax.ppermute(block, 'tm', [(i - distance, i) for i in range(BLOCKS) if 0...]
    unnamed x88 -> x24, local copies, waits for them, and re-layouts: 68.7 us -> 2.64 us
    all_to_all x4 -> x6, waiting for transfers between devices: 69.7 us -> 4.71 us  [the longest x3 4.71 us: over_chips(): lax.all_to_all(share.reshape(4, m // 4, n), 'roll', split_axis=0, concat_...]
    psum x1 -> x0, waiting for transfers between devices: 53.4 us -> none  [together(): so_far = lax.psum(jnp.concatenate([a.ravel() for a in arrays]), axis)]
    dot_general x21 -> x2, matrix products: 57.8 us -> 8.84 us  [the longest x1 4.61 us: local(): jnp.dot(heads_out, w_output, preferred_element_type=f32).astype(bf16)]
  transfers between devices with their start and end apart: 9 -> 14, of which waited for: 6 -> 5; matrix products, arithmetic and copies ran while one was open for 19% -> 9% of each run, Pallas kernels for 0% -> 8%
where the time goes in v1:
time: 532 us; the launch traced here: 530 us
  waiting for transfers between devices  268 us (50%)
  Pallas kernels  93.5 us (18%)
  starting transfers between devices  52.1 us (10%)
  blocking collectives  45.7 us (9%)
  matrix products  24.3 us (5%)
  other arithmetic  21.1 us (4%)
  between operations  14 us (3%)
  local copies, waits for them, and re-layouts  11.1 us (2%)
    ppermute x2, waiting for transfers between devices, from_behind(): lax.ppermute(block, 'tm', [(i - distance, i) for i in range(BLOCKS) if 0...  157 us
    reduce_scatter x1, waiting for transfers between devices, local(): share_o = lax.psum_scatter(sum_o, 'tm', scatter_dimension=0, tiled=True)  65 us
    pallas_call x1, Pallas kernels, attend(): pl.pallas_call(attend_body, grid_spec=pltpu.PrefetchScalarGridSpec(num_sc...  48.3 us
    all_gather x3, blocking collectives, over_chips(): every = lax.all_gather(total, 'roll', axis=0)  45.7 us
    reduce_scatter x1, waiting for transfers between devices, local(): share_kv = lax.psum_scatter(sum_kv, 'tm', scatter_dimension=0, tiled=True)  42.1 us
    pallas_call x6, Pallas kernels, weight_partial(): pl.pallas_call(partial_body, grid=(m // cut,), in_specs=[pl.BlockSpec((ro...  27.1 us
    all_to_all x2, starting transfers between devices, exchange(): lax.all_to_all(x.reshape(BLOCKS, rows, x.shape[1]), 'tm', split_axis=0, c...  20.4 us
    dot_general x4, matrix products, dot_last(): lax.dot_general(left, right, (((1,), (1,)), ((), ())), preferred_element_...  15.5 us
  transfers between devices with their start and end apart: 14, of which 5 were waited for; matrix products, arithmetic and copies ran while one was open for 9% of the time, Pallas kernels for 8%

profile of v1, /device:TPU:1, one launch (start us, length us, event | category | flops | bytes accessed | tf_op | source)
XLA Modules:
  0.0 530.2 jit_solution(127718898852882889)
XLA Ops:
  8.7 8.6 %all-to-all-start = ((s32[16,1,8]{2,1,0:T(1,128)}), s32[16,1,8]{2,1,0:T(1,128)S(1)}, u32[]{:S(2)}, u32[]{:S(2)}) async-start(s32[16,1,8]{2,1,0:T(1,128)} %bitcast.3), calls=%async_computation | async-start | bytes 16384 | tf_op jit(solution)/shard_map/all_to_all | solution.py:267
  17.3 6.6 %keyval.1.kv_ref.own_ref = bf16[256,2048]{1,0:T(8,128)(2,1)} custom-call(bf16[256,2048]{1,0:T(8,128)(2,1)} %bitcast.47, bf16[2048,1024]{1,0:T(8,128)(2,1)} %wk_ref.1, bf16[2048,1024]{1,0:T(8,128)(2,1)} %wv_ref.1), custom_call_target="tpu_custom_call" | custom-call | tf_op jit(solution)/shard_map/keyval/pallas_call | solution.py:54
  24.9 5.0 send.1
  29.9 6.8 %all-to-all-start.1 = ((bf16[16,96,2048]{2,1,0:T(8,128)(2,1)}), bf16[16,96,2048]{2,1,0:T(8,128)(2,1)}, u32[]{:S(2)}, u32[]{:S(2)}) async-start(bf16[16,96,2048]{2,1,0:T(8,128)(2,1)} %bitcast.53), calls=%async_computation.1 | async-start | bytes 12582912 | tf_op jit(solution)/shard_map/all_to_all | solution.py:248
  42.1 4.2 convolution_convert_fusion.2.q_ref
  47.2 4.3 convolution_convert_fusion.1.g_ref
  51.5 78.2 %collective-permute-done.prev_ref = bf16[128,2048]{1,0:T(8,128)(2,1)S(1)} collective-permute-done((bf16[128,2048]{1,0:T(8,128)(2,1)}, bf16[128,2048]{1,0:T(8,128)(2,1)S(1)}, u32[]{:S(2)}, u32[]{:S(2)}) %collective-permute-start) | collective-permute-done | bytes 524320 | tf_op jit(solution)/shard_map/ppermute | solution.py:241
  130.5 48.3 %attend.1 = (bf16[256,1024]{1,0:T(8,128)(2,1)}, bf16[256,1024]{1,0:T(8,128)(2,1)}, f32[256,2048]{1,0:T(8,128)}, bf16[128,2048]{1,0:T(8,128)(2,1)}, bf16[1536,2048]{1,0:T(8,128)(2,1)}) custom-call(s32[64]{0:T(128)} %get-tuple-element.33.read_ref, s32[64]{0:T(128)} %get-tuple-element.32.add_ref, f32[8,416]{1,0:T(8,128)} %reshape.141.bias_ref, ...), custom_call_target="tpu_custom_call" | custom-call | tf_op jit(solution)/shard_map/attend/pallas_call | solution.py:146
  178.8 13.5 %all-to-all-start.2 = ((bf16[16,96,2048]{2,1,0:T(8,128)(2,1)}), bf16[16,96,2048]{2,1,0:T(8,128)(2,1)}, u32[]{:S(2)}, u32[]{:S(2)}) async-start(bf16[16,96,2048]{2,1,0:T(8,128)(2,1)} %bitcast.54), calls=%async_computation.2 | async-start | bytes 12582912 | tf_op jit(solution)/shard_map/all_to_all | solution.py:248
  193.2 4.2 wgrad.7
  200.0 4.2 wgrad.6
  210.1 4.3 wgrad.11
  216.6 78.3 %collective-permute-done.1.rim_ref = bf16[128,2048]{1,0:T(8,128)(2,1)S(1)} collective-permute-done((bf16[128,2048]{1,0:T(8,128)(2,1)}, bf16[128,2048]{1,0:T(8,128)(2,1)S(1)}, u32[]{:S(2)}, u32[]{:S(2)}) %collective-permute-start.1) | collective-permute-done | bytes 524320 | tf_op jit(solution)/shard_map/ppermute | solution.py:241
  295.7 6.5 %collect.1 = (bf16[256,1024]{1,0:T(8,128)(2,1)}, bf16[256,1024]{1,0:T(8,128)(2,1)}) custom-call(s32[48]{0:T(128)} %broadcast_select_fusion.2.pick_ref, f32[256,2048]{1,0:T(8,128)} %get-tuple-element.15.own_ref, bf16[128,2048]{1,0:T(8,128)(2,1)} %copy-done.9, bf16[1536,2048]{1,0:T(8,128)(2,1)} %bitcast.10.back_ref), custom_call_target="tpu_custom_call" | custom-call | tf_op jit(solution)/shard_map/collect/pallas_call | solution.py:195
  304.5 5.0 wgrad.9
  309.5 3.6 collective-permute-start.3
  313.0 4.3 wgrad.10
  317.3 3.9 add_convert_fusion.1
  321.4 5.1 wgrad.8
  326.5 7.5 %add_convert_fusion = bf16[2048,1024]{1,0:T(8,128)(2,1)} fusion(bf16[2048,1024]{1,0:T(8,128)(2,1)} %collective-permute-done.3, bf16[2048,1024]{1,0:T(8,128)(2,1)} %wgrad.8), kind=kLoop, calls=%fused_computation | loop fusion | flops 8388608 | bytes 12582912 | tf_op jit(solution)/shard_map/convert_element_type | solution.py:237
  335.1 4.6 convolution_convert_fusion
  341.1 4.0 all-to-all-start.3
  345.1 4.8 fusion.10
  349.9 65.0 %reduce-scatter.8.cloned.1.call-done = bf16[64,1024]{1,0:T(8,128)(2,1)} async-done(((bf16[1024,1024]{1,0:T(8,128)(2,1)}), bf16[64,1024]{1,0:T(8,128)(2,1)}) %reduce-scatter.8.cloned.1.call-update) | async-done | bytes 131088 | tf_op jit(solution)/shard_map/reduce_scatter | solution.py:313
  414.9 4.0 all-to-all-start.5
  418.9 5.1 fusion.1
  424.1 16.1 %all-gather = bf16[256,512]{1,0:T(8,128)(2,1)S(1)} all-gather(bf16[32,512]{1,0:T(8,128)(2,1)S(1)} %reduce_sum.56), channel_id=2, replica_groups=mesh['tm'=16,'roll'=8] {'roll'}, dimensions={0}, use_global_device_ids=true | all-gather | bytes 294912 | tf_op jit(solution)/shard_map/all_gather | solution.py:333
  440.2 12.8 %all-gather.2 = bf16[128,1024]{1,0:T(8,128)(2,1)S(1)} all-gather(bf16[16,1024]{1,0:T(8,128)(2,1)S(1)} %reduce_sum.58), channel_id=4, replica_groups=mesh['tm'=16,'roll'=8] {'roll'}, dimensions={0}, use_global_device_ids=true | all-gather | bytes 294912 | tf_op jit(solution)/shard_map/all_gather | solution.py:333
  454.0 42.1 %reduce-scatter.6.cloned.1.call-done = bf16[128,1024]{1,0:T(8,128)(2,1)} async-done(((bf16[2048,1024]{1,0:T(8,128)(2,1)}), bf16[128,1024]{1,0:T(8,128)(2,1)}) %reduce-scatter.6.cloned.1.call-update) | async-done | bytes 262160 | tf_op jit(solution)/shard_map/reduce_scatter | solution.py:320
  496.1 4.0 all-to-all-start.4
  500.9 4.7 all-to-all-done.4
  505.6 16.8 %all-gather.1 = bf16[256,1024]{1,0:T(8,128)(2,1)S(1)} all-gather(bf16[32,1024]{1,0:T(8,128)(2,1)S(1)} %reduce_sum.57), channel_id=3, replica_groups=mesh['tm'=16,'roll'=8] {'roll'}, dimensions={0}, use_global_device_ids=true | all-gather | bytes 589824 | tf_op jit(solution)/shard_map/all_gather | solution.py:333
  (89 shorter events, 29.7 us)
Async XLA Ops:
  8.7 15.2 %all-to-all-start = ((s32[16,1,8]{2,1,0:T(1,128)}), s32[16,1,8]{2,1,0:T(1,128)S(1)}, u32[]{:S(2)}, u32[]{:S(2)}) async-start(s32[16,1,8]{2,1,0:T(1,128)} %bitcast.3), calls=%async_computation | async-start | bytes 16384 | tf_op jit(solution)/shard_map/all_to_all | solution.py:267
  29.9 6.9 %copy-start.1 = (bf16[256,2048]{1,0:T(8,128)(2,1)S(1)}, bf16[256,2048]{1,0:T(8,128)(2,1)}, u32[]{:S(2)}) copy-start(bf16[256,2048]{1,0:T(8,128)(2,1)} %keyval.1.kv_ref.own_ref) | copy-start | bytes 3145732
  29.9 12.2 %copy-start.10 = (s32[1,8,8]{2,1,0:T(8,128)S(1)}, s32[1,8,8]{2,1,0:T(8,128)}, u32[]{:S(2)}) copy-start(s32[1,8,8]{2,1,0:T(8,128)} %param.9) | copy-start | bytes 772
  29.9 12.2 %copy-start = (bf16[1,8,32,2048]{3,2,1,0:T(8,128)(2,1)S(1)}, bf16[1,8,32,2048]{3,2,1,0:T(8,128)(2,1)}, u32[]{:S(2)}) copy-start(bf16[1,8,32,2048]{3,2,1,0:T(8,128)(2,1)} %param.7) | copy-start | bytes 3145732
  29.9 99.7 %all-to-all-start.1 = ((bf16[16,96,2048]{2,1,0:T(8,128)(2,1)}), bf16[16,96,2048]{2,1,0:T(8,128)(2,1)}, u32[]{:S(2)}, u32[]{:S(2)}) async-start(bf16[16,96,2048]{2,1,0:T(8,128)(2,1)} %bitcast.53), calls=%async_computation.1 | async-start | bytes 12582912 | tf_op jit(solution)/shard_map/all_to_all | solution.py:248
  36.8 10.4 %copy-start.5 = (bf16[1,8,32,2048]{3,2,1,0:T(8,128)(2,1)S(1)}, bf16[1,8,32,2048]{3,2,1,0:T(8,128)(2,1)}, u32[]{:S(2)}) copy-start(bf16[1,8,32,2048]{3,2,1,0:T(8,128)(2,1)} %param.8) | copy-start | bytes 3145732
  37.6 92.0 %collective-permute-start = (bf16[128,2048]{1,0:T(8,128)(2,1)}, bf16[128,2048]{1,0:T(8,128)(2,1)S(1)}, u32[]{:S(2)}, u32[]{:S(2)}) collective-permute-start(bf16[128,2048]{1,0:T(8,128)(2,1)} %slice.34), channel_id=1, source_target_pairs={{0,8},{8,16},{16,24},{24,32},{32,40},{40,48},{48,56},{56,64},{64,7... | collective-permute-start | bytes 1572872 | tf_op jit(solution)/shard_map/ppermute | solution.py:241
  129.7 0.8 copy-start.6
  178.8 13.6 %copy-start.3 = (bf16[256,1024]{1,0:T(8,128)(2,1)S(1)}, bf16[256,1024]{1,0:T(8,128)(2,1)}, u32[]{:S(2)}) copy-start(bf16[256,1024]{1,0:T(8,128)(2,1)} %get-tuple-element.14) | copy-start | bytes 1572868
  178.8 116.1 %all-to-all-start.2 = ((bf16[16,96,2048]{2,1,0:T(8,128)(2,1)}), bf16[16,96,2048]{2,1,0:T(8,128)(2,1)}, u32[]{:S(2)}, u32[]{:S(2)}) async-start(bf16[16,96,2048]{2,1,0:T(8,128)(2,1)} %bitcast.54), calls=%async_computation.2 | async-start | bytes 12582912 | tf_op jit(solution)/shard_map/all_to_all | solution.py:248
  192.3 148.8 %reduce-scatter.4.cloned.1.call-start = ((), (), s32[]{:S(2)}) async-start(), calls=%async_computation.9 | async-start | bytes 2228224 | tf_op jit(solution)/shard_map/reduce_scatter | solution.py:312
  197.4 6.8 %collective-permute-start.2 = (bf16[2048,512]{1,0:T(8,128)(2,1)}, bf16[2048,512]{1,0:T(8,128)(2,1)S(1)}, u32[]{:S(2)}, u32[]{:S(2)}) collective-permute-start(bf16[2048,512]{1,0:T(8,128)(2,1)} %wgrad.7), channel_id=1, source_target_pairs={{0,1},{1,0},{2,3},{3,2},{4,5},{5,4},{6,7},{7,6},{8,9},{9,8},{10,11... | collective-permute-start | bytes 6291464 | tf_op jit(solution)/shard_map/ppermute | solution.py:233
  207.8 8.3 %copy-start.11 = (s32[48]{0:T(128)S(1)}, s32[48]{0:T(128)}, u32[]{:S(2)}) copy-start(s32[48]{0:T(128)} %reshape.144.pick_ref) | copy-start | bytes 580
  207.8 207.1 %reduce-scatter.8.cloned.1.call-start = ((), (), s32[]{:S(2)}) async-start(), calls=%async_computation.11 | async-start | bytes 2228224 | tf_op jit(solution)/shard_map/reduce_scatter | solution.py:313
  214.4 102.9 %collective-permute-start.4 = (bf16[1024,1024]{1,0:T(8,128)(2,1)}, bf16[1024,1024]{1,0:T(8,128)(2,1)S(1)}, u32[]{:S(2)}, u32[]{:S(2)}) collective-permute-start(bf16[1024,1024]{1,0:T(8,128)(2,1)} %wgrad.11), channel_id=1, source_target_pairs={{0,1},{1,0},{2,3},{3,2},{4,5},{5,4},{6,7},{7,6},{8,9},{9,8},{10,11... | collective-permute-start | bytes 6291464 | tf_op jit(solution)/shard_map/ppermute | solution.py:233
  214.5 80.4 %collective-permute-start.1 = (bf16[128,2048]{1,0:T(8,128)(2,1)}, bf16[128,2048]{1,0:T(8,128)(2,1)S(1)}, u32[]{:S(2)}, u32[]{:S(2)}) collective-permute-start(bf16[128,2048]{1,0:T(8,128)(2,1)} %get-tuple-element.16), channel_id=1, source_target_pairs={{8,0},{16,8},{24,16},{32,24},{40,32},{48,40},{56,48},{64,56},{72,6... | collective-permute-start | bytes 1572872 | tf_op jit(solution)/shard_map/ppermute | solution.py:241
  294.9 0.8 copy-start.9
  309.5 17.1 %collective-permute-start.3 = (bf16[2048,1024]{1,0:T(8,128)(2,1)}, bf16[2048,1024]{1,0:T(8,128)(2,1)}, u32[]{:S(2)}, u32[]{:S(2)}) collective-permute-start(bf16[2048,1024]{1,0:T(8,128)(2,1)} %wgrad.9), channel_id=1, source_target_pairs={{0,1},{1,0},{2,3},{3,2},{4,5},{5,4},{6,7},{7,6},{8,9},{9,8},{10,11... | collective-permute-start | bytes 12582920 | tf_op jit(solution)/shard_map/ppermute | solution.py:233
  321.2 174.9 %reduce-scatter.6.cloned.1.call-start = ((), (), s32[]{:S(2)}) async-start(), calls=%async_computation.10 | async-start | bytes 4456448 | tf_op jit(solution)/shard_map/reduce_scatter | solution.py:320
  334.1 1.0 copy-start.4
  335.1 4.6 copy-start.2
  335.1 4.6 copy-start.8
  339.7 5.4 %copy-start.7 = (bf16[256,1024]{1,0:T(8,128)(2,1)S(1)}, bf16[256,1024]{1,0:T(8,128)(2,1)}, u32[]{:S(2)}) copy-start(bf16[256,1024]{1,0:T(8,128)(2,1)} %get-tuple-element.18) | copy-start | bytes 1572868
  341.1 73.8 %all-to-all-start.3 = ((bf16[4,32,512]{2,1,0:T(8,128)(2,1)}), bf16[4,32,512]{2,1,0:T(8,128)(2,1)S(1)}, u32[]{:S(2)}, u32[]{:S(2)}) async-start(bf16[4,32,512]{2,1,0:T(8,128)(2,1)} %bitcast.68), calls=%async_computation.4 | async-start | bytes 262144 | tf_op jit(solution)/shard_map/all_to_all | solution.py:328
  414.9 9.1 %all-to-all-start.5 = ((bf16[4,16,1024]{2,1,0:T(8,128)(2,1)}), bf16[4,16,1024]{2,1,0:T(8,128)(2,1)S(1)}, u32[]{:S(2)}, u32[]{:S(2)}) async-start(bf16[4,16,1024]{2,1,0:T(8,128)(2,1)} %bitcast.69), calls=%async_computation.8 | async-start | bytes 262144 | tf_op jit(solution)/shard_map/all_to_all | solution.py:328
  496.1 9.5 %all-to-all-start.4 = ((bf16[4,32,1024]{2,1,0:T(8,128)(2,1)}), bf16[4,32,1024]{2,1,0:T(8,128)(2,1)S(1)}, u32[]{:S(2)}, u32[]{:S(2)}) async-start(bf16[4,32,1024]{2,1,0:T(8,128)(2,1)} %bitcast.67), calls=%async_computation.6 | async-start | bytes 524288 | tf_op jit(solution)/shard_map/all_to_all | solution.py:328
Sparse Core Ops, SparseCore 0:
  207.9 129.0 reduce-scatter.3
  340.3 74.5 reduce-scatter.7
  418.2 77.7 reduce-scatter.5

commit v2 on v1

v2 whole, which is shorter than its diff:
```python
import jax
import jax.numpy as jnp
from jax import lax
from jax.experimental import pallas as pl
from jax.experimental.pallas import tpu as pltpu
from jax.sharding import PartitionSpec as P

HEADS = 8
HEAD = 128
BAND = 4
MEM = 8
CAP = 3
FRAMES = 8
TOK = 32
BLOCKS = 16
ROWS = FRAMES * TOK
GROUPS = 2
GH = HEADS // GROUPS
GW = GH * 2 * HEAD
KEYS = (BAND + 1 + MEM) * TOK
CHIPS = 4
SPARE = BLOCKS * CAP
masked_score = -1e30
f32, bf16 = jnp.float32, jnp.bfloat16
VMEM_LIMIT = 60 * 1024 * 1024


def params(n=1):
    return pltpu.CompilerParams(
        dimension_semantics=("arbitrary",) * n, vmem_limit_bytes=VMEM_LIMIT
    )


def dot_last(left, right):
    return lax.dot_general(left, right, (((1,), (1,)), ((), ())), preferred_element_type=f32)


def dot_first(left, right):
    return lax.dot_general(left, right, (((0,), (0,)), ((), ())), preferred_element_type=f32)


def dot(left, right):
    return lax.dot_general(left, right, (((1,), (0,)), ((), ())), preferred_element_type=f32)


def keyval_body(x_ref, wk_ref, wv_ref, out_ref):
    pieces = []
    for h in range(wk_ref.shape[1] // HEAD):
        pieces += [wk_ref[:, h * HEAD : (h + 1) * HEAD], wv_ref[:, h * HEAD : (h + 1) * HEAD]]
    out_ref[...] = dot(x_ref[...], jnp.concatenate(pieces, axis=1)).astype(bf16)


def keyval_rows(x, w_key, w_value):
    rows, width = x.shape
    cols = 256
    steps = GW // (2 * cols)
    return pl.pallas_call(
        keyval_body,
        grid=(w_key.shape[1] // cols,),
        in_specs=[
            pl.BlockSpec((rows, width), lambda j: (0, 0)),
            pl.BlockSpec((width, cols), lambda j: (0, j)),
            pl.BlockSpec((width, cols), lambda j: (0, j)),
        ],
        out_specs=pl.BlockSpec((None, rows, 2 * cols), lambda j: (j // steps, 0, j % steps)),
        out_shape=jax.ShapeDtypeStruct((GROUPS, rows, GW), bf16),
        compiler_params=params(),
        name="keyval",
    )(x, w_key, w_value)


def send_body(pick_ref, kv_ref, out_ref, sem):
    def copy(i):
        at = pl.multiple_of(pick_ref[i] * TOK, TOK)
        return pltpu.make_async_copy(
            kv_ref.at[0, pl.ds(at, TOK), :], out_ref.at[pl.ds(i * TOK, TOK), :], sem.at[i]
        )

    for i in range(BLOCKS * CAP):
        copy(i).start()
    for i in range(BLOCKS * CAP):
        copy(i).wait()


def named_frames(pick, kv, group):
    return pl.pallas_call(
        send_body,
        grid_spec=pltpu.PrefetchScalarGridSpec(
            num_scalar_prefetch=1,
            grid=(1,),
            in_specs=[pl.BlockSpec((1, ROWS, GW), lambda i, *_: (group, 0, 0))],
            out_specs=pl.BlockSpec(memory_space=pl.ANY),
            scratch_shapes=[pltpu.SemaphoreType.DMA((BLOCKS * CAP,))],
        ),
        out_shape=jax.ShapeDtypeStruct((BLOCKS * CAP * TOK, GW), bf16),
        compiler_params=params(),
        name="send",
    )(pick, kv)


def attend_body(
    read_ref, add_ref, bias_ref, q_ref, g_ref, own_ref, prev_ref, slot_ref,
    o_ref, dq_ref, down_ref, rim_ref, dslot_ref,
    acc_own, acc_prev, acc_slot, kv_scr, s_scr, gp_scr, half_scr, ds_scr,
):
    scale = HEAD ** (-0.5)
    acc_own[...] = jnp.zeros_like(acc_own)
    acc_prev[...] = jnp.zeros_like(acc_prev)
    acc_slot[...] = jnp.zeros_like(acc_slot)
    spans = [slice(f * TOK, (f + 1) * TOK) for f in range(FRAMES)]
    for f, rows in enumerate(spans):
        at = 0
        if f < BAND:
            at = (BAND - f) * TOK
            kv_scr[f, :at, :] = prev_ref[f * TOK : BAND * TOK, :]
        kv_scr[f, at : (BAND + 1) * TOK, :] = own_ref[max(f - BAND, 0) * TOK : (f + 1) * TOK, :]
        for m in range(MEM):
            at = pl.multiple_of(read_ref[f * MEM + m] * TOK, TOK)
            kv_scr[f, (BAND + 1 + m) * TOK : (BAND + 2 + m) * TOK, :] = slot_ref[pl.ds(at, TOK), :]
    for f, rows in enumerate(spans):
        s_scr[rows, :] = dot_last(q_ref[rows, :], kv_scr[f, :, :HEAD]) * scale + bias_ref[f : f + 1, :]
        gp_scr[rows, :] = dot_last(g_ref[rows, :], kv_scr[f, :, HEAD:])
    for f, rows in enumerate(spans):
        s = s_scr[rows, :]
        gp = gp_scr[rows, :]
        e = jnp.exp(s - jnp.max(s, axis=1, keepdims=True))
        w = e * (1.0 / jnp.sum(e, axis=1, keepdims=True))
        half_scr[rows, :] = w.astype(bf16)
        ds_scr[rows, :] = (w * (gp - jnp.sum(w * gp, axis=1, keepdims=True))).astype(bf16)
    for f, rows in enumerate(spans):
        o_ref[rows, :] = dot(half_scr[rows, :], kv_scr[f, :, HEAD:]).astype(bf16)
        dq_ref[rows, :] = (dot(ds_scr[rows, :], kv_scr[f, :, :HEAD]) * scale).astype(bf16)
    for f, rows in enumerate(spans):
        dk = dot_first(ds_scr[rows, :], q_ref[rows, :]) * scale
        dv = dot_first(half_scr[rows, :], g_ref[rows, :])
        start = 0
        own = slice(max(f - BAND, 0) * TOK, (f + 1) * TOK)
        if f < BAND:
            start = (BAND - f) * TOK
            prev = slice(f * TOK, BAND * TOK)
            acc_prev[prev, :HEAD] += dk[:start]
            acc_prev[prev, HEAD:] += dv[:start]
        acc_own[own, :HEAD] += dk[start : (BAND + 1) * TOK]
        acc_own[own, HEAD:] += dv[start : (BAND + 1) * TOK]
        spots = [pl.multiple_of(add_ref[f * MEM + m] * TOK, TOK) for m in range(MEM)]
        base = (BAND + 1) * TOK
        for d, cols in ((dk, slice(0, HEAD)), (dv, slice(HEAD, 2 * HEAD))):
            olds = [acc_slot[pl.ds(at, TOK), cols] for at in spots]
            for m, at in enumerate(spots):
                acc_slot[pl.ds(at, TOK), cols] = olds[m] + d[base + m * TOK : base + (m + 1) * TOK]
    down_ref[...] = acc_own[...]
    rim_ref[...] = acc_prev[...].astype(bf16)
    dslot_ref[...] = acc_slot[: SPARE * TOK, :].astype(bf16)


def attend(read, add, bias, q, g, own, prev, slots, group):
    first = group * GH
    col = lambda rows, width: pl.BlockSpec((rows, width), lambda h, *_: (0, h))
    shifted = pl.BlockSpec((ROWS, HEAD), lambda h, *_: (0, h + first))
    grouped = lambda rows: pl.BlockSpec((None, rows, 2 * HEAD), lambda h, *_: (group, 0, h))
    return pl.pallas_call(
        attend_body,
        grid_spec=pltpu.PrefetchScalarGridSpec(
            num_scalar_prefetch=2,
            grid=(GH,),
            in_specs=[
                pl.BlockSpec(bias.shape, lambda h, *_: (0, 0)),
                shifted, shifted, grouped(ROWS), grouped(BAND * TOK), col(SPARE * TOK, 2 * HEAD),
            ],
            out_specs=[
                col(ROWS, HEAD), col(ROWS, HEAD),
                col(ROWS, 2 * HEAD), col(BAND * TOK, 2 * HEAD), col(SPARE * TOK, 2 * HEAD),
            ],
            scratch_shapes=[
                pltpu.VMEM((ROWS, 2 * HEAD), f32),
                pltpu.VMEM((BAND * TOK, 2 * HEAD), f32),
                pltpu.VMEM(((SPARE + 1) * TOK, 2 * HEAD), f32),
                pltpu.VMEM((FRAMES, KEYS, 2 * HEAD), bf16),
                pltpu.VMEM((ROWS, KEYS), f32),
                pltpu.VMEM((ROWS, KEYS), f32),
                pltpu.VMEM((ROWS, KEYS), bf16),
                pltpu.VMEM((ROWS, KEYS), bf16),
            ],
        ),
        out_shape=[
            jax.ShapeDtypeStruct((ROWS, GH * HEAD), bf16),
            jax.ShapeDtypeStruct((ROWS, GH * HEAD), bf16),
            jax.ShapeDtypeStruct((ROWS, GW), f32),
            jax.ShapeDtypeStruct((BAND * TOK, GW), bf16),
            jax.ShapeDtypeStruct((SPARE * TOK, GW), bf16),
        ],
        compiler_params=params(),
        name="attend",
    )(read, add, bias, q, g, own, prev, slots)


def collect_body(pick_ref, own_ref, rim_ref, back_ref, dk_ref, dv_ref, acc):
    acc[:ROWS, :] = own_ref[...]
    acc[ROWS:, :] = jnp.zeros_like(acc[ROWS:, :])
    tail = slice((FRAMES - BAND) * TOK, ROWS)
    acc[tail, :] += rim_ref[...].astype(f32)
    for i in range(BLOCKS * CAP):
        at = pl.multiple_of(pick_ref[i] * TOK, TOK)
        acc[pl.ds(at, TOK), :] += back_ref[i * TOK : (i + 1) * TOK, :].astype(f32)
    for h in range(own_ref.shape[1] // (2 * HEAD)):
        dk_ref[:, h * HEAD : (h + 1) * HEAD] = acc[:ROWS, 2 * h * HEAD : (2 * h + 1) * HEAD].astype(bf16)
        dv_ref[:, h * HEAD : (h + 1) * HEAD] = acc[:ROWS, (2 * h + 1) * HEAD : (2 * h + 2) * HEAD].astype(bf16)


def collect(pick, own, rim, back):
    width = own.shape[1]
    cols = 512
    col = lambda rows, w: pl.BlockSpec((rows, w), lambda h, *_: (0, h))
    return pl.pallas_call(
        collect_body,
        grid_spec=pltpu.PrefetchScalarGridSpec(
            num_scalar_prefetch=1,
            grid=(width // cols,),
            in_specs=[col(ROWS, cols), col(BAND * TOK, cols), col(SPARE * TOK, cols)],
            out_specs=[col(ROWS, cols // 2), col(ROWS, cols // 2)],
            scratch_shapes=[pltpu.VMEM((ROWS + TOK, cols), f32)],
        ),
        out_shape=[jax.ShapeDtypeStruct((ROWS, width // 2), bf16)] * 2,
        compiler_params=params(),
        name="collect",
    )(pick, own, rim, back)


def keyval_partial(x, g, got=None, chips_first=True):
    rows, m = x.shape
    n = g.shape[1]
    shard, cut = m // BLOCKS, 512
    piece = shard // CHIPS
    if chips_first:
        shape = (CHIPS, BLOCKS, piece, n)
        spec = pl.BlockSpec((CHIPS, cut // shard, piece, n), lambda i: (0, i, 0, 0))
    else:
        shape = (BLOCKS, shard, n)
        spec = pl.BlockSpec((cut // shard, shard, n), lambda i: (i, 0, 0))

    def body(a_ref, b_ref, *refs):
        out_ref = refs[-1]
        total = dot_first(a_ref[...], b_ref[...])
        for t in range(cut // shard):
            for c in range(CHIPS if chips_first else 1):
                size = piece if chips_first else shard
                at = t * shard + c * size
                where = (c, t) if chips_first else (t,)
                part = total[at : at + size]
                if len(refs) == 2:
                    part = part + refs[0][where].astype(f32)
                out_ref[where] = part.astype(bf16)

    return pl.pallas_call(
        body,
        grid=(m // cut,),
        in_specs=[
            pl.BlockSpec((rows, cut), lambda i: (0, i)),
            pl.BlockSpec((rows, n), lambda i: (0, 0)),
        ] + [spec] * (got is not None),
        out_specs=spec,
        out_shape=jax.ShapeDtypeStruct(shape, bf16),
        compiler_params=params(),
        name="keyval_partial",
    )(x, g, *([] if got is None else [got]))


def query_output_partial(x, q, heads, cot, got=None):
    rows, m = x.shape
    n = q.shape[1]
    inner = heads.shape[1]
    per = 4
    q_shard, o_shard = m // BLOCKS, inner // BLOCKS
    q_piece, o_piece = q_shard // CHIPS, o_shard // CHIPS
    height = q_piece + 2 * o_piece
    spec = pl.BlockSpec((CHIPS, per, height, n), lambda i: (0, i, 0, 0))

    def body(x_ref, q_ref, h_ref, c_ref, *refs):
        out_ref = refs[-1]
        dq = dot_first(x_ref[...], q_ref[...])
        do = dot_first(h_ref[...], c_ref[...])
        for t in range(per):
            for c in range(CHIPS):
                at = t * q_shard + c * q_piece
                parts = [dq[at : at + q_piece]]
                at = t * o_shard + c * o_piece
                parts += [do[at : at + o_piece, :n], do[at : at + o_piece, n:]]
                part = jnp.concatenate(parts, axis=0)
                if len(refs) == 2:
                    part = part + refs[0][c, t].astype(f32)
                out_ref[c, t] = part.astype(bf16)

    return pl.pallas_call(
        body,
        grid=(BLOCKS // per,),
        in_specs=[
            pl.BlockSpec((rows, per * q_shard), lambda i: (0, i)),
            pl.BlockSpec((rows, n), lambda i: (0, 0)),
            pl.BlockSpec((rows, per * o_shard), lambda i: (0, i)),
            pl.BlockSpec((rows, 2 * n), lambda i: (0, 0)),
        ] + [spec] * (got is not None),
        out_specs=spec,
        out_shape=jax.ShapeDtypeStruct((CHIPS, BLOCKS, height, n), bf16),
        compiler_params=params(),
        name="query_output_partial",
    )(x, q, heads, cot, *([] if got is None else [got]))


def other_core(x):
    return lax.ppermute(x, "roll", [(i, i ^ 1) for i in range(lax.axis_size("roll"))])


def from_behind(block, distance):
    return lax.ppermute(
        block, "tm", [(i - distance, i) for i in range(BLOCKS) if 0 <= i - distance < BLOCKS]
    )


def exchange(x, axis="tm", groups=None):
    return lax.all_to_all(
        x, axis, split_axis=0, concat_axis=0, tiled=True, axis_index_groups=groups
    )


def summed(parts):
    return jnp.sum(parts.astype(f32), axis=0).astype(bf16)


def over_chips(x):
    return summed(exchange(x, "roll", [[c + 2 * i for i in range(CHIPS)] for c in range(2)]))


def over_blocks(x):
    return summed(exchange(x))


def everyone(x):
    parts = exchange(jnp.broadcast_to(x, (2 * CHIPS, *x.shape)), "roll")
    return parts.reshape(CHIPS, 2, *x.shape)


def slots_exchange(x):
    return exchange(x.reshape(BLOCKS, CAP * TOK, GW)).reshape(x.shape)


def local(inputs, cotangent, memory_lists, w_query, w_key, w_value, w_output):
    model_width = inputs.shape[-1]
    inner = w_query.shape[1]
    position = lax.axis_index("tm")
    core = lax.axis_index("roll") % 2
    first_core = core == 0
    x = inputs.reshape(ROWS, model_width)
    cot = cotangent.reshape(ROWS, model_width)
    recalled = memory_lists[0]
    first_frame = position * FRAMES

    targets = jnp.arange(BLOCKS * FRAMES, dtype=jnp.int32)
    wanted = jnp.any(recalled.reshape(-1, 1) == targets[None, :], axis=0)
    wanted = wanted.astype(jnp.int32).reshape(BLOCKS, FRAMES)
    asked = exchange(wanted)

    keyval = keyval_rows(x, w_key, w_value)
    before = from_behind(keyval[:, (FRAMES - BAND) * TOK :], 1)
    queries = jnp.dot(x, w_query, preferred_element_type=f32).astype(bf16)
    grad_heads = dot_last(cot, w_output).astype(bf16)

    slot_rank = jnp.cumsum(wanted, axis=1) - 1
    slot_table = (jnp.arange(BLOCKS, dtype=jnp.int32)[:, None] * CAP + slot_rank).reshape(-1)
    mem_ok = recalled >= 0
    flat = jnp.where(mem_ok, recalled, 0).reshape(-1)
    hit = flat[:, None] == targets[None, :]
    slot_ids = jnp.sum(jnp.where(hit, slot_table[None, :], 0), axis=1)
    ok_flat = mem_ok.reshape(-1)
    read = jnp.clip(jnp.where(ok_flat, slot_ids, 0), 0, SPARE - 1)
    add = jnp.clip(jnp.where(ok_flat, slot_ids, SPARE), 0, SPARE)
    band_index = (
        jnp.arange(FRAMES, dtype=jnp.int32)[:, None] + jnp.arange(BAND + 1, dtype=jnp.int32)[None, :]
    )
    band_ok = first_frame + band_index - BAND >= 0
    key_valid = jnp.concatenate([band_ok, mem_ok], axis=1)
    bias = jnp.repeat(jnp.where(key_valid, 0.0, masked_score).astype(f32), TOK, axis=1)

    asked_rank = jnp.cumsum(asked, axis=1) - 1
    places = jnp.arange(CAP, dtype=jnp.int32)[None, :, None]
    chosen = (asked[:, None, :] > 0) & (asked_rank[:, None, :] == places)
    frame_no = jnp.arange(FRAMES, dtype=jnp.int32)[None, None, :]
    pick = jnp.sum(jnp.where(chosen, frame_no, 0), axis=2).reshape(-1)
    pick_add = jnp.where(jnp.any(chosen, axis=2).reshape(-1), pick, FRAMES)

    slots = [slots_exchange(named_frames(pick, keyval, g)) for g in range(GROUPS)]
    heads, dqs, owns, passed, returned = [], [], [], [], []
    for g in range(GROUPS):
        heads_g, dq_g, own_g, rim_g, dslot_g = attend(
            read, add, bias, queries, grad_heads, keyval, before, slots[g], g
        )
        returned.append(slots_exchange(dslot_g))
        passed.append(from_behind(rim_g, -1))
        heads.append(heads_g)
        dqs.append(dq_g)
        owns.append(own_g)

    heads_out = jnp.concatenate(heads, axis=1)
    grad_query = jnp.concatenate(dqs, axis=1)
    half_out = model_width // 2
    q_keep, q_send = jnp.where(first_core, dqs[0], dqs[1]), jnp.where(first_core, dqs[1], dqs[0])
    c_keep = jnp.where(first_core, cot[:, :half_out], cot[:, half_out:])
    c_send = jnp.where(first_core, cot[:, half_out:], cot[:, :half_out])
    got = other_core(query_output_partial(x, q_send, heads_out, c_send))
    share = over_blocks(over_chips(query_output_partial(x, q_keep, heads_out, c_keep, got)))
    both = everyone(share).astype(f32)
    piece = model_width // BLOCKS // CHIPS
    total_q = jnp.concatenate([both[:, c, :piece].reshape(-1, inner // 2) for c in range(2)], axis=1)
    o_piece = piece // 2
    total_o = jnp.concatenate(
        [
            both[:, c, piece + k * o_piece : piece + (k + 1) * o_piece].reshape(-1, inner // 2)
            for c in range(2)
            for k in range(2)
        ],
        axis=1,
    )
    attended = jnp.dot(heads_out, w_output, preferred_element_type=f32).astype(bf16)
    grad_input = dot_last(grad_query, w_query)

    k_cols, v_cols = [], []
    for g in range(GROUPS):
        dk, dv = collect(pick_add, owns[g], passed[g], returned[g])
        cols = slice(g * GH * HEAD, (g + 1) * GH * HEAD)
        grad_input = grad_input + dot_last(dk, w_key[:, cols]) + dot_last(dv, w_value[:, cols])
        keep, send = jnp.where(first_core, dk, dv), jnp.where(first_core, dv, dk)
        early = g < GROUPS - 1
        got = other_core(keyval_partial(x, send, None, early))
        total = keyval_partial(x, keep, got, early)
        if early:
            both = everyone(over_blocks(over_chips(total))).astype(f32)
            both = jnp.swapaxes(both, 0, 1).reshape(2, -1, total.shape[-1])
        else:
            both = jnp.sum(everyone(over_blocks(total)).astype(f32), axis=0)
        k_cols.append(both[0])
        v_cols.append(both[1])
    shape = (1, FRAMES, TOK, model_width)
    return (
        attended.reshape(shape),
        grad_input.astype(bf16).reshape(shape),
        total_q,
        jnp.concatenate(k_cols, axis=1),
        jnp.concatenate(v_cols, axis=1),
        total_o,
    )


def solution(mesh):
    block = P("roll", "tm", None, None)
    return jax.shard_map(
        local,
        mesh=mesh,
        in_specs=(block, block, P("roll", "tm", None), P(), P(), P(), P()),
        out_specs=(block, block, P("tm", None), P("tm", None), P("tm", None), P("tm", None)),
        check_vma=False,
    )
```

time: 532 us -> 494 us (0.929)
  blocking collectives: 45.7 us -> 0 us
  starting transfers between devices: 52.1 us -> 85.8 us
  Pallas kernels: 93.5 us -> 73.2 us
  between operations: 14 us -> 1.05 us
  local copies, waits for them, and re-layouts: 11.1 us -> 18.1 us
    all_to_all x6 -> x13, waiting for transfers between devices: 4.71 us -> 192 us  [exchange(): lax.all_to_all(x, axis, split_axis=0, concat_axis=0, tiled=True, axis_ind...]
    reduce_scatter x3 -> x0, waiting for transfers between devices: 107 us -> none  [the longest x1 65 us: local(): share_o = lax.psum_scatter(sum_o, 'tm', scatter_dimension=0, tiled=True)]
    ppermute x2 -> x3, waiting for transfers between devices: 157 us -> 76.4 us  [from_behind(): lax.ppermute(block, 'tm', [(i - distance, i) for i in range(BLOCKS) if 0...]
    all_gather x3 -> x0, blocking collectives: 45.7 us -> none  [over_chips(): every = lax.all_gather(total, 'roll', axis=0)]
    all_to_all x6 -> x13, starting transfers between devices: 41 us -> 74.6 us  [exchange(): lax.all_to_all(x, axis, split_axis=0, concat_axis=0, tiled=True, axis_ind...]
    pallas_call x1 -> x2, Pallas kernels: 48.3 us -> 21.4 us  [attend(): pl.pallas_call(attend_body, grid_spec=pltpu.PrefetchScalarGridSpec(num_sc...]
    convert_element_type x6 -> x0, other arithmetic: 15.1 us -> none  [the longest x3 14.9 us: core_sum(): return (kept.astype(f32) + other_core(sent).astype(f32)).astype(bf16)]
    reduce_sum x3 -> x6, other arithmetic: 0.08 us -> 9.1 us  [the longest x5 8.95 us: summed(): return jnp.sum(parts.astype(f32), axis=0).astype(bf16)]
  transfers between devices with their start and end apart: 14 -> 19, of which waited for: 5 -> 13; matrix products, arithmetic and copies ran while one was open for 9% -> 9% of each run, Pallas kernels for 8% -> 12%
where the time goes in v2:
time: 494 us; the launch traced here: 492 us
  waiting for transfers between devices  268 us (54%)
  starting transfers between devices  85.8 us (17%)
  Pallas kernels  73.2 us (15%)
  matrix products  27.4 us (6%)
  other arithmetic  18.4 us (4%)
  local copies, waits for them, and re-layouts  18.1 us (4%)
    all_to_all x13, waiting for transfers between devices, exchange(): lax.all_to_all(x, axis, split_axis=0, concat_axis=0, tiled=True, axis_ind...  192 us
    ppermute x3, waiting for transfers between devices, from_behind(): lax.ppermute(block, 'tm', [(i - distance, i) for i in range(BLOCKS) if 0...  76.4 us
    all_to_all x13, starting transfers between devices, exchange(): lax.all_to_all(x, axis, split_axis=0, concat_axis=0, tiled=True, axis_ind...  74.6 us
    pallas_call x2, Pallas kernels, attend(): pl.pallas_call(attend_body, grid_spec=pltpu.PrefetchScalarGridSpec(num_sc...  21.4 us
    dot_general x6, matrix products, dot_last(): lax.dot_general(left, right, (((1,), (1,)), ((), ())), preferred_element_...  18.6 us
    pallas_call x4, Pallas kernels, keyval_partial(): pl.pallas_call(body, grid=(m // cut,), in_specs=[pl.BlockSpec((rows, cut)...  17.8 us
    pallas_call x2, Pallas kernels, query_output_partial(): pl.pallas_call(body, grid=(BLOCKS // per,), in_specs=[pl.BlockSpec((rows,...  11.3 us
    unnamed x57, local copies, waits for them, and re-layouts  10.8 us
  transfers between devices with their start and end apart: 19, of which 13 were waited for; matrix products, arithmetic and copies ran while one was open for 9% of the time, Pallas kernels for 12%

profile of v2, /device:TPU:1, one launch (start us, length us, event | category | flops | bytes accessed | tf_op | source)
XLA Modules:
  0.0 492.1 jit_solution(3241216236603062837)
XLA Ops:
  2.2 8.6 %all-to-all-start = ((s32[16,1,8]{2,1,0:T(1,128)}), s32[16,1,8]{2,1,0:T(1,128)S(1)}, u32[]{:S(2)}, u32[]{:S(2)}) async-start(s32[16,1,8]{2,1,0:T(1,128)} %bitcast.3), calls=%async_computation | async-start | bytes 16384 | tf_op jit(solution)/shard_map/all_to_all | solution.py:320
  10.8 6.6 %keyval.1.kv_ref.own_ref = bf16[2,256,1024]{2,1,0:T(8,128)(2,1)} custom-call(bf16[256,2048]{1,0:T(8,128)(2,1)} %bitcast.49, bf16[2048,1024]{1,0:T(8,128)(2,1)} %wk_ref.1, bf16[2048,1024]{1,0:T(8,128)(2,1)} %wv_ref.1), custom_call_target="tpu_custom_call" | custom-call | tf_op jit(solution)/shard_map/keyval/pallas_call | solution.py:57
  22.3 6.7 %all-to-all-start.2 = ((bf16[16,96,1024]{2,1,0:T(8,128)(2,1)}), bf16[16,96,1024]{2,1,0:T(8,128)(2,1)S(1)}, u32[]{:S(2)}, u32[]{:S(2)}) async-start(bf16[16,96,1024]{2,1,0:T(8,128)(2,1)} %bitcast.60), calls=%async_computation.2 | async-start | bytes 6291456 | tf_op jit(solution)/shard_map/all_to_all | solution.py:320
  32.8 41.5 %all-to-all-done.2 = bf16[16,96,1024]{2,1,0:T(8,128)(2,1)S(1)} async-done(((bf16[16,96,1024]{2,1,0:T(8,128)(2,1)}), bf16[16,96,1024]{2,1,0:T(8,128)(2,1)S(1)}, u32[]{:S(2)}, u32[]{:S(2)}) %all-to-all-start.2) | async-done | bytes 3145760 | tf_op jit(solution)/shard_map/all_to_all | solution.py:320
  76.0 4.6 all-to-all-start.1
  85.1 4.3 convolution_convert_fusion.2.q_ref
  94.5 33.9 %collective-permute-done.prev_ref = bf16[2,128,1024]{2,1,0:T(8,128)(2,1)S(1)} collective-permute-done((bf16[2,128,1024]{2,1,0:T(8,128)(2,1)S(1)}, bf16[2,128,1024]{2,1,0:T(8,128)(2,1)S(1)}, u32[]{:S(2)}, u32[]{:S(2)}) %collective-permute-start) | collective-permute-done | bytes 524320 | tf_op jit(solution)/shard_map/ppermute | solution.py:314
  129.2 10.7 %attend.3 = (bf16[256,512]{1,0:T(8,128)(2,1)}, bf16[256,512]{1,0:T(8,128)(2,1)}, f32[256,1024]{1,0:T(8,128)}, bf16[128,1024]{1,0:T(8,128)(2,1)}, bf16[1536,1024]{1,0:T(8,128)(2,1)}) custom-call(s32[64]{0:T(128)} %get-tuple-element.53.read_ref, s32[64]{0:T(128)} %get-tuple-element.52.add_ref, f32[8,416]{1,0:T(8,128)} %reshape.131.bias_ref, ...), custom_call_target="tpu_custom_call" | custom-call | tf_op jit(solution)/shard_map/attend/pallas_call | solution.py:161
  139.9 10.3 %all-to-all-start.4 = ((bf16[16,96,1024]{2,1,0:T(8,128)(2,1)}), bf16[16,96,1024]{2,1,0:T(8,128)(2,1)S(1)}, u32[]{:S(2)}, u32[]{:S(2)}) async-start(bf16[16,96,1024]{2,1,0:T(8,128)(2,1)} %bitcast.65), calls=%async_computation.4 | async-start | bytes 6291456 | tf_op jit(solution)/shard_map/all_to_all | solution.py:320
  150.2 10.7 %attend.2 = (bf16[256,512]{1,0:T(8,128)(2,1)}, bf16[256,512]{1,0:T(8,128)(2,1)}, f32[256,1024]{1,0:T(8,128)}, bf16[128,1024]{1,0:T(8,128)(2,1)}, bf16[1536,1024]{1,0:T(8,128)(2,1)}) custom-call(s32[64]{0:T(128)} %get-tuple-element.53.read_ref, s32[64]{0:T(128)} %get-tuple-element.52.add_ref, f32[8,416]{1,0:T(8,128)} %reshape.131.bias_ref, ...), custom_call_target="tpu_custom_call" | custom-call | tf_op jit(solution)/shard_map/attend/pallas_call | solution.py:161
  160.9 30.8 %all-to-all-done.4 = bf16[16,96,1024]{2,1,0:T(8,128)(2,1)S(1)} async-done(((bf16[16,96,1024]{2,1,0:T(8,128)(2,1)}), bf16[16,96,1024]{2,1,0:T(8,128)(2,1)S(1)}, u32[]{:S(2)}, u32[]{:S(2)}) %all-to-all-start.4) | async-done | bytes 3145760 | tf_op jit(solution)/shard_map/all_to_all | solution.py:320
  193.5 5.8 %all-to-all-start.3 = ((bf16[16,96,1024]{2,1,0:T(8,128)(2,1)}), bf16[16,96,1024]{2,1,0:T(8,128)(2,1)}, u32[]{:S(2)}, u32[]{:S(2)}) async-start(bf16[16,96,1024]{2,1,0:T(8,128)(2,1)} %bitcast.64), calls=%async_computation.3 | async-start | bytes 6291456 | tf_op jit(solution)/shard_map/all_to_all | solution.py:320
  202.6 41.9 %collective-permute-done.2.rim_ref = bf16[128,1024]{1,0:T(8,128)(2,1)S(1)} collective-permute-done((bf16[128,1024]{1,0:T(8,128)(2,1)S(1)}, bf16[128,1024]{1,0:T(8,128)(2,1)S(1)}, u32[]{:S(2)}, u32[]{:S(2)}) %collective-permute-start.2) | collective-permute-done | bytes 262176 | tf_op jit(solution)/shard_map/ppermute | solution.py:314
  261.4 5.0 %collective-permute-start.4 = (bf16[4,16,32,512]{3,2,1,0:T(8,128)(2,1)}, bf16[4,16,32,512]{3,2,1,0:T(8,128)(2,1)S(1)}, u32[]{:S(2)}, u32[]{:S(2)}) collective-permute-start(bf16[4,16,32,512]{3,2,1,0:T(8,128)(2,1)} %keyval_partial.4), channel_id=1, source_target_pairs={{0,1},{1,0},{2,3},{3,2},{4,5},{5,4},{6,7},{7,6},{8,9},{9,8},{10,11... | collective-permute-start | bytes 6291464 | tf_op jit(solution)/shard_map/ppermute | solution.py:310
  274.6 5.2 %query_output_partial.2 = bf16[4,16,64,512]{3,2,1,0:T(8,128)(2,1)} custom-call(bf16[256,2048]{1,0:T(8,128)(2,1)} %bitcast.52, bf16[256,512]{1,0:T(8,128)(2,1)} %get-tuple-element.50.q_ref, bf16[256,1024]{1,0:T(8,128)(2,1)} %copy-done.7, bf16[256,1024]{1,0:T(8,128)(2,1)} %get-tuple-element.34.c_ref), custom_call_target="tpu_custom_call" | custom-call | tf_op jit(solution)/shard_map/query_output_partial/pallas_call | solution.py:293
  281.6 4.6 keyval_partial.5
  290.1 4.7 keyval_partial.7
  294.9 21.4 %all-to-all-done.8 = bf16[4,16,32,512]{3,2,1,0:T(8,128)(2,1)S(1)} async-done(((bf16[4,16,32,512]{3,2,1,0:T(8,128)(2,1)}), bf16[4,16,32,512]{3,2,1,0:T(8,128)(2,1)S(1)}, u32[]{:S(2)}, u32[]{:S(2)}) %all-to-all-start.8) | async-done | bytes 2097184 | tf_op jit(solution)/shard_map/all_to_all | solution.py:320
  324.4 26.4 %all-to-all-done.11 = bf16[16,128,512]{2,1,0:T(8,128)(2,1)S(1)} async-done(((bf16[16,128,512]{2,1,0:T(8,128)(2,1)}), bf16[16,128,512]{2,1,0:T(8,128)(2,1)S(1)}, u32[]{:S(2)}, u32[]{:S(2)}) %all-to-all-start.11) | async-done | bytes 2097184 | tf_op jit(solution)/shard_map/all_to_all | solution.py:320
  350.8 5.0 %all-to-all-start.9 = ((bf16[16,32,512]{2,1,0:T(8,128)(2,1)}), bf16[16,32,512]{2,1,0:T(8,128)(2,1)S(1)}, u32[]{:S(2)}, u32[]{:S(2)}) async-start(bf16[16,32,512]{2,1,0:T(8,128)(2,1)} %reduce_sum.91), calls=%async_computation.9 | async-start | bytes 1048576 | tf_op jit(solution)/shard_map/all_to_all | solution.py:320
  355.8 6.2 %query_output_partial.3 = bf16[4,16,64,512]{3,2,1,0:T(8,128)(2,1)} custom-call(bf16[256,2048]{1,0:T(8,128)(2,1)} %bitcast.55, bf16[256,512]{1,0:T(8,128)(2,1)} %get-tuple-element.51.q_ref, bf16[256,1024]{1,0:T(8,128)(2,1)} %copy-done.7, bf16[256,1024]{1,0:T(8,128)(2,1)} %get-tuple-element.35.c_ref, bf16[4,16,64,512]{3,2,1,0:T(8,128)(2,1)} %collective-permute-done.3.refs_0_), custom_call_target="tpu_custom_call" | custom-call | tf_op jit(solution)/shard_map/query_output_partial/pallas_call | solution.py:293
  362.0 4.4 all-to-all-done.9
  366.4 4.8 all-to-all-start.5
  371.3 4.4 convolution_convert_fusion
  375.8 42.6 %all-to-all-done.5 = bf16[4,16,64,512]{3,2,1,0:T(8,128)(2,1)} async-done(((bf16[4,16,64,512]{3,2,1,0:T(8,128)(2,1)}), bf16[4,16,64,512]{3,2,1,0:T(8,128)(2,1)}, u32[]{:S(2)}, u32[]{:S(2)}) %all-to-all-start.5) | async-done | bytes 4194336 | tf_op jit(solution)/shard_map/all_to_all | solution.py:320
  419.1 6.1 %all-to-all-start.10 = ((bf16[8,32,512]{2,1,0:T(8,128)(2,1)}), bf16[8,32,512]{2,1,0:T(8,128)(2,1)S(1)}, u32[]{:S(2)}, u32[]{:S(2)}) async-start(bf16[8,32,512]{2,1,0:T(8,128)(2,1)} %broadcast_in_dim.71), calls=%async_computation.10 | async-start | bytes 524288 | tf_op jit(solution)/shard_map/all_to_all | solution.py:320
  432.7 4.6 all-to-all-start.12
  452.3 4.3 all-to-all-start.6
  456.7 4.6 fusion.2
  461.6 11.1 %all-to-all-done.6 = bf16[16,64,512]{2,1,0:T(8,128)(2,1)} async-done(((bf16[16,64,512]{2,1,0:T(8,128)(2,1)}), bf16[16,64,512]{2,1,0:T(8,128)(2,1)}, u32[]{:S(2)}, u32[]{:S(2)}) %all-to-all-start.6) | async-done | bytes 1048608 | tf_op jit(solution)/shard_map/all_to_all | solution.py:320
  474.9 6.0 %all-to-all-start.7 = ((bf16[8,64,512]{2,1,0:T(8,128)(2,1)}), bf16[8,64,512]{2,1,0:T(8,128)(2,1)S(1)}, u32[]{:S(2)}, u32[]{:S(2)}) async-start(bf16[8,64,512]{2,1,0:T(8,128)(2,1)} %broadcast_in_dim.70), calls=%async_computation.7 | async-start | bytes 1048576 | tf_op jit(solution)/shard_map/all_to_all | solution.py:320
  482.6 7.7 %all-to-all-done.7 = bf16[8,64,512]{2,1,0:T(8,128)(2,1)S(1)} async-done(((bf16[8,64,512]{2,1,0:T(8,128)(2,1)}), bf16[8,64,512]{2,1,0:T(8,128)(2,1)S(1)}, u32[]{:S(2)}, u32[]{:S(2)}) %all-to-all-start.7) | async-done | bytes 524320 | tf_op jit(solution)/shard_map/all_to_all | solution.py:320
  (136 shorter events, 95.4 us)
Async XLA Ops:
  2.2 15.2 %all-to-all-start = ((s32[16,1,8]{2,1,0:T(1,128)}), s32[16,1,8]{2,1,0:T(1,128)S(1)}, u32[]{:S(2)}, u32[]{:S(2)}) async-start(s32[16,1,8]{2,1,0:T(1,128)} %bitcast.3), calls=%async_computation | async-start | bytes 16384 | tf_op jit(solution)/shard_map/all_to_all | solution.py:320
  22.3 52.0 %all-to-all-start.2 = ((bf16[16,96,1024]{2,1,0:T(8,128)(2,1)}), bf16[16,96,1024]{2,1,0:T(8,128)(2,1)S(1)}, u32[]{:S(2)}, u32[]{:S(2)}) async-start(bf16[16,96,1024]{2,1,0:T(8,128)(2,1)} %bitcast.60), calls=%async_computation.2 | async-start | bytes 6291456 | tf_op jit(solution)/shard_map/all_to_all | solution.py:320
  76.0 9.0 %copy-start.25 = (s32[1,8,8]{2,1,0:T(8,128)S(1)}, s32[1,8,8]{2,1,0:T(8,128)}, u32[]{:S(2)}) copy-start(s32[1,8,8]{2,1,0:T(8,128)} %param.9) | copy-start | bytes 772
  76.0 9.0 %copy-start = (bf16[1,8,32,2048]{3,2,1,0:T(8,128)(2,1)S(1)}, bf16[1,8,32,2048]{3,2,1,0:T(8,128)(2,1)}, u32[]{:S(2)}) copy-start(bf16[1,8,32,2048]{3,2,1,0:T(8,128)(2,1)} %param.7) | copy-start | bytes 3145732
  76.0 63.9 %all-to-all-start.1 = ((bf16[16,96,1024]{2,1,0:T(8,128)(2,1)}), bf16[16,96,1024]{2,1,0:T(8,128)(2,1)}, u32[]{:S(2)}, u32[]{:S(2)}) async-start(bf16[16,96,1024]{2,1,0:T(8,128)(2,1)} %bitcast.59), calls=%async_computation.1 | async-start | bytes 6291456 | tf_op jit(solution)/shard_map/all_to_all | solution.py:320
  80.7 47.7 %collective-permute-start = (bf16[2,128,1024]{2,1,0:T(8,128)(2,1)S(1)}, bf16[2,128,1024]{2,1,0:T(8,128)(2,1)S(1)}, u32[]{:S(2)}, u32[]{:S(2)}) collective-permute-start(bf16[2,128,1024]{2,1,0:T(8,128)(2,1)S(1)} %slice.72), channel_id=1, source_target_pairs={{0,8},{8,16},{16,24},{24,32},{32,40},{40,48},{48,56},{56,64},{64,7... | collective-permute-start | bytes 1572872 | tf_op jit(solution)/shard_map/ppermute | solution.py:314
  85.0 5.2 %copy-start.15 = (bf16[1,8,32,2048]{3,2,1,0:T(8,128)(2,1)S(1)}, bf16[1,8,32,2048]{3,2,1,0:T(8,128)(2,1)}, u32[]{:S(2)}) copy-start(bf16[1,8,32,2048]{3,2,1,0:T(8,128)(2,1)} %param.8) | copy-start | bytes 3145732
  139.9 51.8 %all-to-all-start.4 = ((bf16[16,96,1024]{2,1,0:T(8,128)(2,1)}), bf16[16,96,1024]{2,1,0:T(8,128)(2,1)S(1)}, u32[]{:S(2)}, u32[]{:S(2)}) async-start(bf16[16,96,1024]{2,1,0:T(8,128)(2,1)} %bitcast.65), calls=%async_computation.4 | async-start | bytes 6291456 | tf_op jit(solution)/shard_map/all_to_all | solution.py:320
  191.7 7.6 %copy-start.27 = (bf16[128,1024]{1,0:T(8,128)(2,1)S(1)}, bf16[128,1024]{1,0:T(8,128)(2,1)}, u32[]{:S(2)}) copy-start(bf16[128,1024]{1,0:T(8,128)(2,1)} %get-tuple-element.30) | copy-start | bytes 786436
  191.7 10.4 %copy-start.26 = (s32[48]{0:T(128)S(1)}, s32[48]{0:T(128)}, u32[]{:S(2)}) copy-start(s32[48]{0:T(128)} %reshape.134.pick_ref) | copy-start | bytes 580
  193.5 56.6 %all-to-all-start.3 = ((bf16[16,96,1024]{2,1,0:T(8,128)(2,1)}), bf16[16,96,1024]{2,1,0:T(8,128)(2,1)}, u32[]{:S(2)}, u32[]{:S(2)}) async-start(bf16[16,96,1024]{2,1,0:T(8,128)(2,1)} %bitcast.64), calls=%async_computation.3 | async-start | bytes 6291456 | tf_op jit(solution)/shard_map/all_to_all | solution.py:320
  199.3 45.3 %collective-permute-start.2 = (bf16[128,1024]{1,0:T(8,128)(2,1)S(1)}, bf16[128,1024]{1,0:T(8,128)(2,1)S(1)}, u32[]{:S(2)}, u32[]{:S(2)}) collective-permute-start(bf16[128,1024]{1,0:T(8,128)(2,1)S(1)} %copy-done.27), channel_id=1, source_target_pairs={{8,0},{16,8},{24,16},{32,24},{40,32},{48,40},{56,48},{64,56},{72,6... | collective-permute-start | bytes 786440 | tf_op jit(solution)/shard_map/ppermute | solution.py:314
  200.6 49.5 %collective-permute-start.1 = (bf16[128,1024]{1,0:T(8,128)(2,1)}, bf16[128,1024]{1,0:T(8,128)(2,1)S(1)}, u32[]{:S(2)}, u32[]{:S(2)}) collective-permute-start(bf16[128,1024]{1,0:T(8,128)(2,1)} %get-tuple-element.25), channel_id=1, source_target_pairs={{8,0},{16,8},{24,16},{32,24},{40,32},{48,40},{56,48},{64,56},{72,6... | collective-permute-start | bytes 786440 | tf_op jit(solution)/shard_map/ppermute | solution.py:314
  249.5 5.5 %copy-start.12 = (bf16[256,512]{1,0:T(8,128)(2,1)S(1)}, bf16[256,512]{1,0:T(8,128)(2,1)}, u32[]{:S(2)}) copy-start(bf16[256,512]{1,0:T(8,128)(2,1)} %get-tuple-element.32) | copy-start | bytes 786436
  249.5 5.5 %copy-start.14 = (bf16[256,512]{1,0:T(8,128)(2,1)S(1)}, bf16[256,512]{1,0:T(8,128)(2,1)}, u32[]{:S(2)}) copy-start(bf16[256,512]{1,0:T(8,128)(2,1)} %get-tuple-element.33) | copy-start | bytes 786436
  255.0 11.3 %copy-start.16 = (bf16[1,8,32,2048]{3,2,1,0:T(8,128)(2,1)S(1)}, bf16[1,8,32,2048]{3,2,1,0:T(8,128)(2,1)}, u32[]{:S(2)}) copy-start(bf16[1,8,32,2048]{3,2,1,0:T(8,128)(2,1)} %param.8) | copy-start | bytes 3145732
  261.4 12.3 %copy-start.19 = (bf16[256,512]{1,0:T(8,128)(2,1)S(1)}, bf16[256,512]{1,0:T(8,128)(2,1)}, u32[]{:S(2)}) copy-start(bf16[256,512]{1,0:T(8,128)(2,1)} %get-tuple-element.23) | copy-start | bytes 786436
  261.4 12.3 %copy-start.21 = (bf16[256,512]{1,0:T(8,128)(2,1)S(1)}, bf16[256,512]{1,0:T(8,128)(2,1)}, u32[]{:S(2)}) copy-start(bf16[256,512]{1,0:T(8,128)(2,1)} %get-tuple-element.22) | copy-start | bytes 786436
  261.4 18.9 %collective-permute-start.4 = (bf16[4,16,32,512]{3,2,1,0:T(8,128)(2,1)}, bf16[4,16,32,512]{3,2,1,0:T(8,128)(2,1)S(1)}, u32[]{:S(2)}, u32[]{:S(2)}) collective-permute-start(bf16[4,16,32,512]{3,2,1,0:T(8,128)(2,1)} %keyval_partial.4), channel_id=1, source_target_pairs={{0,1},{1,0},{2,3},{3,2},{4,5},{5,4},{6,7},{7,6},{8,9},{9,8},{10,11... | collective-permute-start | bytes 6291464 | tf_op jit(solution)/shard_map/ppermute | solution.py:310
  272.6 17.5 %collective-permute-start.5 = (bf16[16,128,512]{2,1,0:T(8,128)(2,1)}, bf16[16,128,512]{2,1,0:T(8,128)(2,1)}, u32[]{:S(2)}, u32[]{:S(2)}) collective-permute-start(bf16[16,128,512]{2,1,0:T(8,128)(2,1)} %keyval_partial.6), channel_id=1, source_target_pairs={{0,1},{1,0},{2,3},{3,2},{4,5},{5,4},{6,7},{7,6},{8,9},{9,8},{10,11... | collective-permute-start | bytes 6291464 | tf_op jit(solution)/shard_map/ppermute | solution.py:310
  279.8 76.1 %collective-permute-start.3 = (bf16[4,16,64,512]{3,2,1,0:T(8,128)(2,1)}, bf16[4,16,64,512]{3,2,1,0:T(8,128)(2,1)}, u32[]{:S(2)}, u32[]{:S(2)}) collective-permute-start(bf16[4,16,64,512]{3,2,1,0:T(8,128)(2,1)} %query_output_partial.2), channel_id=1, source_target_pairs={{0,1},{1,0},{2,3},{3,2},{4,5},{5,4},{6,7},{7,6},{8,9},{9,8},{10,11... | collective-permute-start | bytes 12582920 | tf_op jit(solution)/shard_map/ppermute | solution.py:310
  286.2 30.1 %all-to-all-start.8 = ((bf16[4,16,32,512]{3,2,1,0:T(8,128)(2,1)}), bf16[4,16,32,512]{3,2,1,0:T(8,128)(2,1)S(1)}, u32[]{:S(2)}, u32[]{:S(2)}) async-start(bf16[4,16,32,512]{3,2,1,0:T(8,128)(2,1)} %keyval_partial.5), calls=%async_computation.8 | async-start | bytes 4194304 | tf_op jit(solution)/shard_map/all_to_all | solution.py:320
  317.6 33.2 %all-to-all-start.11 = ((bf16[16,128,512]{2,1,0:T(8,128)(2,1)}), bf16[16,128,512]{2,1,0:T(8,128)(2,1)S(1)}, u32[]{:S(2)}, u32[]{:S(2)}) async-start(bf16[16,128,512]{2,1,0:T(8,128)(2,1)} %keyval_partial.7), calls=%async_computation.11 | async-start | bytes 4194304 | tf_op jit(solution)/shard_map/all_to_all | solution.py:320
  350.8 15.6 %all-to-all-start.9 = ((bf16[16,32,512]{2,1,0:T(8,128)(2,1)}), bf16[16,32,512]{2,1,0:T(8,128)(2,1)S(1)}, u32[]{:S(2)}, u32[]{:S(2)}) async-start(bf16[16,32,512]{2,1,0:T(8,128)(2,1)} %reduce_sum.91), calls=%async_computation.9 | async-start | bytes 1048576 | tf_op jit(solution)/shard_map/all_to_all | solution.py:320
  362.0 9.3 %copy-start.8 = (bf16[256,1024]{1,0:T(8,128)(2,1)S(1)}, bf16[256,1024]{1,0:T(8,128)(2,1)}, u32[]{:S(2)}) copy-start(bf16[256,1024]{1,0:T(8,128)(2,1)} %copy-done.7) | copy-start | bytes 1572868
  366.4 51.9 %all-to-all-start.5 = ((bf16[4,16,64,512]{3,2,1,0:T(8,128)(2,1)}), bf16[4,16,64,512]{3,2,1,0:T(8,128)(2,1)}, u32[]{:S(2)}, u32[]{:S(2)}) async-start(bf16[4,16,64,512]{3,2,1,0:T(8,128)(2,1)} %query_output_partial.3), calls=%async_computation.5 | async-start | bytes 8388608 | tf_op jit(solution)/shard_map/all_to_all | solution.py:320
  419.1 12.6 %all-to-all-start.10 = ((bf16[8,32,512]{2,1,0:T(8,128)(2,1)}), bf16[8,32,512]{2,1,0:T(8,128)(2,1)S(1)}, u32[]{:S(2)}, u32[]{:S(2)}) async-start(bf16[8,32,512]{2,1,0:T(8,128)(2,1)} %broadcast_in_dim.71), calls=%async_computation.10 | async-start | bytes 524288 | tf_op jit(solution)/shard_map/all_to_all | solution.py:320
  432.7 8.5 %copy-start.13 = (bf16[256,512]{1,0:T(8,128)(2,1)S(1)}, bf16[256,512]{1,0:T(8,128)(2,1)}, u32[]{:S(2)}) copy-start(bf16[256,512]{1,0:T(8,128)(2,1)} %get-tuple-element.27) | copy-start | bytes 786436
  432.7 19.6 %all-to-all-start.12 = ((bf16[8,128,512]{2,1,0:T(8,128)(2,1)}), bf16[8,128,512]{2,1,0:T(8,128)(2,1)S(1)}, u32[]{:S(2)}, u32[]{:S(2)}) async-start(bf16[8,128,512]{2,1,0:T(8,128)(2,1)} %broadcast_in_dim.72), calls=%async_computation.12 | async-start | bytes 2097152 | tf_op jit(solution)/shard_map/all_to_all | solution.py:320
  444.7 12.0 %copy-start.11 = (bf16[256,512]{1,0:T(8,128)(2,1)S(1)}, bf16[256,512]{1,0:T(8,128)(2,1)}, u32[]{:S(2)}) copy-start(bf16[256,512]{1,0:T(8,128)(2,1)} %get-tuple-element.28) | copy-start | bytes 786436
  452.3 20.4 %all-to-all-start.6 = ((bf16[16,64,512]{2,1,0:T(8,128)(2,1)}), bf16[16,64,512]{2,1,0:T(8,128)(2,1)}, u32[]{:S(2)}, u32[]{:S(2)}) async-start(bf16[16,64,512]{2,1,0:T(8,128)(2,1)} %reduce_sum.89), calls=%async_computation.6 | async-start | bytes 2097152 | tf_op jit(solution)/shard_map/all_to_all | solution.py:320
  474.9 15.4 %all-to-all-start.7 = ((bf16[8,64,512]{2,1,0:T(8,128)(2,1)}), bf16[8,64,512]{2,1,0:T(8,128)(2,1)S(1)}, u32[]{:S(2)}, u32[]{:S(2)}) async-start(bf16[8,64,512]{2,1,0:T(8,128)(2,1)} %broadcast_in_dim.70), calls=%async_computation.7 | async-start | bytes 1048576 | tf_op jit(solution)/shard_map/all_to_all | solution.py:320
  (15 other events, 32.6 us)

commit v3 on v2

v3 whole, which is shorter than its diff:
```python
import jax
import jax.numpy as jnp
from jax import lax
from jax.experimental import pallas as pl
from jax.experimental.pallas import tpu as pltpu
from jax.sharding import PartitionSpec as P


HEAD = 128
BAND = 4
MEM = 8
CAP = 3
FRAMES = 8
TOK = 32
BLOCKS = 16
ROWS = FRAMES * TOK
SPLIT = (4, 4)
KEYS = (BAND + 1 + MEM) * TOK
CHIPS = 4
SPARE = BLOCKS * CAP
masked_score = -1e30
f32, bf16 = jnp.float32, jnp.bfloat16
VMEM_LIMIT = 60 * 1024 * 1024


def params(n=1):
    return pltpu.CompilerParams(
        dimension_semantics=("arbitrary",) * n, vmem_limit_bytes=VMEM_LIMIT
    )


def dot_last(left, right):
    return lax.dot_general(left, right, (((1,), (1,)), ((), ())), preferred_element_type=f32)


def dot_first(left, right):
    return lax.dot_general(left, right, (((0,), (0,)), ((), ())), preferred_element_type=f32)


def dot(left, right):
    return lax.dot_general(left, right, (((1,), (0,)), ((), ())), preferred_element_type=f32)


def keyval_body(x_ref, wk_ref, wv_ref, out_ref):
    pieces = []
    for h in range(wk_ref.shape[1] // HEAD):
        pieces += [wk_ref[:, h * HEAD : (h + 1) * HEAD], wv_ref[:, h * HEAD : (h + 1) * HEAD]]
    out_ref[...] = dot(x_ref[...], jnp.concatenate(pieces, axis=1)).astype(bf16)


def keyval_rows(x, w_key, w_value):
    rows, width = x.shape
    cols = 256
    return pl.pallas_call(
        keyval_body,
        grid=(w_key.shape[1] // cols,),
        in_specs=[
            pl.BlockSpec((rows, width), lambda j: (0, 0)),
            pl.BlockSpec((width, cols), lambda j: (0, j)),
            pl.BlockSpec((width, cols), lambda j: (0, j)),
        ],
        out_specs=pl.BlockSpec((rows, 2 * cols), lambda j: (0, j)),
        out_shape=jax.ShapeDtypeStruct((rows, 2 * w_key.shape[1]), bf16),
        compiler_params=params(),
        name="keyval",
    )(x, w_key, w_value)


def send_body(pick_ref, kv_ref, out_ref, sem):
    def copy(i):
        at = pl.multiple_of(pick_ref[i] * TOK, TOK)
        return pltpu.make_async_copy(
            kv_ref.at[pl.ds(at, TOK), :], out_ref.at[pl.ds(i * TOK, TOK), :], sem.at[i]
        )

    for i in range(BLOCKS * CAP):
        copy(i).start()
    for i in range(BLOCKS * CAP):
        copy(i).wait()


def named_frames(pick, kv):
    width = kv.shape[1]
    return pl.pallas_call(
        send_body,
        grid_spec=pltpu.PrefetchScalarGridSpec(
            num_scalar_prefetch=1,
            grid=(1,),
            in_specs=[pl.BlockSpec((ROWS, width), lambda i, *_: (0, 0))],
            out_specs=pl.BlockSpec(memory_space=pl.ANY),
            scratch_shapes=[pltpu.SemaphoreType.DMA((BLOCKS * CAP,))],
        ),
        out_shape=jax.ShapeDtypeStruct((BLOCKS * CAP * TOK, width), bf16),
        compiler_params=params(),
        name="send",
    )(pick, kv)


def attend_body(
    read_ref, add_ref, bias_ref, q_ref, g_ref, own_ref, prev_ref, slot_ref,
    o_ref, dq_ref, down_ref, rim_ref, dslot_ref,
    acc_own, acc_prev, acc_slot, kv_scr, s_scr, gp_scr, half_scr, ds_scr,
):
    scale = HEAD ** (-0.5)
    acc_own[...] = jnp.zeros_like(acc_own)
    acc_prev[...] = jnp.zeros_like(acc_prev)
    acc_slot[...] = jnp.zeros_like(acc_slot)
    spans = [slice(f * TOK, (f + 1) * TOK) for f in range(FRAMES)]
    for f, rows in enumerate(spans):
        at = 0
        if f < BAND:
            at = (BAND - f) * TOK
            kv_scr[f, :at, :] = prev_ref[f * TOK : BAND * TOK, :]
        kv_scr[f, at : (BAND + 1) * TOK, :] = own_ref[max(f - BAND, 0) * TOK : (f + 1) * TOK, :]
        for m in range(MEM):
            at = pl.multiple_of(read_ref[f * MEM + m] * TOK, TOK)
            kv_scr[f, (BAND + 1 + m) * TOK : (BAND + 2 + m) * TOK, :] = slot_ref[pl.ds(at, TOK), :]
    for f, rows in enumerate(spans):
        s_scr[rows, :] = dot_last(q_ref[rows, :], kv_scr[f, :, :HEAD]) * scale + bias_ref[f : f + 1, :]
        gp_scr[rows, :] = dot_last(g_ref[rows, :], kv_scr[f, :, HEAD:])
    for rows in spans:
        s = s_scr[rows, :]
        gp = gp_scr[rows, :]
        e = jnp.exp(s - jnp.max(s, axis=1, keepdims=True))
        w = e * (1.0 / jnp.sum(e, axis=1, keepdims=True))
        half_scr[rows, :] = w.astype(bf16)
        ds_scr[rows, :] = (w * (gp - jnp.sum(w * gp, axis=1, keepdims=True))).astype(bf16)
    for f, rows in enumerate(spans):
        o_ref[rows, :] = dot(half_scr[rows, :], kv_scr[f, :, HEAD:]).astype(bf16)
        dq_ref[rows, :] = (dot(ds_scr[rows, :], kv_scr[f, :, :HEAD]) * scale).astype(bf16)
    for f, rows in enumerate(spans):
        dk = dot_first(ds_scr[rows, :], q_ref[rows, :]) * scale
        dv = dot_first(half_scr[rows, :], g_ref[rows, :])
        start = 0
        own = slice(max(f - BAND, 0) * TOK, (f + 1) * TOK)
        if f < BAND:
            start = (BAND - f) * TOK
            prev = slice(f * TOK, BAND * TOK)
            acc_prev[prev, :HEAD] += dk[:start]
            acc_prev[prev, HEAD:] += dv[:start]
        acc_own[own, :HEAD] += dk[start : (BAND + 1) * TOK]
        acc_own[own, HEAD:] += dv[start : (BAND + 1) * TOK]
        spots = [pl.multiple_of(add_ref[f * MEM + m] * TOK, TOK) for m in range(MEM)]
        base = (BAND + 1) * TOK
        for d, cols in ((dk, slice(0, HEAD)), (dv, slice(HEAD, 2 * HEAD))):
            olds = [acc_slot[pl.ds(at, TOK), cols] for at in spots]
            for m, at in enumerate(spots):
                acc_slot[pl.ds(at, TOK), cols] = olds[m] + d[base + m * TOK : base + (m + 1) * TOK]
    down_ref[...] = acc_own[...]
    rim_ref[...] = acc_prev[...].astype(bf16)
    dslot_ref[...] = acc_slot[: SPARE * TOK, :].astype(bf16)


def attend(read, add, bias, q, g, own, prev, slots, first, heads):
    col = lambda rows, width: pl.BlockSpec((rows, width), lambda h, *_: (0, h))
    src = lambda rows, width: pl.BlockSpec((rows, width), lambda h, *_: (0, h + first))
    return pl.pallas_call(
        attend_body,
        grid_spec=pltpu.PrefetchScalarGridSpec(
            num_scalar_prefetch=2,
            grid=(heads,),
            in_specs=[
                pl.BlockSpec(bias.shape, lambda h, *_: (0, 0)),
                src(ROWS, HEAD), src(ROWS, HEAD),
                src(ROWS, 2 * HEAD), src(BAND * TOK, 2 * HEAD), src(SPARE * TOK, 2 * HEAD),
            ],
            out_specs=[
                col(ROWS, HEAD), col(ROWS, HEAD),
                col(ROWS, 2 * HEAD), col(BAND * TOK, 2 * HEAD), col(SPARE * TOK, 2 * HEAD),
            ],
            scratch_shapes=[
                pltpu.VMEM((ROWS, 2 * HEAD), f32),
                pltpu.VMEM((BAND * TOK, 2 * HEAD), f32),
                pltpu.VMEM(((SPARE + 1) * TOK, 2 * HEAD), f32),
                pltpu.VMEM((FRAMES, KEYS, 2 * HEAD), bf16),
                pltpu.VMEM((ROWS, KEYS), f32),
                pltpu.VMEM((ROWS, KEYS), f32),
                pltpu.VMEM((ROWS, KEYS), bf16),
                pltpu.VMEM((ROWS, KEYS), bf16),
            ],
        ),
        out_shape=[
            jax.ShapeDtypeStruct((ROWS, heads * HEAD), bf16),
            jax.ShapeDtypeStruct((ROWS, heads * HEAD), bf16),
            jax.ShapeDtypeStruct((ROWS, 2 * heads * HEAD), f32),
            jax.ShapeDtypeStruct((BAND * TOK, 2 * heads * HEAD), bf16),
            jax.ShapeDtypeStruct((SPARE * TOK, 2 * heads * HEAD), bf16),
        ],
        compiler_params=params(),
        name="attend",
    )(read, add, bias, q, g, own, prev, slots)


def collect_body(pick_ref, own_ref, rim_ref, back_ref, out_ref, acc):
    acc[:ROWS, :] = own_ref[...]
    acc[ROWS:, :] = jnp.zeros_like(acc[ROWS:, :])
    tail = slice((FRAMES - BAND) * TOK, ROWS)
    acc[tail, :] += rim_ref[...].astype(f32)
    for i in range(BLOCKS * CAP):
        at = pl.multiple_of(pick_ref[i] * TOK, TOK)
        acc[pl.ds(at, TOK), :] += back_ref[i * TOK : (i + 1) * TOK, :].astype(f32)
    for h in range(own_ref.shape[1] // (2 * HEAD)):
        for kind in range(2):
            left = (2 * h + kind) * HEAD
            out_ref[kind, :, h * HEAD : (h + 1) * HEAD] = acc[:ROWS, left : left + HEAD].astype(bf16)


def collect(pick, own, rim, back):
    width = own.shape[1]
    cols = min(512, width)
    col = lambda rows, w: pl.BlockSpec((rows, w), lambda h, *_: (0, h))
    return pl.pallas_call(
        collect_body,
        grid_spec=pltpu.PrefetchScalarGridSpec(
            num_scalar_prefetch=1,
            grid=(width // cols,),
            in_specs=[col(ROWS, cols), col(BAND * TOK, cols), col(SPARE * TOK, cols)],
            out_specs=pl.BlockSpec((2, ROWS, cols // 2), lambda h, *_: (0, 0, h)),
            scratch_shapes=[pltpu.VMEM((ROWS + TOK, cols), f32)],
        ),
        out_shape=jax.ShapeDtypeStruct((2, ROWS, width // 2), bf16),
        compiler_params=params(),
        name="collect",
    )(pick, own, rim, back)


def taken(right):
    if right.ndim == 3:
        rows, n = right.shape[1:]
        return n, pl.BlockSpec((None, rows, n), lambda i, s, *_: (s[1], 0, 0))
    rows, n = right.shape
    return n // 2, pl.BlockSpec((rows, n // 2), lambda i, s, *_: (0, s[1]))


def partial_call(pairs, shards, width, scalars, got=None):
    per = 4
    cuts = [taken(right) for _, right in pairs]
    height = sum(s // CHIPS * (n // width) for (n, _), s in zip(cuts, shards))
    rows = pairs[0][0].shape[0]
    keep = got is not None

    def body(chip_ref, *refs):
        factors, refs = refs[: 2 * len(pairs)], refs[2 * len(pairs) :]
        totals = refs[-len(pairs) :]
        for k, total in enumerate(totals):
            total[...] = dot_first(factors[2 * k][...], factors[2 * k + 1][...])
        for t in range(per):
            for d in range(CHIPS):
                c = lax.rem(chip_ref[0] + d, CHIPS) if keep else d
                at = 0
                for total, shard in zip(totals, shards):
                    piece = shard // CHIPS
                    first = t * shard + c * piece
                    if keep:
                        first = pl.multiple_of(first, piece)
                    for left in range(0, total.shape[1], width):
                        part = total[pl.ds(first, piece), left : left + width]
                        here = slice(at, at + piece)
                        if keep:
                            part = part + refs[0][c, t, here, :].astype(f32)
                            refs[1 + d][t, here, :] = part.astype(bf16)
                        else:
                            refs[0][c, t, here, :] = part.astype(bf16)
                        at += piece

    whole = pl.BlockSpec((CHIPS, per, height, width), lambda i, *_: (0, i, 0, 0))
    one = pl.BlockSpec((per, height, width), lambda i, *_: (i, 0, 0))
    in_specs, operands = [], []
    for (left, right), shard, (_, spec) in zip(pairs, shards, cuts):
        in_specs += [pl.BlockSpec((rows, per * shard), lambda i, *_: (0, i)), spec]
        operands += [left, right]
    if keep:
        in_specs.append(whole)
        operands.append(got)
        out_specs = [one] * CHIPS
        out_shape = [jax.ShapeDtypeStruct((BLOCKS, height, width), bf16)] * CHIPS
    else:
        out_specs = whole
        out_shape = jax.ShapeDtypeStruct((CHIPS, BLOCKS, height, width), bf16)
    return pl.pallas_call(
        body,
        grid_spec=pltpu.PrefetchScalarGridSpec(
            num_scalar_prefetch=1,
            grid=(BLOCKS // per,),
            in_specs=in_specs,
            out_specs=out_specs,
            scratch_shapes=[
                pltpu.VMEM((per * s, n), f32) for (n, _), s in zip(cuts, shards)
            ],
        ),
        out_shape=out_shape,
        compiler_params=params(),
    )(scalars, *operands)


def last_partial(x, g, scalars, got=None):
    rows, m = x.shape
    n, right = taken(g)
    shard, per = m // BLOCKS, 4
    spec = pl.BlockSpec((per, shard, n), lambda i, *_: (i, 0, 0))

    def body(s_ref, a_ref, b_ref, *refs):
        total = dot_first(a_ref[...], b_ref[...])
        for t in range(per):
            part = total[t * shard : (t + 1) * shard]
            if got is not None:
                part = part + refs[0][t].astype(f32)
            refs[-1][t] = part.astype(bf16)

    return pl.pallas_call(
        body,
        grid_spec=pltpu.PrefetchScalarGridSpec(
            num_scalar_prefetch=1,
            grid=(BLOCKS // per,),
            in_specs=[pl.BlockSpec((rows, per * shard), lambda i, *_: (0, i)), right]
            + [spec] * (got is not None),
            out_specs=spec,
        ),
        out_shape=jax.ShapeDtypeStruct((BLOCKS, shard, n), bf16),
        compiler_params=params(),
        name="last_partial",
    )(scalars, x, g, *([] if got is None else [got]))


def other_core(x):
    return lax.ppermute(x, "roll", [(i, i ^ 1) for i in range(lax.axis_size("roll"))])


def from_behind(block, distance):
    return lax.ppermute(
        block, "tm", [(i - distance, i) for i in range(BLOCKS) if 0 <= i - distance < BLOCKS]
    )


def exchange(x, axis="tm", groups=None):
    return lax.all_to_all(
        x, axis, split_axis=0, concat_axis=0, tiled=True, axis_index_groups=groups
    )


def summed(parts):
    return jnp.sum(parts.astype(f32), axis=0).astype(bf16)


def over_chips(pieces):
    total = pieces[0].astype(f32)
    n = 2 * CHIPS
    for d in range(1, CHIPS):
        got = lax.ppermute(pieces[d], "roll", [(i, (i + 2 * d) % n) for i in range(n)])
        total = total + got.astype(f32)
    return total.astype(bf16)


def everyone(x):
    parts = exchange(jnp.broadcast_to(x, (2 * CHIPS, *x.shape)), "roll")
    return parts.reshape(CHIPS, 2, *x.shape)


def slots_exchange(x):
    return exchange(x.reshape(BLOCKS, CAP * TOK, x.shape[1])).reshape(x.shape)


def step(inputs, cotangent, memory_lists, w_query, w_key, w_value, w_output):
    model_width = inputs.shape[-1]
    inner = w_query.shape[1]
    half = inner // 2
    position = lax.axis_index("tm")
    core = lax.axis_index("roll") % 2
    chip = lax.axis_index("roll") // 2
    keeping = jnp.stack([chip, core]).astype(jnp.int32)
    sending = jnp.stack([chip, 1 - core]).astype(jnp.int32)
    x = inputs.reshape(ROWS, model_width)
    cot = cotangent.reshape(ROWS, model_width)
    recalled = memory_lists[0]
    first_frame = position * FRAMES

    targets = jnp.arange(BLOCKS * FRAMES, dtype=jnp.int32)
    wanted = jnp.any(recalled.reshape(-1, 1) == targets[None, :], axis=0)
    wanted = wanted.astype(jnp.int32).reshape(BLOCKS, FRAMES)
    asked = exchange(wanted)

    keyval = keyval_rows(x, w_key, w_value)
    before = from_behind(keyval[(FRAMES - BAND) * TOK :], 1)
    queries = jnp.dot(x, w_query, preferred_element_type=f32).astype(bf16)
    grad_heads = dot_last(cot, w_output).astype(bf16)

    slot_rank = jnp.cumsum(wanted, axis=1) - 1
    slot_table = (jnp.arange(BLOCKS, dtype=jnp.int32)[:, None] * CAP + slot_rank).reshape(-1)
    mem_ok = recalled >= 0
    flat = jnp.where(mem_ok, recalled, 0).reshape(-1)
    hit = flat[:, None] == targets[None, :]
    slot_ids = jnp.sum(jnp.where(hit, slot_table[None, :], 0), axis=1)
    ok_flat = mem_ok.reshape(-1)
    read = jnp.clip(jnp.where(ok_flat, slot_ids, 0), 0, SPARE - 1)
    add = jnp.clip(jnp.where(ok_flat, slot_ids, SPARE), 0, SPARE)
    band_index = (
        jnp.arange(FRAMES, dtype=jnp.int32)[:, None] + jnp.arange(BAND + 1, dtype=jnp.int32)[None, :]
    )
    band_ok = first_frame + band_index - BAND >= 0
    key_valid = jnp.concatenate([band_ok, mem_ok], axis=1)
    bias = jnp.repeat(jnp.where(key_valid, 0.0, masked_score).astype(f32), TOK, axis=1)

    asked_rank = jnp.cumsum(asked, axis=1) - 1
    places = jnp.arange(CAP, dtype=jnp.int32)[None, :, None]
    chosen = (asked[:, None, :] > 0) & (asked_rank[:, None, :] == places)
    frame_no = jnp.arange(FRAMES, dtype=jnp.int32)[None, None, :]
    pick = jnp.sum(jnp.where(chosen, frame_no, 0), axis=2).reshape(-1)
    pick_add = jnp.where(jnp.any(chosen, axis=2).reshape(-1), pick, FRAMES)

    outgoing = named_frames(pick, keyval)
    slots = slots_exchange(outgoing)
    heads, dqs, owns, passed, returned = [], [], [], [], []
    first = 0
    for count in SPLIT:
        heads_g, dq_g, own_g, rim_g, dslot_g = attend(
            read, add, bias, queries, grad_heads, keyval, before, slots, first, count
        )
        passed.append(from_behind(rim_g, -1))
        returned.append(slots_exchange(dslot_g))
        heads.append(heads_g)
        dqs.append(dq_g)
        owns.append(own_g)
        first += count

    heads_out = jnp.concatenate(heads, axis=1)
    grad_query = jnp.concatenate(dqs, axis=1)
    shards = [model_width // BLOCKS, inner // BLOCKS]
    sent = partial_call([(x, grad_query), (heads_out, cot)], shards, half, sending)
    got = other_core(sent)
    kept = partial_call([(x, grad_query), (heads_out, cot)], shards, half, keeping, got)
    sum_qo = over_chips(kept)
    attended = jnp.dot(heads_out, w_output, preferred_element_type=f32).astype(bf16)
    grad_input = dot_last(grad_query, w_query)

    dks, dvs = [], []
    for g, count in enumerate(SPLIT):
        dkv = collect(pick_add, owns[g], passed[g], returned[g])
        dks.append(dkv[0])
        dvs.append(dkv[1])
        width = count * HEAD
        if g == 0:
            sent = partial_call([(x, dkv)], shards[:1], width, sending)
            got = other_core(sent)
            kept = partial_call([(x, dkv)], shards[:1], width, keeping, got)
            sum_kv = over_chips(kept)
            early = summed(exchange(jnp.concatenate([sum_qo, sum_kv], axis=1)))
        else:
            sent = last_partial(x, dkv, sending)
            got = other_core(sent)
            kept = last_partial(x, dkv, keeping, got)
            late = summed(exchange(kept))
    both = everyone(jnp.concatenate([early, late], axis=0)).astype(f32)
    piece = model_width // BLOCKS // CHIPS
    o_piece = inner // BLOCKS // CHIPS
    total_q = jnp.concatenate([both[:, c, :piece].reshape(-1, half) for c in range(2)], axis=1)
    total_o = jnp.concatenate(
        [
            both[:, c, piece + k * o_piece : piece + (k + 1) * o_piece].reshape(-1, half)
            for c in range(2)
            for k in range(2)
        ],
        axis=1,
    )
    at = piece + 2 * o_piece
    kv_first = both[:, :, at : at + piece]
    kv_last = jnp.sum(both[:, :, at + piece :], axis=0)
    total_k, total_v = (
        jnp.concatenate([kv_first[:, c].reshape(-1, half), kv_last[c]], axis=1) for c in range(2)
    )
    grad_input = (
        grad_input
        + dot_last(jnp.concatenate(dks, axis=1), w_key)
        + dot_last(jnp.concatenate(dvs, axis=1), w_value)
    )
    shape = (1, FRAMES, TOK, model_width)
    return (
        attended.reshape(shape),
        grad_input.astype(bf16).reshape(shape),
        total_q,
        total_k,
        total_v,
        total_o,
    )


def solution(mesh):
    block = P("roll", "tm", None, None)
    return jax.shard_map(
        step,
        mesh=mesh,
        in_specs=(block, block, P("roll", "tm", None), P(), P(), P(), P()),
        out_specs=(block, block, P("tm", None), P("tm", None), P("tm", None), P("tm", None)),
        check_vma=False,
    )
```

time: 494 us -> 438 us (0.89)
  waiting for transfers between devices: 268 us -> 235 us
  starting transfers between devices: 85.8 us -> 76.2 us
  matrix products: 27.4 us -> 20.2 us
  other arithmetic: 18.4 us -> 13.4 us
    all_to_all x13 -> x7, waiting for transfers between devices: 192 us -> 49 us  [exchange(): lax.all_to_all(x, axis, split_axis=0, concat_axis=0, tiled=True, axis_ind...]
    ppermute x0 -> x6, waiting for transfers between devices: none -> 55.7 us  [over_chips(): lax.ppermute(pieces[d], 'roll', [(i, (i + 2 * d) % n) for i in range(n)])]
    ppermute x3, waiting for transfers between devices: 76.4 us -> 130 us  [from_behind(): lax.ppermute(block, 'tm', [(i - distance, i) for i in range(BLOCKS) if 0...]
    all_to_all x13 -> x7, starting transfers between devices: 74.6 us -> 56.6 us  [exchange(): lax.all_to_all(x, axis, split_axis=0, concat_axis=0, tiled=True, axis_ind...]
    ppermute x0 -> x6, starting transfers between devices: none -> 7.45 us  [over_chips(): lax.ppermute(pieces[d], 'roll', [(i, (i + 2 * d) % n) for i in range(n)])]
    dot_general x6 -> x4, matrix products: 18.6 us -> 11.5 us  [dot_last(): lax.dot_general(left, right, (((1,), (1,)), ((), ())), preferred_element_...]
    reduce_sum x5 -> x2, other arithmetic: 8.95 us -> 1.93 us  [summed(): return jnp.sum(parts.astype(f32), axis=0).astype(bf16)]
    pallas_call x6, Pallas kernels: 29.2 us -> 34.1 us  [the longest x4 23.9 us: partial_call(): pl.pallas_call(body, grid_spec=pltpu.PrefetchScalarGridSpec(num_scalar_pr...]
  transfers between devices with their start and end apart: 19 -> 19, of which waited for: 13 -> 11; matrix products, arithmetic and copies ran while one was open for 9% -> 7% of each run, Pallas kernels for 12% -> 14%
where the time goes in v3:
time: 438 us; the launch traced here: 437 us
  waiting for transfers between devices  235 us (54%)
  starting transfers between devices  76.2 us (17%)
  Pallas kernels  75.5 us (17%)
  matrix products  20.2 us (5%)
  local copies, waits for them, and re-layouts  15.1 us (3%)
  other arithmetic  13.4 us (3%)
    ppermute x3, waiting for transfers between devices, from_behind(): lax.ppermute(block, 'tm', [(i - distance, i) for i in range(BLOCKS) if 0...  130 us
    all_to_all x7, starting transfers between devices, exchange(): lax.all_to_all(x, axis, split_axis=0, concat_axis=0, tiled=True, axis_ind...  56.6 us
    ppermute x6, waiting for transfers between devices, over_chips(): lax.ppermute(pieces[d], 'roll', [(i, (i + 2 * d) % n) for i in range(n)])  55.7 us
    all_to_all x7, waiting for transfers between devices, exchange(): lax.all_to_all(x, axis, split_axis=0, concat_axis=0, tiled=True, axis_ind...  49 us
    pallas_call x4, Pallas kernels, partial_call(): pl.pallas_call(body, grid_spec=pltpu.PrefetchScalarGridSpec(num_scalar_pr...  23.9 us
    pallas_call x2, Pallas kernels, attend(): pl.pallas_call(attend_body, grid_spec=pltpu.PrefetchScalarGridSpec(num_sc...  21.5 us
    dot_general x4, matrix products, dot_last(): lax.dot_general(left, right, (((1,), (1,)), ((), ())), preferred_element_...  11.5 us
    pallas_call x2, Pallas kernels, last_partial(): pl.pallas_call(body, grid_spec=pltpu.PrefetchScalarGridSpec(num_scalar_pr...  10.3 us
  transfers between devices with their start and end apart: 19, of which 11 were waited for; matrix products, arithmetic and copies ran while one was open for 7% of the time, Pallas kernels for 14%

profile of v3, /device:TPU:1, one launch (start us, length us, event | category | flops | bytes accessed | tf_op | source)
XLA Modules:
  0.0 436.8 jit_solution(272867868952069819)
XLA Ops:
  2.2 8.6 %all-to-all-start = ((s32[16,1,8]{2,1,0:T(1,128)}), s32[16,1,8]{2,1,0:T(1,128)S(1)}, u32[]{:S(2)}, u32[]{:S(2)}) async-start(s32[16,1,8]{2,1,0:T(1,128)} %bitcast.3), calls=%async_computation | async-start | bytes 16384 | tf_op jit(solution)/shard_map/all_to_all | solution.py:336
  10.8 6.6 %keyval.1.kv_ref.own_ref = bf16[256,2048]{1,0:T(8,128)(2,1)} custom-call(bf16[256,2048]{1,0:T(8,128)(2,1)} %bitcast.52, bf16[2048,1024]{1,0:T(8,128)(2,1)} %wk_ref.1, bf16[2048,1024]{1,0:T(8,128)(2,1)} %wv_ref.1), custom_call_target="tpu_custom_call" | custom-call | tf_op jit(solution)/shard_map/keyval/pallas_call | solution.py:54
  18.5 4.9 %send.1 = bf16[1536,2048]{1,0:T(8,128)(2,1)} custom-call(s32[48]{0:T(128)} %reshape.117.pick_ref, bf16[256,2048]{1,0:T(8,128)(2,1)} %keyval.1.kv_ref.own_ref), custom_call_target="tpu_custom_call" | custom-call | tf_op jit(solution)/shard_map/send/pallas_call | solution.py:84
  23.5 6.8 %all-to-all-start.1 = ((bf16[16,96,2048]{2,1,0:T(8,128)(2,1)}), bf16[16,96,2048]{2,1,0:T(8,128)(2,1)}, u32[]{:S(2)}, u32[]{:S(2)}) async-start(bf16[16,96,2048]{2,1,0:T(8,128)(2,1)} %bitcast.60), calls=%async_computation.1 | async-start | bytes 12582912 | tf_op jit(solution)/shard_map/all_to_all | solution.py:336
  34.9 4.3 convolution_convert_fusion.2.q_ref
  40.0 4.3 convolution_convert_fusion.1.g_ref
  44.3 78.8 %collective-permute-done.prev_ref = bf16[128,2048]{1,0:T(8,128)(2,1)S(1)} collective-permute-done((bf16[128,2048]{1,0:T(8,128)(2,1)S(1)}, bf16[128,2048]{1,0:T(8,128)(2,1)S(1)}, u32[]{:S(2)}, u32[]{:S(2)}) %collective-permute-start) | collective-permute-done | bytes 524320 | tf_op jit(solution)/shard_map/ppermute | solution.py:330
  123.9 10.7 %attend.3 = (bf16[256,512]{1,0:T(8,128)(2,1)}, bf16[256,512]{1,0:T(8,128)(2,1)}, f32[256,1024]{1,0:T(8,128)}, bf16[128,1024]{1,0:T(8,128)(2,1)}, bf16[1536,1024]{1,0:T(8,128)(2,1)}) custom-call(s32[64]{0:T(128)} %get-tuple-element.57.read_ref, s32[64]{0:T(128)} %get-tuple-element.56.add_ref, f32[8,416]{1,0:T(8,128)} %reshape.114.bias_ref, ...), custom_call_target="tpu_custom_call" | custom-call | tf_op jit(solution)/shard_map/attend/pallas_call | solution.py:157
  134.6 13.4 %all-to-all-start.3 = ((bf16[16,96,1024]{2,1,0:T(8,128)(2,1)}), bf16[16,96,1024]{2,1,0:T(8,128)(2,1)S(1)}, u32[]{:S(2)}, u32[]{:S(2)}) async-start(bf16[16,96,1024]{2,1,0:T(8,128)(2,1)} %bitcast.65), calls=%async_computation.3 | async-start | bytes 6291456 | tf_op jit(solution)/shard_map/all_to_all | solution.py:336
  148.7 10.8 %attend.2 = (bf16[256,512]{1,0:T(8,128)(2,1)}, bf16[256,512]{1,0:T(8,128)(2,1)}, f32[256,1024]{1,0:T(8,128)}, bf16[128,1024]{1,0:T(8,128)(2,1)}, bf16[1536,1024]{1,0:T(8,128)(2,1)}) custom-call(s32[64]{0:T(128)} %get-tuple-element.57.read_ref, s32[64]{0:T(128)} %get-tuple-element.56.add_ref, f32[8,416]{1,0:T(8,128)} %reshape.114.bias_ref, ...), custom_call_target="tpu_custom_call" | custom-call | tf_op jit(solution)/shard_map/attend/pallas_call | solution.py:157
  163.2 5.9 %shard_map.118 = bf16[4,16,64,512]{3,2,1,0:T(8,128)(2,1)} custom-call(s32[2]{0:T(128)} %pad_add_fusion.1.chip_ref.s_ref, bf16[256,2048]{1,0:T(8,128)(2,1)} %bitcast.53, bf16[256,1024]{1,0:T(8,128)(2,1)} %copy-done.5, bf16[256,1024]{1,0:T(8,128)(2,1)} %copy-done.10, bf16[256,2048]{1,0:T(8,128)(2,1)} %bitcast.62), custom_call_target="tpu_custom_call" | custom-call | tf_op jit(solution)/shard_map/pallas_call | solution.py:280
  171.7 17.8 %all-to-all-done.3 = bf16[16,96,1024]{2,1,0:T(8,128)(2,1)S(1)} async-done(((bf16[16,96,1024]{2,1,0:T(8,128)(2,1)}), bf16[16,96,1024]{2,1,0:T(8,128)(2,1)S(1)}, u32[]{:S(2)}, u32[]{:S(2)}) %all-to-all-start.3) | async-done | bytes 3145760 | tf_op jit(solution)/shard_map/all_to_all | solution.py:336
  191.1 5.9 %all-to-all-start.2 = ((bf16[16,96,1024]{2,1,0:T(8,128)(2,1)}), bf16[16,96,1024]{2,1,0:T(8,128)(2,1)}, u32[]{:S(2)}, u32[]{:S(2)}) async-start(bf16[16,96,1024]{2,1,0:T(8,128)(2,1)} %bitcast.66), calls=%async_computation.2 | async-start | bytes 6291456 | tf_op jit(solution)/shard_map/all_to_all | solution.py:336
  199.1 43.2 %collective-permute-done.2.rim_ref = bf16[128,1024]{1,0:T(8,128)(2,1)S(1)} collective-permute-done((bf16[128,1024]{1,0:T(8,128)(2,1)}, bf16[128,1024]{1,0:T(8,128)(2,1)S(1)}, u32[]{:S(2)}, u32[]{:S(2)}) %collective-permute-start.2) | collective-permute-done | bytes 262176 | tf_op jit(solution)/shard_map/ppermute | solution.py:330
  243.1 4.3 collect.3.b_ref
  247.3 4.9 %last_partial.2 = bf16[16,128,512]{2,1,0:T(8,128)(2,1)} custom-call(s32[2]{0:T(128)} %pad_add_fusion.1.chip_ref.s_ref, bf16[256,2048]{1,0:T(8,128)(2,1)} %bitcast.54, bf16[2,256,512]{2,1,0:T(8,128)(2,1)} %collect.3.b_ref), custom_call_target="tpu_custom_call" | custom-call | tf_op jit(solution)/shard_map/last_partial/pallas_call | solution.py:310
  256.5 8.4 %collective-permute-done.1.rim_ref = bf16[128,1024]{1,0:T(8,128)(2,1)S(1)} collective-permute-done((bf16[128,1024]{1,0:T(8,128)(2,1)S(1)}, bf16[128,1024]{1,0:T(8,128)(2,1)S(1)}, u32[]{:S(2)}, u32[]{:S(2)}) %collective-permute-start.1) | collective-permute-done | bytes 262176 | tf_op jit(solution)/shard_map/ppermute | solution.py:330
  265.6 4.1 collect.2.refs_1_
  269.7 5.0 %shard_map.120 = bf16[4,16,32,512]{3,2,1,0:T(8,128)(2,1)} custom-call(s32[2]{0:T(128)} %pad_add_fusion.1.chip_ref.s_ref, bf16[256,2048]{1,0:T(8,128)(2,1)} %bitcast.55, bf16[2,256,512]{2,1,0:T(8,128)(2,1)} %collect.2.refs_1_), custom_call_target="tpu_custom_call" | custom-call | tf_op jit(solution)/shard_map/pallas_call | solution.py:280
  276.2 7.5 %shard_map.119 = (bf16[16,64,512]{2,1,0:T(8,128)(2,1)}, bf16[16,64,512]{2,1,0:T(8,128)(2,1)}, bf16[16,64,512]{2,1,0:T(8,128)(2,1)}, bf16[16,64,512]{2,1,0:T(8,128)(2,1)}) custom-call(s32[2]{0:T(128)} %pad_add_fusion.chip_ref.s_ref, bf16[256,2048]{1,0:T(8,128)(2,1)} %bitcast.56, bf16[256,1024]{1,0:T(8,128)(2,1)} %copy-done.5, bf16[256,1024]{1,0:T(8,128)(2,1)} %copy-done.10, ...), custom_call_target="tpu_custom_call" | custom-call | tf_op jit(solution)/shard_map/pallas_call | solution.py:280
  286.3 5.3 %last_partial.3 = bf16[16,128,512]{2,1,0:T(8,128)(2,1)} custom-call(s32[2]{0:T(128)} %pad_add_fusion.chip_ref.s_ref, bf16[256,2048]{1,0:T(8,128)(2,1)} %bitcast.57, bf16[2,256,512]{2,1,0:T(8,128)(2,1)} %collect.3.b_ref, bf16[16,128,512]{2,1,0:T(8,128)(2,1)} %copy-done.12), custom_call_target="tpu_custom_call" | custom-call | tf_op jit(solution)/shard_map/last_partial/pallas_call | solution.py:310
  291.6 5.7 %all-to-all-start.5 = ((bf16[16,128,512]{2,1,0:T(8,128)(2,1)}), bf16[16,128,512]{2,1,0:T(8,128)(2,1)S(1)}, u32[]{:S(2)}, u32[]{:S(2)}) async-start(bf16[16,128,512]{2,1,0:T(8,128)(2,1)} %last_partial.3), calls=%async_computation.5 | async-start | bytes 4194304 | tf_op jit(solution)/shard_map/all_to_all | solution.py:336
  301.0 5.6 %shard_map.121 = (bf16[16,32,512]{2,1,0:T(8,128)(2,1)}, bf16[16,32,512]{2,1,0:T(8,128)(2,1)}, bf16[16,32,512]{2,1,0:T(8,128)(2,1)}, bf16[16,32,512]{2,1,0:T(8,128)(2,1)}) custom-call(s32[2]{0:T(128)} %pad_add_fusion.chip_ref.s_ref, bf16[256,2048]{1,0:T(8,128)(2,1)} %bitcast.58, bf16[2,256,512]{2,1,0:T(8,128)(2,1)} %collect.2.refs_1_, ...), custom_call_target="tpu_custom_call" | custom-call | tf_op jit(solution)/shard_map/pallas_call | solution.py:280
  311.3 22.2 %collective-permute-done.5 = bf16[16,64,512]{2,1,0:T(8,128)(2,1)} collective-permute-done((bf16[16,64,512]{2,1,0:T(8,128)(2,1)}, bf16[16,64,512]{2,1,0:T(8,128)(2,1)}, u32[]{:S(2)}, u32[]{:S(2)}) %collective-permute-start.5) | collective-permute-done | bytes 1048608 | tf_op jit(solution)/shard_map/ppermute | solution.py:349
  333.5 11.7 %collective-permute-done.6 = bf16[16,64,512]{2,1,0:T(8,128)(2,1)} collective-permute-done((bf16[16,64,512]{2,1,0:T(8,128)(2,1)}, bf16[16,64,512]{2,1,0:T(8,128)(2,1)}, u32[]{:S(2)}, u32[]{:S(2)}) %collective-permute-start.6) | collective-permute-done | bytes 1048608 | tf_op jit(solution)/shard_map/ppermute | solution.py:349
  347.7 8.1 %collective-permute-done.9 = bf16[16,32,512]{2,1,0:T(8,128)(2,1)S(1)} collective-permute-done((bf16[16,32,512]{2,1,0:T(8,128)(2,1)}, bf16[16,32,512]{2,1,0:T(8,128)(2,1)S(1)}, u32[]{:S(2)}, u32[]{:S(2)}) %collective-permute-start.9) | collective-permute-done | bytes 524320 | tf_op jit(solution)/shard_map/ppermute | solution.py:349
  355.9 11.5 %collective-permute-done.10 = bf16[16,32,512]{2,1,0:T(8,128)(2,1)S(1)} collective-permute-done((bf16[16,32,512]{2,1,0:T(8,128)(2,1)}, bf16[16,32,512]{2,1,0:T(8,128)(2,1)S(1)}, u32[]{:S(2)}, u32[]{:S(2)}) %collective-permute-start.10) | collective-permute-done | bytes 524320 | tf_op jit(solution)/shard_map/ppermute | solution.py:349
  369.1 6.5 %all-to-all-start.4 = ((bf16[16,96,512]{2,1,0:T(8,128)(2,1)}), bf16[16,96,512]{2,1,0:T(8,128)(2,1)}, u32[]{:S(2)}, u32[]{:S(2)}) async-start(bf16[16,96,512]{2,1,0:T(8,128)(2,1)} %pad_maximum_fusion), calls=%async_computation.4 | async-start | bytes 3145728 | tf_op jit(solution)/shard_map/all_to_all | solution.py:336
  375.6 4.4 %convolution_convert_fusion = bf16[256,2048]{1,0:T(8,128)(2,1)} fusion(bf16[256,1024]{1,0:T(8,128)(2,1)S(1)} %copy-done.11, bf16[1024,2048]{1,0:T(8,128)(2,1)} %param.13), kind=kOutput, calls=%fused_computation.3 | convolution fusion | flops 1074266112 | bytes 5767168 | tf_op jit(solution)/shard_map/dot_general | solution.py:432
  380.3 16.2 %all-to-all-done.4 = bf16[16,96,512]{2,1,0:T(8,128)(2,1)} async-done(((bf16[16,96,512]{2,1,0:T(8,128)(2,1)}), bf16[16,96,512]{2,1,0:T(8,128)(2,1)}, u32[]{:S(2)}, u32[]{:S(2)}) %all-to-all-start.4) | async-done | bytes 1572896 | tf_op jit(solution)/shard_map/all_to_all | solution.py:336
  399.6 9.6 %all-to-all-start.6 = ((bf16[8,224,512]{2,1,0:T(8,128)(2,1)}), bf16[8,224,512]{2,1,0:T(8,128)(2,1)S(1)}, u32[]{:S(2)}, u32[]{:S(2)}) async-start(bf16[8,224,512]{2,1,0:T(8,128)(2,1)} %broadcast_in_dim.64), calls=%async_computation.6 | async-start | bytes 3670016 | tf_op jit(solution)/shard_map/all_to_all | solution.py:336
  417.6 15.0 %all-to-all-done.6 = bf16[8,224,512]{2,1,0:T(8,128)(2,1)S(1)} async-done(((bf16[8,224,512]{2,1,0:T(8,128)(2,1)}), bf16[8,224,512]{2,1,0:T(8,128)(2,1)S(1)}, u32[]{:S(2)}, u32[]{:S(2)}) %all-to-all-start.6) | async-done | bytes 1835040 | tf_op jit(solution)/shard_map/all_to_all | solution.py:336
  (121 shorter events, 57.6 us)
Async XLA Ops:
  2.2 15.2 %all-to-all-start = ((s32[16,1,8]{2,1,0:T(1,128)}), s32[16,1,8]{2,1,0:T(1,128)S(1)}, u32[]{:S(2)}, u32[]{:S(2)}) async-start(s32[16,1,8]{2,1,0:T(1,128)} %bitcast.3), calls=%async_computation | async-start | bytes 16384 | tf_op jit(solution)/shard_map/all_to_all | solution.py:336
  23.4 6.9 %copy-start.1 = (bf16[256,2048]{1,0:T(8,128)(2,1)S(1)}, bf16[256,2048]{1,0:T(8,128)(2,1)}, u32[]{:S(2)}) copy-start(bf16[256,2048]{1,0:T(8,128)(2,1)} %keyval.1.kv_ref.own_ref) | copy-start | bytes 3145732
  23.5 11.4 %copy-start.19 = (s32[1,8,8]{2,1,0:T(8,128)S(1)}, s32[1,8,8]{2,1,0:T(8,128)}, u32[]{:S(2)}) copy-start(s32[1,8,8]{2,1,0:T(8,128)} %param.9) | copy-start | bytes 772
  23.5 11.4 %copy-start = (bf16[1,8,32,2048]{3,2,1,0:T(8,128)(2,1)S(1)}, bf16[1,8,32,2048]{3,2,1,0:T(8,128)(2,1)}, u32[]{:S(2)}) copy-start(bf16[1,8,32,2048]{3,2,1,0:T(8,128)(2,1)} %param.7) | copy-start | bytes 3145732
  23.5 99.6 %all-to-all-start.1 = ((bf16[16,96,2048]{2,1,0:T(8,128)(2,1)}), bf16[16,96,2048]{2,1,0:T(8,128)(2,1)}, u32[]{:S(2)}, u32[]{:S(2)}) async-start(bf16[16,96,2048]{2,1,0:T(8,128)(2,1)} %bitcast.60), calls=%async_computation.1 | async-start | bytes 12582912 | tf_op jit(solution)/shard_map/all_to_all | solution.py:336
  30.4 92.7 %collective-permute-start = (bf16[128,2048]{1,0:T(8,128)(2,1)S(1)}, bf16[128,2048]{1,0:T(8,128)(2,1)S(1)}, u32[]{:S(2)}, u32[]{:S(2)}) collective-permute-start(bf16[128,2048]{1,0:T(8,128)(2,1)S(1)} %slice.67), channel_id=1, source_target_pairs={{0,8},{8,16},{16,24},{24,32},{32,40},{40,48},{48,56},{56,64},{64,7... | collective-permute-start | bytes 1572872 | tf_op jit(solution)/shard_map/ppermute | solution.py:330
  34.9 5.2 %copy-start.9 = (bf16[1,8,32,2048]{3,2,1,0:T(8,128)(2,1)S(1)}, bf16[1,8,32,2048]{3,2,1,0:T(8,128)(2,1)}, u32[]{:S(2)}) copy-start(bf16[1,8,32,2048]{3,2,1,0:T(8,128)(2,1)} %param.8) | copy-start | bytes 3145732
  134.6 54.9 %all-to-all-start.3 = ((bf16[16,96,1024]{2,1,0:T(8,128)(2,1)}), bf16[16,96,1024]{2,1,0:T(8,128)(2,1)S(1)}, u32[]{:S(2)}, u32[]{:S(2)}) async-start(bf16[16,96,1024]{2,1,0:T(8,128)(2,1)} %bitcast.65), calls=%async_computation.3 | async-start | bytes 6291456 | tf_op jit(solution)/shard_map/all_to_all | solution.py:336
  148.7 13.7 %copy-start.18 = (bf16[256,512]{1,0:T(8,128)(2,1)S(1)}, bf16[256,512]{1,0:T(8,128)(2,1)}, u32[]{:S(2)}) copy-start(bf16[256,512]{1,0:T(8,128)(2,1)} %get-tuple-element.27) | copy-start | bytes 786436
  169.1 107.2 %collective-permute-start.3 = (bf16[4,16,64,512]{3,2,1,0:T(8,128)(2,1)}, bf16[4,16,64,512]{3,2,1,0:T(8,128)(2,1)}, u32[]{:S(2)}, u32[]{:S(2)}) collective-permute-start(bf16[4,16,64,512]{3,2,1,0:T(8,128)(2,1)} %shard_map.118), channel_id=1, source_target_pairs={{0,1},{1,0},{2,3},{3,2},{4,5},{5,4},{6,7},{7,6},{8,9},{9,8},{10,11... | collective-permute-start | bytes 12582920 | tf_op jit(solution)/shard_map/ppermute | solution.py:326
  189.5 9.0 %copy-start.20 = (s32[48]{0:T(128)S(1)}, s32[48]{0:T(128)}, u32[]{:S(2)}) copy-start(s32[48]{0:T(128)} %reshape.117.pick_ref) | copy-start | bytes 580
  191.1 73.8 %all-to-all-start.2 = ((bf16[16,96,1024]{2,1,0:T(8,128)(2,1)}), bf16[16,96,1024]{2,1,0:T(8,128)(2,1)}, u32[]{:S(2)}, u32[]{:S(2)}) async-start(bf16[16,96,1024]{2,1,0:T(8,128)(2,1)} %bitcast.66), calls=%async_computation.2 | async-start | bytes 6291456 | tf_op jit(solution)/shard_map/all_to_all | solution.py:336
  197.0 45.4 %collective-permute-start.2 = (bf16[128,1024]{1,0:T(8,128)(2,1)}, bf16[128,1024]{1,0:T(8,128)(2,1)S(1)}, u32[]{:S(2)}, u32[]{:S(2)}) collective-permute-start(bf16[128,1024]{1,0:T(8,128)(2,1)} %get-tuple-element.32), channel_id=1, source_target_pairs={{8,0},{16,8},{24,16},{32,24},{40,32},{48,40},{56,48},{64,56},{72,6... | collective-permute-start | bytes 786440 | tf_op jit(solution)/shard_map/ppermute | solution.py:330
  243.1 12.1 %copy-start.21 = (bf16[128,1024]{1,0:T(8,128)(2,1)S(1)}, bf16[128,1024]{1,0:T(8,128)(2,1)}, u32[]{:S(2)}) copy-start(bf16[128,1024]{1,0:T(8,128)(2,1)} %get-tuple-element.29) | copy-start | bytes 786436
  252.3 32.7 %collective-permute-start.11 = (bf16[16,128,512]{2,1,0:T(8,128)(2,1)}, bf16[16,128,512]{2,1,0:T(8,128)(2,1)S(1)}, u32[]{:S(2)}, u32[]{:S(2)}) collective-permute-start(bf16[16,128,512]{2,1,0:T(8,128)(2,1)} %last_partial.2), channel_id=1, source_target_pairs={{0,1},{1,0},{2,3},{3,2},{4,5},{5,4},{6,7},{7,6},{8,9},{9,8},{10,11... | collective-permute-start | bytes 6291464 | tf_op jit(solution)/shard_map/ppermute | solution.py:326
  255.2 9.7 %collective-permute-start.1 = (bf16[128,1024]{1,0:T(8,128)(2,1)S(1)}, bf16[128,1024]{1,0:T(8,128)(2,1)S(1)}, u32[]{:S(2)}, u32[]{:S(2)}) collective-permute-start(bf16[128,1024]{1,0:T(8,128)(2,1)S(1)} %copy-done.21), channel_id=1, source_target_pairs={{8,0},{16,8},{24,16},{32,24},{40,32},{48,40},{56,48},{64,56},{72,6... | collective-permute-start | bytes 786440 | tf_op jit(solution)/shard_map/ppermute | solution.py:330
  274.7 26.3 %collective-permute-start.7 = (bf16[4,16,32,512]{3,2,1,0:T(8,128)(2,1)}, bf16[4,16,32,512]{3,2,1,0:T(8,128)(2,1)}, u32[]{:S(2)}, u32[]{:S(2)}) collective-permute-start(bf16[4,16,32,512]{3,2,1,0:T(8,128)(2,1)} %shard_map.120), channel_id=1, source_target_pairs={{0,1},{1,0},{2,3},{3,2},{4,5},{5,4},{6,7},{7,6},{8,9},{9,8},{10,11... | collective-permute-start | bytes 6291464 | tf_op jit(solution)/shard_map/ppermute | solution.py:326
  283.7 26.2 %collective-permute-start.4 = (bf16[16,64,512]{2,1,0:T(8,128)(2,1)}, bf16[16,64,512]{2,1,0:T(8,128)(2,1)}, u32[]{:S(2)}, u32[]{:S(2)}) collective-permute-start(bf16[16,64,512]{2,1,0:T(8,128)(2,1)} %get-tuple-element.35), channel_id=1, source_target_pairs={{0,2},{1,3},{2,4},{3,5},{4,6},{5,7},{6,0},{7,1},{8,10},{9,11},{10,... | collective-permute-start | bytes 3145736 | tf_op jit(solution)/shard_map/ppermute | solution.py:349
  291.6 53.6 %copy-start.14 = (bf16[16,64,512]{2,1,0:T(8,128)(2,1)S(1)}, bf16[16,64,512]{2,1,0:T(8,128)(2,1)}, u32[]{:S(2)}) copy-start(bf16[16,64,512]{2,1,0:T(8,128)(2,1)} %get-tuple-element.34) | copy-start | bytes 3145732
  291.6 77.5 %all-to-all-start.5 = ((bf16[16,128,512]{2,1,0:T(8,128)(2,1)}), bf16[16,128,512]{2,1,0:T(8,128)(2,1)S(1)}, u32[]{:S(2)}, u32[]{:S(2)}) async-start(bf16[16,128,512]{2,1,0:T(8,128)(2,1)} %last_partial.3), calls=%async_computation.5 | async-start | bytes 4194304 | tf_op jit(solution)/shard_map/all_to_all | solution.py:336
  297.3 36.2 %collective-permute-start.5 = (bf16[16,64,512]{2,1,0:T(8,128)(2,1)}, bf16[16,64,512]{2,1,0:T(8,128)(2,1)}, u32[]{:S(2)}, u32[]{:S(2)}) collective-permute-start(bf16[16,64,512]{2,1,0:T(8,128)(2,1)} %get-tuple-element.36), channel_id=1, source_target_pairs={{0,4},{1,5},{2,6},{3,7},{4,0},{5,1},{6,2},{7,3},{8,12},{9,13},{10,... | collective-permute-start | bytes 3145736 | tf_op jit(solution)/shard_map/ppermute | solution.py:349
  299.9 45.3 %collective-permute-start.6 = (bf16[16,64,512]{2,1,0:T(8,128)(2,1)}, bf16[16,64,512]{2,1,0:T(8,128)(2,1)}, u32[]{:S(2)}, u32[]{:S(2)}) collective-permute-start(bf16[16,64,512]{2,1,0:T(8,128)(2,1)} %get-tuple-element.37), channel_id=1, source_target_pairs={{0,6},{1,7},{2,0},{3,1},{4,2},{5,3},{6,4},{7,5},{8,14},{9,15},{10,... | collective-permute-start | bytes 3145736 | tf_op jit(solution)/shard_map/ppermute | solution.py:349
  306.6 60.8 %copy-start.15 = (bf16[16,32,512]{2,1,0:T(8,128)(2,1)S(1)}, bf16[16,32,512]{2,1,0:T(8,128)(2,1)}, u32[]{:S(2)}) copy-start(bf16[16,32,512]{2,1,0:T(8,128)(2,1)} %get-tuple-element.38) | copy-start | bytes 1572868
  306.6 41.2 %collective-permute-start.8 = (bf16[16,32,512]{2,1,0:T(8,128)(2,1)}, bf16[16,32,512]{2,1,0:T(8,128)(2,1)S(1)}, u32[]{:S(2)}, u32[]{:S(2)}) collective-permute-start(bf16[16,32,512]{2,1,0:T(8,128)(2,1)} %get-tuple-element.39), channel_id=1, source_target_pairs={{0,2},{1,3},{2,4},{3,5},{4,6},{5,7},{6,0},{7,1},{8,10},{9,11},{10,... | collective-permute-start | bytes 1572872 | tf_op jit(solution)/shard_map/ppermute | solution.py:349
  307.0 48.9 %collective-permute-start.9 = (bf16[16,32,512]{2,1,0:T(8,128)(2,1)}, bf16[16,32,512]{2,1,0:T(8,128)(2,1)S(1)}, u32[]{:S(2)}, u32[]{:S(2)}) collective-permute-start(bf16[16,32,512]{2,1,0:T(8,128)(2,1)} %get-tuple-element.40), channel_id=1, source_target_pairs={{0,4},{1,5},{2,6},{3,7},{4,0},{5,1},{6,2},{7,3},{8,12},{9,13},{10,... | collective-permute-start | bytes 1572872 | tf_op jit(solution)/shard_map/ppermute | solution.py:349
  310.0 57.4 %collective-permute-start.10 = (bf16[16,32,512]{2,1,0:T(8,128)(2,1)}, bf16[16,32,512]{2,1,0:T(8,128)(2,1)S(1)}, u32[]{:S(2)}, u32[]{:S(2)}) collective-permute-start(bf16[16,32,512]{2,1,0:T(8,128)(2,1)} %get-tuple-element.41), channel_id=1, source_target_pairs={{0,6},{1,7},{2,0},{3,1},{4,2},{5,3},{6,4},{7,5},{8,14},{9,15},{10,... | collective-permute-start | bytes 1572872 | tf_op jit(solution)/shard_map/ppermute | solution.py:349
  367.7 7.9 %copy-start.11 = (bf16[256,1024]{1,0:T(8,128)(2,1)S(1)}, bf16[256,1024]{1,0:T(8,128)(2,1)}, u32[]{:S(2)}) copy-start(bf16[256,1024]{1,0:T(8,128)(2,1)} %copy-done.10) | copy-start | bytes 1572868
  369.1 27.5 %all-to-all-start.4 = ((bf16[16,96,512]{2,1,0:T(8,128)(2,1)}), bf16[16,96,512]{2,1,0:T(8,128)(2,1)}, u32[]{:S(2)}, u32[]{:S(2)}) async-start(bf16[16,96,512]{2,1,0:T(8,128)(2,1)} %pad_maximum_fusion), calls=%async_computation.4 | async-start | bytes 3145728 | tf_op jit(solution)/shard_map/all_to_all | solution.py:336
  398.1 11.0 %copy-start.4 = (bf16[2,256,512]{2,1,0:T(8,128)(2,1)S(1)}, bf16[2,256,512]{2,1,0:T(8,128)(2,1)}, u32[]{:S(2)}) copy-start(bf16[2,256,512]{2,1,0:T(8,128)(2,1)} %collect.2.refs_1_) | copy-start | bytes 1572868
  398.2 11.1 %copy-start.3 = (bf16[2,256,512]{2,1,0:T(8,128)(2,1)S(1)}, bf16[2,256,512]{2,1,0:T(8,128)(2,1)}, u32[]{:S(2)}) copy-start(bf16[2,256,512]{2,1,0:T(8,128)(2,1)} %collect.3.b_ref) | copy-start | bytes 1572868
  399.6 33.0 %all-to-all-start.6 = ((bf16[8,224,512]{2,1,0:T(8,128)(2,1)}), bf16[8,224,512]{2,1,0:T(8,128)(2,1)S(1)}, u32[]{:S(2)}, u32[]{:S(2)}) async-start(bf16[8,224,512]{2,1,0:T(8,128)(2,1)} %broadcast_in_dim.64), calls=%async_computation.6 | async-start | bytes 3670016 | tf_op jit(solution)/shard_map/all_to_all | solution.py:336
  409.3 3.6 copy-start.7
  (9 other events, 10.5 us)

commit v4 on v3

--- a/solution.py
+++ b/solution.py
@@ -224,6 +224,9 @@
     )(pick, own, rim, back)
 
 
+LANES = 512
+
+
 def taken(right):
     if right.ndim == 3:
         rows, n = right.shape[1:]
@@ -232,56 +235,110 @@
     return n // 2, pl.BlockSpec((rows, n // 2), lambda i, s, *_: (0, s[1]))
 
 
-def partial_call(pairs, shards, width, scalars, got=None):
+def packed_rows(rows, n):
+    return rows * n // LANES
+
+
+def packed(part):
+    rows, n = part.shape
+    if n >= LANES:
+        return jnp.concatenate([part[:, at : at + LANES] for at in range(0, n, LANES)], axis=0)
+    return jnp.concatenate([part[: rows // 2], part[rows // 2 :]], axis=1)
+
+
+def unpacked(x, n):
+    if n >= LANES:
+        return jnp.concatenate(jnp.split(x, n // LANES, axis=-2), axis=-1)
+    return jnp.concatenate([x[..., :n], x[..., n:]], axis=-2)
+
+
+def partial_call(pairs, scalars, got=None, by_chip=True, extra=None):
     per = 4
+    steps = BLOCKS // per
+    chips = CHIPS if by_chip else 1
     cuts = [taken(right) for _, right in pairs]
-    height = sum(s // CHIPS * (n // width) for (n, _), s in zip(cuts, shards))
-    rows = pairs[0][0].shape[0]
+    across = [left.shape[0] == right.shape[-2] for left, right in pairs]
+    shards = [left.shape[1 if a else 0] // BLOCKS for (left, _), a in zip(pairs, across)]
+    height = sum(packed_rows(s // chips, n) for (n, _), s in zip(cuts, shards))
     keep = got is not None
 
     def body(chip_ref, *refs):
         factors, refs = refs[: 2 * len(pairs)], refs[2 * len(pairs) :]
         totals = refs[-len(pairs) :]
         for k, total in enumerate(totals):
-            total[...] = dot_first(factors[2 * k][...], factors[2 * k + 1][...])
-        for t in range(per):
-            for d in range(CHIPS):
-                c = lax.rem(chip_ref[0] + d, CHIPS) if keep else d
-                at = 0
-                for total, shard in zip(totals, shards):
-                    piece = shard // CHIPS
-                    first = t * shard + c * piece
-                    if keep:
-                        first = pl.multiple_of(first, piece)
-                    for left in range(0, total.shape[1], width):
-                        part = total[pl.ds(first, piece), left : left + width]
-                        here = slice(at, at + piece)
+            product = dot_first if across[k] else dot
+            total[...] = product(factors[2 * k][...], factors[2 * k + 1][...])
+
+        def write(half):
+            for t in range(per):
+                for d in range(chips):
+                    c = lax.rem(chip_ref[0] + d, CHIPS) if keep and by_chip else d
+                    parts = []
+                    for total, shard in zip(totals, shards):
+                        piece = shard // chips
+                        first = t * shard + c * piece
+                        if keep and by_chip:
+                            first = pl.multiple_of(first, piece)
+                        parts.append(packed(total[pl.ds(first, piece), :]))
+                    part = parts[0] if len(parts) == 1 else jnp.concatenate(parts, axis=0)
+                    if not by_chip:
                         if keep:
-                            part = part + refs[0][c, t, here, :].astype(f32)
-                            refs[1 + d][t, here, :] = part.astype(bf16)
+                            part = part + refs[0][t].astype(f32)
+                        out_ref = refs[-1 - len(totals)]
+                        if extra is None:
+                            out_ref[t] = part.astype(bf16)
                         else:
-                            refs[0][c, t, here, :] = part.astype(bf16)
-                        at += piece
-
-    whole = pl.BlockSpec((CHIPS, per, height, width), lambda i, *_: (0, i, 0, 0))
-    one = pl.BlockSpec((per, height, width), lambda i, *_: (i, 0, 0))
+                            more = extra.shape[1]
+                            out_ref[t, :more, :] = refs[1][t]
+                            out_ref[t, more:, :] = part.astype(bf16)
+                    elif keep:
+                        part = part + refs[0][c, t].astype(f32)
+                        refs[1 + 2 * d + half][t] = part.astype(bf16)
+                    else:
+                        refs[0][c, t] = part.astype(bf16)
+
+        if keep and by_chip:
+            early = pl.program_id(0) < steps // 2
+            pl.when(early)(lambda: write(0))
+            pl.when(jnp.logical_not(early))(lambda: write(1))
+        else:
+            write(0)
+
+    if by_chip:
+        whole = pl.BlockSpec((CHIPS, per, height, LANES), lambda i, *_: (0, i, 0, 0))
+        shape = (CHIPS, BLOCKS, height, LANES)
+    else:
+        whole = pl.BlockSpec((per, height, LANES), lambda i, *_: (i, 0, 0))
+        shape = (BLOCKS, height, LANES)
     in_specs, operands = [], []
-    for (left, right), shard, (_, spec) in zip(pairs, shards, cuts):
-        in_specs += [pl.BlockSpec((rows, per * shard), lambda i, *_: (0, i)), spec]
+    for (left, right), shard, (_, spec), a in zip(pairs, shards, cuts, across):
+        if a:
+            in_specs += [pl.BlockSpec((left.shape[0], per * shard), lambda i, *_: (0, i)), spec]
+        else:
+            in_specs += [pl.BlockSpec((per * shard, left.shape[1]), lambda i, *_: (i, 0)), spec]
         operands += [left, right]
+    out_specs, out_shape = whole, jax.ShapeDtypeStruct(shape, bf16)
     if keep:
         in_specs.append(whole)
         operands.append(got)
-        out_specs = [one] * CHIPS
-        out_shape = [jax.ShapeDtypeStruct((BLOCKS, height, width), bf16)] * CHIPS
-    else:
-        out_specs = whole
-        out_shape = jax.ShapeDtypeStruct((CHIPS, BLOCKS, height, width), bf16)
+        if extra is not None:
+            more = extra.shape[1]
+            in_specs.append(pl.BlockSpec((per, more, LANES), lambda i, *_: (i, 0, 0)))
+            operands.append(extra)
+            out_specs = pl.BlockSpec((per, more + height, LANES), lambda i, *_: (i, 0, 0))
+            out_shape = jax.ShapeDtypeStruct((BLOCKS, more + height, LANES), bf16)
+        if by_chip:
+            halves = [
+                pl.BlockSpec((per, height, LANES), lambda i, *_: (jnp.minimum(i, steps // 2 - 1), 0, 0)),
+                pl.BlockSpec((per, height, LANES), lambda i, *_: (jnp.maximum(i - steps // 2, 0), 0, 0)),
+            ]
+            out_specs = halves * CHIPS
+            out_shape = [jax.ShapeDtypeStruct((BLOCKS // 2, height, LANES), bf16)] * (2 * CHIPS)
     return pl.pallas_call(
         body,
         grid_spec=pltpu.PrefetchScalarGridSpec(
             num_scalar_prefetch=1,
-            grid=(BLOCKS // per,),
+            grid=(steps,),
             in_specs=in_specs,
             out_specs=out_specs,
             scratch_shapes=[
@@ -293,35 +350,6 @@
     )(scalars, *operands)
 
 
-def last_partial(x, g, scalars, got=None):
-    rows, m = x.shape
-    n, right = taken(g)
-    shard, per = m // BLOCKS, 4
-    spec = pl.BlockSpec((per, shard, n), lambda i, *_: (i, 0, 0))
-
-    def body(s_ref, a_ref, b_ref, *refs):
-        total = dot_first(a_ref[...], b_ref[...])
-        for t in range(per):
-            part = total[t * shard : (t + 1) * shard]
-            if got is not None:
-                part = part + refs[0][t].astype(f32)
-            refs[-1][t] = part.astype(bf16)
-
-    return pl.pallas_call(
-        body,
-        grid_spec=pltpu.PrefetchScalarGridSpec(
-            num_scalar_prefetch=1,
-            grid=(BLOCKS // per,),
-            in_specs=[pl.BlockSpec((rows, per * shard), lambda i, *_: (0, i)), right]
-            + [spec] * (got is not None),
-            out_specs=spec,
-        ),
-        out_shape=jax.ShapeDtypeStruct((BLOCKS, shard, n), bf16),
-        compiler_params=params(),
-        name="last_partial",
-    )(scalars, x, g, *([] if got is None else [got]))
-
-
 def other_core(x):
     return lax.ppermute(x, "roll", [(i, i ^ 1) for i in range(lax.axis_size("roll"))])
 
@@ -342,13 +370,24 @@
     return jnp.sum(parts.astype(f32), axis=0).astype(bf16)
 
 
+def along_chips(x, d):
+    n = 2 * CHIPS
+    return lax.ppermute(x, "roll", [(i, (i + 2 * d) % n) for i in range(n)])
+
+
+def plus(a, b):
+    return (a.astype(f32) + b.astype(f32)).astype(bf16)
+
+
 def over_chips(pieces):
-    total = pieces[0].astype(f32)
-    n = 2 * CHIPS
-    for d in range(1, CHIPS):
-        got = lax.ppermute(pieces[d], "roll", [(i, (i + 2 * d) % n) for i in range(n)])
-        total = total + got.astype(f32)
-    return total.astype(bf16)
+    own0, own1, next0, next1, far0, far1, last0, last1 = pieces
+    up, down = along_chips(far0, 1), along_chips(far1, -1)
+    from_next, from_last = along_chips(next1, 1), along_chips(last0, -1)
+    came0 = along_chips(plus(next0, up), 1)
+    came1 = along_chips(plus(last1, down), -1)
+    half0 = own0.astype(f32) + from_last.astype(f32) + came0.astype(f32)
+    half1 = own1.astype(f32) + from_next.astype(f32) + came1.astype(f32)
+    return jnp.concatenate([half0.astype(bf16), half1.astype(bf16)], axis=0)
 
 
 def everyone(x):
@@ -371,6 +410,7 @@
     sending = jnp.stack([chip, 1 - core]).astype(jnp.int32)
     x = inputs.reshape(ROWS, model_width)
     cot = cotangent.reshape(ROWS, model_width)
+    x_t = x.T
     recalled = memory_lists[0]
     first_frame = position * FRAMES
 
@@ -424,49 +464,49 @@
 
     heads_out = jnp.concatenate(heads, axis=1)
     grad_query = jnp.concatenate(dqs, axis=1)
-    shards = [model_width // BLOCKS, inner // BLOCKS]
-    sent = partial_call([(x, grad_query), (heads_out, cot)], shards, half, sending)
+    sent = partial_call([(x_t, grad_query), (heads_out, cot)], sending)
     got = other_core(sent)
-    kept = partial_call([(x, grad_query), (heads_out, cot)], shards, half, keeping, got)
+    kept = partial_call([(x_t, grad_query), (heads_out, cot)], keeping, got)
     sum_qo = over_chips(kept)
+    share_qo = summed(exchange(sum_qo))
+    both = everyone(share_qo).astype(f32)
     attended = jnp.dot(heads_out, w_output, preferred_element_type=f32).astype(bf16)
     grad_input = dot_last(grad_query, w_query)
-
-    dks, dvs = [], []
+    piece = model_width // BLOCKS // CHIPS
+    q_rows = packed_rows(piece, half)
+    total_q, total_o = (
+        jnp.concatenate([cut[:, c].reshape(-1, cut.shape[-1]) for c in range(2)], axis=1)
+        for cut in (
+            unpacked(both[:, :, :q_rows], half),
+            unpacked(both[:, :, q_rows:], model_width // 2),
+        )
+    )
+
+    dks, dvs, sums = [], [], []
     for g, count in enumerate(SPLIT):
+        last = g == len(SPLIT) - 1
         dkv = collect(pick_add, owns[g], passed[g], returned[g])
         dks.append(dkv[0])
         dvs.append(dkv[1])
+        sent = partial_call([(x_t, dkv)], sending, by_chip=not last)
+        got = other_core(sent)
+        extra = jnp.concatenate(sums, axis=1) if last else None
+        kept = partial_call([(x_t, dkv)], keeping, got, not last, extra)
+        if not last:
+            sums.append(over_chips(kept))
+    late = summed(exchange(kept))
+    both = everyone(late).astype(f32)
+    at, cols = 0, []
+    for g, count in enumerate(SPLIT):
         width = count * HEAD
-        if g == 0:
-            sent = partial_call([(x, dkv)], shards[:1], width, sending)
-            got = other_core(sent)
-            kept = partial_call([(x, dkv)], shards[:1], width, keeping, got)
-            sum_kv = over_chips(kept)
-            early = summed(exchange(jnp.concatenate([sum_qo, sum_kv], axis=1)))
+        if g < len(SPLIT) - 1:
+            size = packed_rows(piece, width)
+            cut = unpacked(both[:, :, at : at + size], width)
+            cols.append([cut[:, c].reshape(-1, width) for c in range(2)])
+            at += size
         else:
-            sent = last_partial(x, dkv, sending)
-            got = other_core(sent)
-            kept = last_partial(x, dkv, keeping, got)
-            late = summed(exchange(kept))
-    both = everyone(jnp.concatenate([early, late], axis=0)).astype(f32)
-    piece = model_width // BLOCKS // CHIPS
-    o_piece = inner // BLOCKS // CHIPS
-    total_q = jnp.concatenate([both[:, c, :piece].reshape(-1, half) for c in range(2)], axis=1)
-    total_o = jnp.concatenate(
-        [
-            both[:, c, piece + k * o_piece : piece + (k + 1) * o_piece].reshape(-1, half)
-            for c in range(2)
-            for k in range(2)
-        ],
-        axis=1,
-    )
-    at = piece + 2 * o_piece
-    kv_first = both[:, :, at : at + piece]
-    kv_last = jnp.sum(both[:, :, at + piece :], axis=0)
-    total_k, total_v = (
-        jnp.concatenate([kv_first[:, c].reshape(-1, half), kv_last[c]], axis=1) for c in range(2)
-    )
+            cols.append(unpacked(jnp.sum(both[:, :, at:], axis=0), width))
+    total_k, total_v = (jnp.concatenate([c[kind] for c in cols], axis=1) for kind in range(2))
     grad_input = (
         grad_input
         + dot_last(jnp.concatenate(dks, axis=1), w_key)

time: 438 us -> 424 us (0.968)
  waiting for transfers between devices: 235 us -> 196 us
  other arithmetic: 13.4 us -> 19.8 us
  matrix products: 20.2 us -> 26.5 us
  starting transfers between devices: 76.2 us -> 82.2 us
  local copies, waits for them, and re-layouts: 15.1 us -> 20.9 us
    ppermute x6 -> x12, waiting for transfers between devices: 55.7 us -> 23.8 us  [along_chips(): return lax.ppermute(x, 'roll', [(i, (i + 2 * d) % n) for i in range(n)])]
    pallas_call x4 -> x6, Pallas kernels: 23.9 us -> 34.2 us  [partial_call(): pl.pallas_call(body, grid_spec=pltpu.PrefetchScalarGridSpec(num_scalar_pr...]
    pallas_call x2 -> x0, Pallas kernels: 10.3 us -> none  [last_partial(): pl.pallas_call(body, grid_spec=pltpu.PrefetchScalarGridSpec(num_scalar_pr...]
    ppermute x3, waiting for transfers between devices: 130 us -> 122 us  [from_behind(): lax.ppermute(block, 'tm', [(i - distance, i) for i in range(BLOCKS) if 0...]
    convert_element_type x3 -> x9, other arithmetic: 3.37 us -> 10 us  [the longest x4 5.2 us: over_chips(): return jnp.concatenate([half0.astype(bf16), half1.astype(bf16)], axis=0)]
    dot_general x4, matrix products: 11.5 us -> 17.6 us  [dot_last(): lax.dot_general(left, right, (((1,), (1,)), ((), ())), preferred_element_...]
    ppermute x6 -> x12, starting transfers between devices: 7.45 us -> 10.3 us  [along_chips(): return lax.ppermute(x, 'roll', [(i, (i + 2 * d) % n) for i in range(n)])]
    all_to_all x7 -> x8, starting transfers between devices: 56.6 us -> 59.3 us  [exchange(): lax.all_to_all(x, axis, split_axis=0, concat_axis=0, tiled=True, axis_ind...]
  transfers between devices with their start and end apart: 19 -> 26, of which waited for: 11 -> 13; matrix products, arithmetic and copies ran while one was open for 7% -> 13% of each run, Pallas kernels for 14% -> 14%
where the time goes in v4:
time: 424 us; the launch traced here: 422 us
  waiting for transfers between devices  196 us (46%)
  starting transfers between devices  82.2 us (19%)
  Pallas kernels  75.7 us (18%)
  matrix products  26.5 us (6%)
  local copies, waits for them, and re-layouts  20.9 us (5%)
  other arithmetic  19.8 us (5%)
    ppermute x3, waiting for transfers between devices, from_behind(): lax.ppermute(block, 'tm', [(i - distance, i) for i in range(BLOCKS) if 0...  122 us
    all_to_all x8, starting transfers between devices, exchange(): lax.all_to_all(x, axis, split_axis=0, concat_axis=0, tiled=True, axis_ind...  59.3 us
    all_to_all x8, waiting for transfers between devices, exchange(): lax.all_to_all(x, axis, split_axis=0, concat_axis=0, tiled=True, axis_ind...  49.7 us
    pallas_call x6, Pallas kernels, partial_call(): pl.pallas_call(body, grid_spec=pltpu.PrefetchScalarGridSpec(num_scalar_pr...  34.2 us
    ppermute x12, waiting for transfers between devices, along_chips(): return lax.ppermute(x, 'roll', [(i, (i + 2 * d) % n) for i in range(n)])  23.8 us
    pallas_call x2, Pallas kernels, attend(): pl.pallas_call(attend_body, grid_spec=pltpu.PrefetchScalarGridSpec(num_sc...  21.5 us
    dot_general x4, matrix products, dot_last(): lax.dot_general(left, right, (((1,), (1,)), ((), ())), preferred_element_...  17.6 us
    ppermute x12, starting transfers between devices, along_chips(): return lax.ppermute(x, 'roll', [(i, (i + 2 * d) % n) for i in range(n)])  10.3 us
  transfers between devices with their start and end apart: 26, of which 13 were waited for; matrix products, arithmetic and copies ran while one was open for 13% of the time, Pallas kernels for 14%

profile of v4, /device:TPU:1, one launch (start us, length us, event | category | flops | bytes accessed | tf_op | source)
XLA Modules:
  0.0 421.7 jit_solution(17450404861322829443)
XLA Ops:
  2.2 8.6 %all-to-all-start = ((s32[16,1,8]{2,1,0:T(1,128)}), s32[16,1,8]{2,1,0:T(1,128)S(1)}, u32[]{:S(2)}, u32[]{:S(2)}) async-start(s32[16,1,8]{2,1,0:T(1,128)} %bitcast.3), calls=%async_computation | async-start | bytes 16384 | tf_op jit(solution)/shard_map/all_to_all | solution.py:364
  10.8 6.6 %keyval.1.kv_ref.own_ref = bf16[256,2048]{1,0:T(8,128)(2,1)} custom-call(bf16[256,2048]{1,0:T(8,128)(2,1)} %bitcast.61, bf16[2048,1024]{1,0:T(8,128)(2,1)} %wk_ref.1, bf16[2048,1024]{1,0:T(8,128)(2,1)} %wv_ref.1), custom_call_target="tpu_custom_call" | custom-call | tf_op jit(solution)/shard_map/keyval/pallas_call | solution.py:54
  18.4 5.0 %send.1 = bf16[1536,2048]{1,0:T(8,128)(2,1)} custom-call(s32[48]{0:T(128)} %reshape.120.pick_ref, bf16[256,2048]{1,0:T(8,128)(2,1)} %keyval.1.kv_ref.own_ref), custom_call_target="tpu_custom_call" | custom-call | tf_op jit(solution)/shard_map/send/pallas_call | solution.py:84
  23.4 6.8 %all-to-all-start.1 = ((bf16[16,96,2048]{2,1,0:T(8,128)(2,1)}), bf16[16,96,2048]{2,1,0:T(8,128)(2,1)}, u32[]{:S(2)}, u32[]{:S(2)}) async-start(bf16[16,96,2048]{2,1,0:T(8,128)(2,1)} %bitcast.59), calls=%async_computation.1 | async-start | bytes 12582912 | tf_op jit(solution)/shard_map/all_to_all | solution.py:364
  34.8 4.3 %convolution_convert_fusion.2.q_ref = bf16[256,1024]{1,0:T(8,128)(2,1)} fusion(bf16[256,2048]{1,0:T(8,128)(2,1)S(1)} %bitcast.63, bf16[2048,1024]{1,0:T(8,128)(2,1)} %param.10), kind=kOutput, calls=%fused_computation.6 | convolution fusion | flops 1074003968 | bytes 5767168 | tf_op jit(solution)/shard_map/dot_general | solution.py:424
  40.0 4.3 %convolution_convert_fusion.1.g_ref = bf16[256,1024]{1,0:T(8,128)(2,1)} fusion(bf16[256,2048]{1,0:T(8,128)(2,1)S(1)} %bitcast.66, bf16[1024,2048]{1,0:T(8,128)(2,1)} %param.13), kind=kOutput, calls=%fused_computation.5 | convolution fusion | flops 1074003968 | bytes 5767168 | tf_op jit(solution)/shard_map/dot_general | solution.py:33
  44.3 78.8 %collective-permute-done.prev_ref = bf16[128,2048]{1,0:T(8,128)(2,1)S(1)} collective-permute-done((bf16[128,2048]{1,0:T(8,128)(2,1)S(1)}, bf16[128,2048]{1,0:T(8,128)(2,1)S(1)}, u32[]{:S(2)}, u32[]{:S(2)}) %collective-permute-start) | collective-permute-done | bytes 524320 | tf_op jit(solution)/shard_map/ppermute | solution.py:358
  123.9 10.7 %attend.2 = (bf16[256,512]{1,0:T(8,128)(2,1)}, bf16[256,512]{1,0:T(8,128)(2,1)}, f32[256,1024]{1,0:T(8,128)}, bf16[128,1024]{1,0:T(8,128)(2,1)}, bf16[1536,1024]{1,0:T(8,128)(2,1)}) custom-call(s32[64]{0:T(128)} %get-tuple-element.73.read_ref, s32[64]{0:T(128)} %get-tuple-element.72.add_ref, f32[8,416]{1,0:T(8,128)} %reshape.117.bias_ref, ...), custom_call_target="tpu_custom_call" | custom-call | tf_op jit(solution)/shard_map/attend/pallas_call | solution.py:157
  134.5 13.5 %all-to-all-start.2 = ((bf16[16,96,1024]{2,1,0:T(8,128)(2,1)}), bf16[16,96,1024]{2,1,0:T(8,128)(2,1)S(1)}, u32[]{:S(2)}, u32[]{:S(2)}) async-start(bf16[16,96,1024]{2,1,0:T(8,128)(2,1)} %bitcast.68), calls=%async_computation.2 | async-start | bytes 6291456 | tf_op jit(solution)/shard_map/all_to_all | solution.py:364
  150.9 10.8 %attend.3 = (bf16[256,512]{1,0:T(8,128)(2,1)}, bf16[256,512]{1,0:T(8,128)(2,1)}, f32[256,1024]{1,0:T(8,128)}, bf16[128,1024]{1,0:T(8,128)(2,1)}, bf16[1536,1024]{1,0:T(8,128)(2,1)}) custom-call(s32[64]{0:T(128)} %get-tuple-element.73.read_ref, s32[64]{0:T(128)} %get-tuple-element.72.add_ref, f32[8,416]{1,0:T(8,128)} %reshape.117.bias_ref, ...), custom_call_target="tpu_custom_call" | custom-call | tf_op jit(solution)/shard_map/attend/pallas_call | solution.py:157
  165.7 5.8 %shard_map.118 = bf16[4,16,64,512]{3,2,1,0:T(8,128)(2,1)} custom-call(s32[2]{0:T(128)} %pad_add_fusion.1.chip_ref, bf16[2048,256]{1,0:T(8,128)(2,1)} %bitcast.53, bf16[256,1024]{1,0:T(8,128)(2,1)} %copy-done.4, bf16[256,1024]{1,0:T(8,128)(2,1)} %copy-done.10, bf16[256,2048]{1,0:T(8,128)(2,1)} %bitcast.64), custom_call_target="tpu_custom_call" | custom-call | tf_op jit(solution)/shard_map/pallas_call | solution.py:337
  174.1 15.4 %all-to-all-done.2 = bf16[16,96,1024]{2,1,0:T(8,128)(2,1)S(1)} async-done(((bf16[16,96,1024]{2,1,0:T(8,128)(2,1)}), bf16[16,96,1024]{2,1,0:T(8,128)(2,1)S(1)}, u32[]{:S(2)}, u32[]{:S(2)}) %all-to-all-start.2) | async-done | bytes 3145760 | tf_op jit(solution)/shard_map/all_to_all | solution.py:364
  191.1 5.8 %all-to-all-start.3 = ((bf16[16,96,1024]{2,1,0:T(8,128)(2,1)}), bf16[16,96,1024]{2,1,0:T(8,128)(2,1)}, u32[]{:S(2)}, u32[]{:S(2)}) async-start(bf16[16,96,1024]{2,1,0:T(8,128)(2,1)} %bitcast.67), calls=%async_computation.3 | async-start | bytes 6291456 | tf_op jit(solution)/shard_map/all_to_all | solution.py:364
  199.1 43.3 %collective-permute-done.1.rim_ref = bf16[128,1024]{1,0:T(8,128)(2,1)S(1)} collective-permute-done((bf16[128,1024]{1,0:T(8,128)(2,1)}, bf16[128,1024]{1,0:T(8,128)(2,1)S(1)}, u32[]{:S(2)}, u32[]{:S(2)}) %collective-permute-start.1) | collective-permute-done | bytes 262176 | tf_op jit(solution)/shard_map/ppermute | solution.py:358
  243.0 4.1 collect.2.refs_1_
  247.1 4.9 %shard_map.121 = bf16[4,16,32,512]{3,2,1,0:T(8,128)(2,1)} custom-call(s32[2]{0:T(128)} %pad_add_fusion.1.chip_ref, bf16[2048,256]{1,0:T(8,128)(2,1)} %bitcast.54, bf16[2,256,512]{2,1,0:T(8,128)(2,1)} %collect.2.refs_1_), custom_call_target="tpu_custom_call" | custom-call | tf_op jit(solution)/shard_map/pallas_call | solution.py:337
  255.6 7.5 %shard_map.119 = (bf16[8,64,512]{2,1,0:T(8,128)(2,1)}, bf16[8,64,512]{2,1,0:T(8,128)(2,1)}, bf16[8,64,512]{2,1,0:T(8,128)(2,1)}, bf16[8,64,512]{2,1,0:T(8,128)(2...) custom-call(s32[2]{0:T(128)} %pad_add_fusion.chip_ref, ...), custom_call_target="tpu_custom_call" | custom-call | tf_op jit(solution)/shard_map/pallas_call | solution.py:337
  267.3 9.9 %collective-permute-done.8 = bf16[8,64,512]{2,1,0:T(8,128)(2,1)S(1)} collective-permute-done((bf16[8,64,512]{2,1,0:T(8,128)(2,1)}, bf16[8,64,512]{2,1,0:T(8,128)(2,1)S(1)}, u32[]{:S(2)}, u32[]{:S(2)}) %collective-permute-start.8) | collective-permute-done | bytes 524320 | tf_op jit(solution)/shard_map/ppermute | solution.py:375
  282.5 4.3 %collect.3.refs_1_ = bf16[2,256,512]{2,1,0:T(8,128)(2,1)} custom-call(s32[48]{0:T(128)} %broadcast_select_fusion.pick_ref, f32[256,1024]{1,0:T(8,128)} %get-tuple-element.39.own_ref, bf16[128,1024]{1,0:T(8,128)(2,1)} %copy-done.17, bf16[1536,1024]{1,0:T(8,128)(2,1)} %bitcast.13.back_ref), custom_call_target="tpu_custom_call" | custom-call | tf_op jit(solution)/shard_map/collect/pallas_call | solution.py:212
  286.7 4.9 %shard_map.120 = bf16[16,128,512]{2,1,0:T(8,128)(2,1)} custom-call(s32[2]{0:T(128)} %pad_add_fusion.1.chip_ref, bf16[2048,256]{1,0:T(8,128)(2,1)} %bitcast.56, bf16[2,256,512]{2,1,0:T(8,128)(2,1)} %collect.3.refs_1_), custom_call_target="tpu_custom_call" | custom-call | tf_op jit(solution)/shard_map/pallas_call | solution.py:337
  295.5 5.7 %shard_map.122 = (bf16[8,32,512]{2,1,0:T(8,128)(2,1)}, bf16[8,32,512]{2,1,0:T(8,128)(2,1)}, bf16[8,32,512]{2,1,0:T(8,128)(2,1)}, bf16[8,32,512]{2,1,0:T(8,128)(2...) custom-call(s32[2]{0:T(128)} %pad_add_fusion.chip_ref, ...), custom_call_target="tpu_custom_call" | custom-call | tf_op jit(solution)/shard_map/pallas_call | solution.py:337
  311.2 4.2 all-to-all-start.4
  323.8 4.5 %collective-permute-done.12 = bf16[8,32,512]{2,1,0:T(8,128)(2,1)S(1)} collective-permute-done((bf16[8,32,512]{2,1,0:T(8,128)(2,1)}, bf16[8,32,512]{2,1,0:T(8,128)(2,1)S(1)}, u32[]{:S(2)}, u32[]{:S(2)}) %collective-permute-start.12) | collective-permute-done | bytes 262176 | tf_op jit(solution)/shard_map/ppermute | solution.py:375
  332.4 5.6 %shard_map.123 = bf16[16,160,512]{2,1,0:T(8,128)(2,1)} custom-call(s32[2]{0:T(128)} %pad_add_fusion.chip_ref, bf16[2048,256]{1,0:T(8,128)(2,1)} %bitcast.58, bf16[2,256,512]{2,1,0:T(8,128)(2,1)} %collect.3.refs_1_, bf16[16,128,512]{2,1,0:T(8,128)(2,1)} %copy-done.13, bf16[16,32,512]{2,1,0:T(8,128)(2,1)} %pad_maximum_fusion.2.refs_3_), custom_call_target="tpu_custom_call" | custom-call | tf_op jit(solution)/shard_map/pallas_call | solution.py:337
  339.0 5.5 %all-to-all-start.6 = ((bf16[16,160,512]{2,1,0:T(8,128)(2,1)}), bf16[16,160,512]{2,1,0:T(8,128)(2,1)S(1)}, u32[]{:S(2)}, u32[]{:S(2)}) async-start(bf16[16,160,512]{2,1,0:T(8,128)(2,1)} %shard_map.123), calls=%async_computation.6 | async-start | bytes 5242880 | tf_op jit(solution)/shard_map/all_to_all | solution.py:364
  344.5 4.5 %convolution_convert_fusion = bf16[256,2048]{1,0:T(8,128)(2,1)} fusion(bf16[256,1024]{1,0:T(8,128)(2,1)S(1)} %copy-done.11, bf16[1024,2048]{1,0:T(8,128)(2,1)} %param.13), kind=kOutput, calls=%fused_computation.3 | convolution fusion | flops 1074266112 | bytes 5767168 | tf_op jit(solution)/shard_map/dot_general | solution.py:473
  351.2 24.6 %all-to-all-done.6 = bf16[16,160,512]{2,1,0:T(8,128)(2,1)S(1)} async-done(((bf16[16,160,512]{2,1,0:T(8,128)(2,1)}), bf16[16,160,512]{2,1,0:T(8,128)(2,1)S(1)}, u32[]{:S(2)}, u32[]{:S(2)}) %all-to-all-start.6) | async-done | bytes 2621472 | tf_op jit(solution)/shard_map/all_to_all | solution.py:364
  376.6 10.5 %all-to-all-start.5 = ((bf16[8,64,512]{2,1,0:T(8,128)(2,1)}), bf16[8,64,512]{2,1,0:T(8,128)(2,1)}, u32[]{:S(2)}, u32[]{:S(2)}) async-start(bf16[8,64,512]{2,1,0:T(8,128)(2,1)} %broadcast_in_dim.67), calls=%async_computation.5 | async-start | bytes 1048576 | tf_op jit(solution)/shard_map/all_to_all | solution.py:364
  387.1 5.1 %fusion.6 = f32[256,2048]{1,0:T(8,128)} fusion(bf16[2048,1024]{1,0:T(8,128)(2,1)} %wv_ref.1, bf16[256,512]{1,0:T(8,128)(2,1)S(1)} %get-tuple-element.71, bf16[256,512]{1,0:T(8,128)(2,1)} %get-tuple-element.69), kind=kOutput, calls=%fused_computation.16 | convolution fusion | flops 1074790400 | bytes 6815744 | tf_op jit(solution)/shard_map/dot_general | solution.py:33
  397.8 4.4 %all-to-all-start.7 = ((bf16[8,160,512]{2,1,0:T(8,128)(2,1)}), bf16[8,160,512]{2,1,0:T(8,128)(2,1)S(1)}, u32[]{:S(2)}, u32[]{:S(2)}) async-start(bf16[8,160,512]{2,1,0:T(8,128)(2,1)} %broadcast_in_dim.68), calls=%async_computation.7 | async-start | bytes 2621440 | tf_op jit(solution)/shard_map/all_to_all | solution.py:364
  402.2 5.7 %fusion.1 = bf16[256,2048]{1,0:T(8,128)(2,1)} fusion(f32[256,2048]{1,0:T(8,128)} %fusion.6, f32[256,2048]{1,0:T(8,128)} %fusion.2, bf16[256,1024]{1,0:T(8,128)(2,1)S(1)} %copy-done.5, bf16[2048,1024]{1,0:T(8,128)(2,1)} %param.10), kind=kOutput, calls=%fused_computation.2 | convolution fusion | flops 1075314688 | bytes 9961472 | tf_op jit(solution)/shard_map/dot_general | solution.py:33
  411.7 8.3 %all-to-all-done.7 = bf16[8,160,512]{2,1,0:T(8,128)(2,1)S(1)} async-done(((bf16[8,160,512]{2,1,0:T(8,128)(2,1)}), bf16[8,160,512]{2,1,0:T(8,128)(2,1)S(1)}, u32[]{:S(2)}, u32[]{:S(2)}) %all-to-all-start.7) | async-done | bytes 1310752 | tf_op jit(solution)/shard_map/all_to_all | solution.py:364
  (146 shorter events, 77.1 us)
Async XLA Ops:
  2.2 15.2 %all-to-all-start = ((s32[16,1,8]{2,1,0:T(1,128)}), s32[16,1,8]{2,1,0:T(1,128)S(1)}, u32[]{:S(2)}, u32[]{:S(2)}) async-start(s32[16,1,8]{2,1,0:T(1,128)} %bitcast.3), calls=%async_computation | async-start | bytes 16384 | tf_op jit(solution)/shard_map/all_to_all | solution.py:364
  23.4 11.4 %copy-start.20 = (s32[1,8,8]{2,1,0:T(8,128)S(1)}, s32[1,8,8]{2,1,0:T(8,128)}, u32[]{:S(2)}) copy-start(s32[1,8,8]{2,1,0:T(8,128)} %param.9) | copy-start | bytes 772
  23.4 11.4 %copy-start.6 = (bf16[1,8,32,2048]{3,2,1,0:T(8,128)(2,1)S(1)}, bf16[1,8,32,2048]{3,2,1,0:T(8,128)(2,1)}, u32[]{:S(2)}) copy-start(bf16[1,8,32,2048]{3,2,1,0:T(8,128)(2,1)} %param.7) | copy-start | bytes 3145732
  23.4 99.6 %all-to-all-start.1 = ((bf16[16,96,2048]{2,1,0:T(8,128)(2,1)}), bf16[16,96,2048]{2,1,0:T(8,128)(2,1)}, u32[]{:S(2)}, u32[]{:S(2)}) async-start(bf16[16,96,2048]{2,1,0:T(8,128)(2,1)} %bitcast.59), calls=%async_computation.1 | async-start | bytes 12582912 | tf_op jit(solution)/shard_map/all_to_all | solution.py:364
  30.3 92.7 %collective-permute-start = (bf16[128,2048]{1,0:T(8,128)(2,1)S(1)}, bf16[128,2048]{1,0:T(8,128)(2,1)S(1)}, u32[]{:S(2)}, u32[]{:S(2)}) collective-permute-start(bf16[128,2048]{1,0:T(8,128)(2,1)S(1)} %slice.65), channel_id=1, source_target_pairs={{0,8},{8,16},{16,24},{24,32},{32,40},{40,48},{48,56},{56,64},{64,7... | collective-permute-start | bytes 1572872 | tf_op jit(solution)/shard_map/ppermute | solution.py:358
  134.5 55.0 %all-to-all-start.2 = ((bf16[16,96,1024]{2,1,0:T(8,128)(2,1)}), bf16[16,96,1024]{2,1,0:T(8,128)(2,1)S(1)}, u32[]{:S(2)}, u32[]{:S(2)}) async-start(bf16[16,96,1024]{2,1,0:T(8,128)(2,1)} %bitcast.68), calls=%async_computation.2 | async-start | bytes 6291456 | tf_op jit(solution)/shard_map/all_to_all | solution.py:364
  150.9 10.8 %copy-start.19 = (bf16[256,512]{1,0:T(8,128)(2,1)S(1)}, bf16[256,512]{1,0:T(8,128)(2,1)}, u32[]{:S(2)}) copy-start(bf16[256,512]{1,0:T(8,128)(2,1)} %get-tuple-element.32) | copy-start | bytes 786436
  171.5 84.1 %collective-permute-start.3 = (bf16[4,16,64,512]{3,2,1,0:T(8,128)(2,1)}, bf16[4,16,64,512]{3,2,1,0:T(8,128)(2,1)}, u32[]{:S(2)}, u32[]{:S(2)}) collective-permute-start(bf16[4,16,64,512]{3,2,1,0:T(8,128)(2,1)} %shard_map.118), channel_id=1, source_target_pairs={{0,1},{1,0},{2,3},{3,2},{4,5},{5,4},{6,7},{7,6},{8,9},{9,8},{10,11... | collective-permute-start | bytes 12582920 | tf_op jit(solution)/shard_map/ppermute | solution.py:354
  191.1 90.6 %all-to-all-start.3 = ((bf16[16,96,1024]{2,1,0:T(8,128)(2,1)}), bf16[16,96,1024]{2,1,0:T(8,128)(2,1)}, u32[]{:S(2)}, u32[]{:S(2)}) async-start(bf16[16,96,1024]{2,1,0:T(8,128)(2,1)} %bitcast.67), calls=%async_computation.3 | async-start | bytes 6291456 | tf_op jit(solution)/shard_map/all_to_all | solution.py:364
  197.0 45.3 %collective-permute-start.1 = (bf16[128,1024]{1,0:T(8,128)(2,1)}, bf16[128,1024]{1,0:T(8,128)(2,1)S(1)}, u32[]{:S(2)}, u32[]{:S(2)}) collective-permute-start(bf16[128,1024]{1,0:T(8,128)(2,1)} %get-tuple-element.37), channel_id=1, source_target_pairs={{8,0},{16,8},{24,16},{32,24},{40,32},{48,40},{56,48},{64,56},{72,6... | collective-permute-start | bytes 786440 | tf_op jit(solution)/shard_map/ppermute | solution.py:358
  252.0 41.9 %collective-permute-start.11 = (bf16[4,16,32,512]{3,2,1,0:T(8,128)(2,1)}, bf16[4,16,32,512]{3,2,1,0:T(8,128)(2,1)}, u32[]{:S(2)}, u32[]{:S(2)}) collective-permute-start(bf16[4,16,32,512]{3,2,1,0:T(8,128)(2,1)} %shard_map.121), channel_id=1, source_target_pairs={{0,1},{1,0},{2,3},{3,2},{4,5},{5,4},{6,7},{7,6},{8,9},{9,8},{10,11... | collective-permute-start | bytes 6291464 | tf_op jit(solution)/shard_map/ppermute | solution.py:354
  263.0 14.1 %collective-permute-start.8 = (bf16[8,64,512]{2,1,0:T(8,128)(2,1)}, bf16[8,64,512]{2,1,0:T(8,128)(2,1)S(1)}, u32[]{:S(2)}, u32[]{:S(2)}) collective-permute-start(bf16[8,64,512]{2,1,0:T(8,128)(2,1)} %get-tuple-element.49), channel_id=1, source_target_pairs={{0,6},{1,7},{2,0},{3,1},{4,2},{5,3},{6,4},{7,5},{8,14},{9,15},{10,... | collective-permute-start | bytes 1572872 | tf_op jit(solution)/shard_map/ppermute | solution.py:375
  265.6 27.2 %collective-permute-start.5 = (bf16[8,64,512]{2,1,0:T(8,128)(2,1)}, bf16[8,64,512]{2,1,0:T(8,128)(2,1)}, u32[]{:S(2)}, u32[]{:S(2)}) collective-permute-start(bf16[8,64,512]{2,1,0:T(8,128)(2,1)} %get-tuple-element.45), channel_id=1, source_target_pairs={{0,2},{1,3},{2,4},{3,5},{4,6},{5,7},{6,0},{7,1},{8,10},{9,11},{10,... | collective-permute-start | bytes 1572872 | tf_op jit(solution)/shard_map/ppermute | solution.py:375
  265.6 16.2 %collective-permute-start.2 = (bf16[128,1024]{1,0:T(8,128)(2,1)S(1)}, bf16[128,1024]{1,0:T(8,128)(2,1)S(1)}, u32[]{:S(2)}, u32[]{:S(2)}) collective-permute-start(bf16[128,1024]{1,0:T(8,128)(2,1)S(1)} %copy-done.22), channel_id=1, source_target_pairs={{8,0},{16,8},{24,16},{32,24},{40,32},{48,40},{56,48},{64,56},{72,6... | collective-permute-start | bytes 786440 | tf_op jit(solution)/shard_map/ppermute | solution.py:358
  267.1 34.1 %collective-permute-start.7 = (bf16[8,64,512]{2,1,0:T(8,128)(2,1)}, bf16[8,64,512]{2,1,0:T(8,128)(2,1)}, u32[]{:S(2)}, u32[]{:S(2)}) collective-permute-start(bf16[8,64,512]{2,1,0:T(8,128)(2,1)} %get-tuple-element.47), channel_id=1, source_target_pairs={{0,2},{1,3},{2,4},{3,5},{4,6},{5,7},{6,0},{7,1},{8,10},{9,11},{10,... | collective-permute-start | bytes 1572872 | tf_op jit(solution)/shard_map/ppermute | solution.py:375
  278.4 24.1 %collective-permute-start.9 = (bf16[8,64,512]{2,1,0:T(8,128)(2,1)S(1)}, bf16[8,64,512]{2,1,0:T(8,128)(2,1)}, u32[]{:S(2)}, u32[]{:S(2)}) collective-permute-start(bf16[8,64,512]{2,1,0:T(8,128)(2,1)S(1)} %add_convert_fusion.1), channel_id=1, source_target_pairs={{0,6},{1,7},{2,0},{3,1},{4,2},{5,3},{6,4},{7,5},{8,14},{9,15},{10,... | collective-permute-start | bytes 1572872 | tf_op jit(solution)/shard_map/ppermute | solution.py:375
  282.5 10.3 %copy-start.14 = (bf16[8,64,512]{2,1,0:T(8,128)(2,1)S(1)}, bf16[8,64,512]{2,1,0:T(8,128)(2,1)}, u32[]{:S(2)}) copy-start(bf16[8,64,512]{2,1,0:T(8,128)(2,1)} %get-tuple-element.44) | copy-start | bytes 1572868
  291.6 39.5 %collective-permute-start.10 = (bf16[16,128,512]{2,1,0:T(8,128)(2,1)}, bf16[16,128,512]{2,1,0:T(8,128)(2,1)S(1)}, u32[]{:S(2)}, u32[]{:S(2)}) collective-permute-start(bf16[16,128,512]{2,1,0:T(8,128)(2,1)} %shard_map.120), channel_id=1, source_target_pairs={{0,1},{1,0},{2,3},{3,2},{4,5},{5,4},{6,7},{7,6},{8,9},{9,8},{10,11... | collective-permute-start | bytes 6291464 | tf_op jit(solution)/shard_map/ppermute | solution.py:354
  292.7 13.7 %collective-permute-start.4 = (bf16[8,64,512]{2,1,0:T(8,128)(2,1)}, bf16[8,64,512]{2,1,0:T(8,128)(2,1)}, u32[]{:S(2)}, u32[]{:S(2)}) collective-permute-start(bf16[8,64,512]{2,1,0:T(8,128)(2,1)} %get-tuple-element.43), channel_id=1, source_target_pairs={{0,6},{1,7},{2,0},{3,1},{4,2},{5,3},{6,4},{7,5},{8,14},{9,15},{10,... | collective-permute-start | bytes 1572872 | tf_op jit(solution)/shard_map/ppermute | solution.py:375
  293.9 14.8 %copy-start.15 = (bf16[8,64,512]{2,1,0:T(8,128)(2,1)S(1)}, bf16[8,64,512]{2,1,0:T(8,128)(2,1)}, u32[]{:S(2)}) copy-start(bf16[8,64,512]{2,1,0:T(8,128)(2,1)} %get-tuple-element.42) | copy-start | bytes 1572868
  293.9 14.8 %collective-permute-start.6 = (bf16[8,64,512]{2,1,0:T(8,128)(2,1)S(1)}, bf16[8,64,512]{2,1,0:T(8,128)(2,1)}, u32[]{:S(2)}, u32[]{:S(2)}) collective-permute-start(bf16[8,64,512]{2,1,0:T(8,128)(2,1)S(1)} %add_convert_fusion.3), channel_id=1, source_target_pairs={{0,2},{1,3},{2,4},{3,5},{4,6},{5,7},{6,0},{7,1},{8,10},{9,11},{10,... | collective-permute-start | bytes 1572872 | tf_op jit(solution)/shard_map/ppermute | solution.py:375
  301.1 14.3 %collective-permute-start.16 = (bf16[8,32,512]{2,1,0:T(8,128)(2,1)}, bf16[8,32,512]{2,1,0:T(8,128)(2,1)}, u32[]{:S(2)}, u32[]{:S(2)}) collective-permute-start(bf16[8,32,512]{2,1,0:T(8,128)(2,1)} %get-tuple-element.57), channel_id=1, source_target_pairs={{0,6},{1,7},{2,0},{3,1},{4,2},{5,3},{6,4},{7,5},{8,14},{9,15},{10,... | collective-permute-start | bytes 786440 | tf_op jit(solution)/shard_map/ppermute | solution.py:375
  302.4 18.6 %collective-permute-start.15 = (bf16[8,32,512]{2,1,0:T(8,128)(2,1)}, bf16[8,32,512]{2,1,0:T(8,128)(2,1)}, u32[]{:S(2)}, u32[]{:S(2)}) collective-permute-start(bf16[8,32,512]{2,1,0:T(8,128)(2,1)} %get-tuple-element.55), channel_id=1, source_target_pairs={{0,2},{1,3},{2,4},{3,5},{4,6},{5,7},{6,0},{7,1},{8,10},{9,11},{10,... | collective-permute-start | bytes 786440 | tf_op jit(solution)/shard_map/ppermute | solution.py:375
  306.5 13.5 %collective-permute-start.13 = (bf16[8,32,512]{2,1,0:T(8,128)(2,1)}, bf16[8,32,512]{2,1,0:T(8,128)(2,1)}, u32[]{:S(2)}, u32[]{:S(2)}) collective-permute-start(bf16[8,32,512]{2,1,0:T(8,128)(2,1)} %get-tuple-element.53), channel_id=1, source_target_pairs={{0,2},{1,3},{2,4},{3,5},{4,6},{5,7},{6,0},{7,1},{8,10},{9,11},{10,... | collective-permute-start | bytes 786440 | tf_op jit(solution)/shard_map/ppermute | solution.py:375
  308.7 11.2 %copy-start.16 = (bf16[8,32,512]{2,1,0:T(8,128)(2,1)S(1)}, bf16[8,32,512]{2,1,0:T(8,128)(2,1)}, u32[]{:S(2)}) copy-start(bf16[8,32,512]{2,1,0:T(8,128)(2,1)} %get-tuple-element.52) | copy-start | bytes 786436
  311.2 26.8 %all-to-all-start.4 = ((bf16[16,64,512]{2,1,0:T(8,128)(2,1)}), bf16[16,64,512]{2,1,0:T(8,128)(2,1)S(1)}, u32[]{:S(2)}, u32[]{:S(2)}) async-start(bf16[16,64,512]{2,1,0:T(8,128)(2,1)} %pad_maximum_fusion), calls=%async_computation.4 | async-start | bytes 2097152 | tf_op jit(solution)/shard_map/all_to_all | solution.py:364
  316.5 6.2 %collective-permute-start.17 = (bf16[8,32,512]{2,1,0:T(8,128)(2,1)S(1)}, bf16[8,32,512]{2,1,0:T(8,128)(2,1)S(1)}, u32[]{:S(2)}, u32[]{:S(2)}) collective-permute-start(bf16[8,32,512]{2,1,0:T(8,128)(2,1)S(1)} %add_convert_fusion.5), channel_id=1, source_target_pairs={{0,6},{1,7},{2,0},{3,1},{4,2},{5,3},{6,4},{7,5},{8,14},{9,15},{10,... | collective-permute-start | bytes 786440 | tf_op jit(solution)/shard_map/ppermute | solution.py:375
  317.0 11.3 %collective-permute-start.12 = (bf16[8,32,512]{2,1,0:T(8,128)(2,1)}, bf16[8,32,512]{2,1,0:T(8,128)(2,1)S(1)}, u32[]{:S(2)}, u32[]{:S(2)}) collective-permute-start(bf16[8,32,512]{2,1,0:T(8,128)(2,1)} %get-tuple-element.51), channel_id=1, source_target_pairs={{0,6},{1,7},{2,0},{3,1},{4,2},{5,3},{6,4},{7,5},{8,14},{9,15},{10,... | collective-permute-start | bytes 786440 | tf_op jit(solution)/shard_map/ppermute | solution.py:375
  321.0 8.2 %collective-permute-start.14 = (bf16[8,32,512]{2,1,0:T(8,128)(2,1)S(1)}, bf16[8,32,512]{2,1,0:T(8,128)(2,1)S(1)}, u32[]{:S(2)}, u32[]{:S(2)}) collective-permute-start(bf16[8,32,512]{2,1,0:T(8,128)(2,1)S(1)} %add_convert_fusion.7), channel_id=1, source_target_pairs={{0,2},{1,3},{2,4},{3,5},{4,6},{5,7},{6,0},{7,1},{8,10},{9,11},{10,... | collective-permute-start | bytes 786440 | tf_op jit(solution)/shard_map/ppermute | solution.py:375
  339.0 36.8 %all-to-all-start.6 = ((bf16[16,160,512]{2,1,0:T(8,128)(2,1)}), bf16[16,160,512]{2,1,0:T(8,128)(2,1)S(1)}, u32[]{:S(2)}, u32[]{:S(2)}) async-start(bf16[16,160,512]{2,1,0:T(8,128)(2,1)} %shard_map.123), calls=%async_computation.6 | async-start | bytes 5242880 | tf_op jit(solution)/shard_map/all_to_all | solution.py:364
  376.6 19.9 %all-to-all-start.5 = ((bf16[8,64,512]{2,1,0:T(8,128)(2,1)}), bf16[8,64,512]{2,1,0:T(8,128)(2,1)}, u32[]{:S(2)}, u32[]{:S(2)}) async-start(bf16[8,64,512]{2,1,0:T(8,128)(2,1)} %broadcast_in_dim.67), calls=%async_computation.5 | async-start | bytes 1048576 | tf_op jit(solution)/shard_map/all_to_all | solution.py:364
  397.8 22.2 %all-to-all-start.7 = ((bf16[8,160,512]{2,1,0:T(8,128)(2,1)}), bf16[8,160,512]{2,1,0:T(8,128)(2,1)S(1)}, u32[]{:S(2)}, u32[]{:S(2)}) async-start(bf16[8,160,512]{2,1,0:T(8,128)(2,1)} %broadcast_in_dim.68), calls=%async_computation.7 | async-start | bytes 2621440 | tf_op jit(solution)/shard_map/all_to_all | solution.py:364
  (17 other events, 67.4 us)
